TPU v7x, 256 devices: a 8x8x2 block of a 8x8x16 slice. The times are simulated.
256 devices in a mesh: rep: 2 (over z), exp: 128 (over x, y, core).
Axes of the slice: x: 8, y: 8, z: 2, core: 2. Of those that a mesh axis runs over, the one named last changes fastest.
The devices are a block of a 8x8x16 slice.
Arguments:
- a_tokens: bfloat16 [512, 7168], P(('rep', 'exp')), parts along dimension 0, may hold values from -6 to 6
- a_gain: float32 [7168], replicated, may hold values from 0.25 to 1.75
- dense_gate: bfloat16 [7168, 18432], P(None, 'exp'), may hold values from -0.0625 to 0.0625
- dense_up: bfloat16 [7168, 18432], P(None, 'exp'), may hold values from -0.0625 to 0.0625
- dense_down: bfloat16 [18432, 7168], P('exp'), may hold values from -0.046875 to 0.046875
- b_tokens: bfloat16 [1024, 7168], P(('rep', 'exp')), parts along dimension 0, may hold values from -6 to 6
- b_gain: float32 [7168], replicated, may hold values from 0.25 to 1.75
- expert_ids: int32 [1024, 8], P(('rep', 'exp')), parts along dimension 0, may hold values from 0 to 15, all different within a row; in each aligned block of 4 rows (0 to 3, 4 to 7, ...) at most 3 rows name the same one
- route_weights: float32 [1024, 8], P(('rep', 'exp')), parts along dimension 0, may hold values from 0.05 to 0.5
- expert_gate: bfloat16 [128, 7168, 128], P('exp'), may hold values from -0.0625 to 0.0625
- expert_up: bfloat16 [128, 7168, 128], P('exp'), may hold values from -0.0625 to 0.0625
- expert_down: bfloat16 [128, 128, 7168], P('exp'), may hold values from -0.1875 to 0.1875
Outputs:
- a_out: bfloat16 [512, 7168], P(('rep', 'exp')), parts along dimension 0
- b_out: bfloat16 [1024, 7168], P(('rep', 'exp')), parts along dimension 0
There are 2 independent parts, one for each index of `rep`. A program takes and returns all parts, laid end to end along the dimension named above; an argument that names none is the same for every part. Nothing has to cross between parts.
Inputs may be any that keep to these rules, and one draw needn't show every extreme that they name: `expert_ids`: each row names 8 different experts. Among the rows of one device no expert is named more than 3 times, and in some devices one expert is named exactly 3 times.
All inputs are finite; a program needn't handle non-finite values.
Results may differ from a plain program's by a relative error of at most 0.008.
Values may be sent and summed in bfloat16 or wider, within the bound.
No kernel may reach another device: no remote copies, remote signals or barrier semaphores. Data moves between devices by JAX's collectives and lax.ppermute only.
A program may use at most 128 MiB of HBM per device.

v0:
```python
import jax
import jax.numpy as jnp
from jax import lax
from jax.experimental import pallas as pl
from jax.experimental.pallas import tpu as pltpu
from jax.sharding import Mesh
from jax.sharding import PartitionSpec as P


EXPERTS = 16
RING = 8
CORES = 2
EXP = ("exp_0", "exp_1", "exp_2")
REP_EXP = ("rep", "exp_0", "exp_1", "exp_2")


def pairs_along(stage, partner):
    pairs = []
    for x in range(RING):
        for y in range(RING):
            for c in range(CORES):
                along_x = (stage == 2) == (c == 0)
                to_x = partner(x) if along_x else x
                to_y = y if along_x else partner(y)
                pairs.append(((x * RING + y) * CORES + c, (to_x * RING + to_y) * CORES + c))
    return pairs


def even_partner(i):
    return i ^ 1


def odd_partner(i):
    return (((i + 1) % RING) ^ 1) - 1 if i else RING - 1


def over_even(array):
    return lax.ppermute(array, EXP, pairs_along(2, even_partner))


def over_odd(array):
    return lax.ppermute(array, EXP, pairs_along(2, odd_partner))


def swap_cores(array):
    devices = RING * RING * CORES
    return lax.ppermute(array, EXP, [(i, i ^ 1) for i in range(devices)])


def normed(values, gain_vec):
    return values * lax.rsqrt(jnp.mean(values * values, axis=-1, keepdims=True) + 1e-06) * gain_vec


GROUPS = ((0,), (1, -1), (2, -2), (3, -3, 4))


def stage_1_groups():
    first = [[(x * RING + y) * CORES for y in range(RING)] for x in range(RING)]
    second = [[(x * RING + y) * CORES + 1 for x in range(RING)] for y in range(RING)]
    return first + second


def exchange(blocks):
    return lax.all_to_all(
        blocks, EXP, split_axis=0, concat_axis=0, tiled=True, axis_index_groups=stage_1_groups()
    )


def gather_ring(block, cut):
    slots = {0: block}
    for k in (1, 2, 3):
        slots[k] = over_even(slots[1 - k])
        slots[-k] = over_odd(slots[k - 1])
    slots[4] = (over_even(slots[-3][:, :cut]), over_odd(slots[3][:, cut:]))
    return slots


def scatter_ring(own, other, streams):
    count = len(streams) - 1
    cuts = [(hi - lo) // 2 for lo, hi in zip(streams, streams[1:])]

    def part(k, i):
        at = slice(streams[i], streams[i + 1])
        return own[k][:, at].astype(jnp.float32) + other[k][:, at].astype(jnp.float32)

    low, high = [None] * count, [None] * count
    for i in range(count):
        far = part(4, i).astype(jnp.bfloat16)
        low[i] = over_even(far[:, : cuts[i]])
        high[i] = over_odd(far[:, cuts[i] :])
    for i in range(count):
        first, second = low[i].astype(jnp.float32), high[i].astype(jnp.float32)
        low[i] = jnp.concatenate([part(-3, i)[:, : cuts[i]] + first, part(-3, i)[:, cuts[i] :]], 1)
        high[i] = jnp.concatenate([part(3, i)[:, : cuts[i]], part(3, i)[:, cuts[i] :] + second], 1)
    for k in (2, 1, 0):
        for i in range(count):
            one, two = low[i].astype(jnp.bfloat16), high[i].astype(jnp.bfloat16)
            one = over_even(one) if k == 1 else over_odd(one)
            two = over_odd(two) if k == 1 else over_even(two)
            low[i], high[i] = one.astype(jnp.float32), two.astype(jnp.float32)
        if k:
            side = 1 if k == 2 else -1
            for i in range(count):
                low[i] = part(side * k, i) + low[i]
                high[i] = part(-side * k, i) + high[i]
    return jnp.concatenate([part(0, i) + low[i] + high[i] for i in range(count)], 1)


def layers(own, other, a_count, weights, pick, cut):
    units = pick.shape[1]
    width, dense_units = weights[2].shape[1], weights[2].shape[0]
    extra = dense_units - units
    full = width + units
    parts = []
    slots = 0
    for block in own + other:
        if isinstance(block, tuple):
            parts += [(block[0], slots, 0, cut), (block[1], slots, cut, None)]
        else:
            parts.append((block, slots, 0, None))
        slots += 1
    rows = parts[0][0].shape[0]
    b_count = rows - a_count
    half = slots // 2
    n_blocks = len(parts)
    inputs = [p[0] for p in parts] + list(weights) + [pick]
    n_in = len(inputs)
    chunk = 1024

    def body(*refs):
        ins = refs[:n_in]
        own_ref, other_ref = refs[n_in : n_in + 2]
        gate, up, da, e_gate, e_up, db = ins[n_blocks : n_blocks + 6]
        xa, xb, a_acc, b_acc, ha, hb, sems = refs[n_in + 2 :]
        a_copies, b_copies = [], []
        for i, (_, slot, lo, hi) in enumerate(parts):
            a_cols = pl.ds(lo, (width if hi is None else hi) - lo)
            b_cols = pl.ds(lo, (full if hi is None else hi) - lo)
            from_a = ins[i].at[pl.ds(0, a_count), pl.ds(0, a_cols.size)]
            from_b = ins[i].at[pl.ds(a_count, b_count), :]
            a_copies.append(
                pltpu.make_async_copy(from_a, xa.at[pl.ds(slot * a_count, a_count), a_cols], sems.at[2 * i])
            )
            b_copies.append(
                pltpu.make_async_copy(from_b, xb.at[pl.ds(slot * b_count, b_count), b_cols], sems.at[2 * i + 1])
            )
        for c in b_copies + a_copies:
            c.start()
        a_acc[...] = jnp.zeros_like(a_acc)
        b_acc[...] = jnp.zeros_like(b_acc)
        for c in b_copies:
            c.wait()

        def b_step(i, carry):
            at = pl.ds(pl.multiple_of(i * chunk, chunk), chunk)
            w = jnp.concatenate([e_gate[at, :], e_up[at, :]], 1)
            b_acc[...] += jnp.dot(xb[:, at], w, preferred_element_type=jnp.float32)
            return carry

        lax.fori_loop(0, width // chunk, b_step, 0)
        g = b_acc[:, :units]
        value = g * (1.0 / (1.0 + jnp.exp(-g))) * b_acc[:, units:]
        tail = xb[:, width:].astype(jnp.float32) * ins[n_in - 1][...]
        hb[...] = (value * jnp.sum(tail, axis=1, keepdims=True)).astype(jnp.bfloat16)
        for c in a_copies:
            c.wait()

        def a_step(i, carry):
            at = pl.ds(pl.multiple_of(i * chunk, chunk), chunk)
            w = jnp.concatenate([gate[:units, at], up[:units, at], gate[units:, at], up[units:, at]], 0)
            a_acc[...] += lax.dot_general(
                xa[:, at], w, (((1,), (1,)), ((), ())), preferred_element_type=jnp.float32
            )
            return carry

        lax.fori_loop(0, width // chunk, a_step, 0)
        for lo, n, to in ((0, units, 0), (2 * units, extra, units)):
            g = a_acc[:, lo : lo + n]
            u = a_acc[:, lo + n : lo + 2 * n]
            ha[:, to : to + n] = (g * (1.0 / (1.0 + jnp.exp(-g))) * u).astype(jnp.bfloat16)

        def out_step(i, carry):
            at = pl.ds(pl.multiple_of(i * chunk, chunk), chunk)
            for lo, count, h, w in ((0, a_count, ha, da), (a_count, b_count, hb, db)):
                r = jnp.dot(h[...], w[:, at], preferred_element_type=jnp.float32).astype(jnp.bfloat16)
                for slot in range(slots):
                    ref = own_ref if slot < half else other_ref
                    to = pl.ds(slot % half * rows + lo, count)
                    ref[to, at] = r[slot * count : (slot + 1) * count]
            return carry

        lax.fori_loop(0, width // chunk, out_step, 0)

    hbm_spec = pl.BlockSpec(memory_space=pltpu.HBM)
    vmem_spec = pl.BlockSpec(memory_space=pltpu.VMEM)
    a_total, b_total = slots * a_count, slots * b_count
    scratch = [
        ((a_total, width), jnp.bfloat16),
        ((b_total, full), jnp.bfloat16),
        ((a_total, 2 * dense_units), jnp.float32),
        ((b_total, 2 * units), jnp.float32),
        ((a_total, dense_units), jnp.bfloat16),
        ((b_total, units), jnp.bfloat16),
    ]
    return pl.pallas_call(
        body,
        in_specs=[hbm_spec] * n_blocks + [vmem_spec] * 7,
        out_specs=[vmem_spec] * 2,
        out_shape=[jax.ShapeDtypeStruct((half * rows, width), jnp.bfloat16)] * 2,
        scratch_shapes=[pltpu.VMEM(*s) for s in scratch]
        + [pltpu.SemaphoreType.DMA((2 * n_blocks,))],
        cost_estimate=pl.CostEstimate(
            flops=6 * width * (a_total * dense_units + b_total * units),
            bytes_accessed=6 * (dense_units + units) * width + 4 * (a_total + b_total) * width,
            transcendentals=0,
        ),
        compiler_params=pltpu.CompilerParams(vmem_limit_bytes=14 * 1024 * 1024),
    )(*inputs)


def prepare(a_tokens, a_gain, b_tokens, b_gain, expert_ids, route_weights):
    a_rows, width = a_tokens.shape
    rows = a_rows + b_tokens.shape[0]
    lanes = 128
    full = width + lanes

    def body(a_ref, ag_ref, b_ref, bg_ref, id_ref, w_ref, out_ref, hold):
        hold[:a_rows, :width] = normed(a_ref[...].astype(jnp.float32), ag_ref[...])
        hold[:a_rows, width:] = jnp.zeros((a_rows, lanes), jnp.float32)
        hold[a_rows:rows, :width] = normed(b_ref[...].astype(jnp.float32), bg_ref[...])
        lane = lax.broadcasted_iota(jnp.int32, (rows - a_rows, lanes), 1)
        expert = lane & (EXPERTS - 1)
        weight = jnp.zeros((rows - a_rows, lanes), jnp.float32)
        for k in range(expert_ids.shape[1]):
            weight += jnp.where(id_ref[:, k : k + 1] == expert, w_ref[:, k : k + 1], 0.0)
        first = weight.astype(jnp.bfloat16).astype(jnp.float32)
        second = (weight - first).astype(jnp.bfloat16).astype(jnp.float32)
        third = weight - first - second
        part = jnp.where(lane < EXPERTS, first, jnp.where(lane < 2 * EXPERTS, second, third))
        hold[a_rows:rows, width:] = jnp.where(lane < 3 * EXPERTS, part, 0.0)
        value = hold[:rows, :].astype(jnp.bfloat16)
        for i in range(RING):
            out_ref[i] = value

    vmem_spec = pl.BlockSpec(memory_space=pltpu.VMEM)
    return pl.pallas_call(
        body,
        in_specs=[vmem_spec] * 6,
        out_specs=vmem_spec,
        out_shape=jax.ShapeDtypeStruct((RING, rows, full), jnp.bfloat16),
        scratch_shapes=[pltpu.VMEM((8, full), jnp.float32)],
        cost_estimate=pl.CostEstimate(flops=20_000_000_000, bytes_accessed=1_000_000, transcendentals=0),
        compiler_params=pltpu.CompilerParams(vmem_limit_bytes=4 * 1024 * 1024),
        name="prepare",
    )(a_tokens, a_gain[None], b_tokens, b_gain[None], expert_ids, route_weights)


def pack(near, a_rows):
    places, rows, full = near.shape
    b_rows = rows - a_rows

    def body(near_ref, out_ref, hold):
        for i in range(places):
            value = near_ref[i].astype(jnp.float32)
            hold[pl.ds(i * a_rows, a_rows), :] = value[:a_rows]
            hold[pl.ds(places * a_rows + i * b_rows, b_rows), :] = value[a_rows:]
        out_ref[...] = hold[...].astype(jnp.bfloat16)

    vmem_spec = pl.BlockSpec(memory_space=pltpu.VMEM)
    return pl.pallas_call(
        body,
        in_specs=[vmem_spec],
        out_specs=vmem_spec,
        out_shape=jax.ShapeDtypeStruct((places * rows, full), jnp.bfloat16),
        scratch_shapes=[pltpu.VMEM((places * rows, full), jnp.float32)],
        compiler_params=pltpu.CompilerParams(vmem_limit_bytes=6 * 1024 * 1024),
        name="pack",
    )(near)


def shards(
    a_tokens,
    a_gain,
    dense_gate,
    dense_up,
    dense_down,
    b_tokens,
    b_gain,
    expert_ids,
    route_weights,
    expert_gate,
    expert_up,
    expert_down,
):
    devices = lax.axis_size(EXP)
    group_size = devices // EXPERTS
    width = b_tokens.shape[1]
    a_rows = a_tokens.shape[0]
    b_rows = b_tokens.shape[0]
    a_float = a_tokens.astype(jnp.float32)
    b_float = b_tokens.astype(jnp.float32)
    ready = prepare(a_tokens, a_gain, b_tokens, b_gain, expert_ids, route_weights)
    full = ready.shape[2]
    block = pack(exchange(ready), a_rows)
    cut = width // 2
    slots = gather_ring(block, cut)
    swapped = {
        k: tuple(swap_cores(p) for p in s) if isinstance(s, tuple) else swap_cores(s)
        for k, s in slots.items()
    }
    expert = lax.axis_index(EXP) // group_size
    lanes = jnp.arange(full - width)
    pick = ((lanes % EXPERTS == expert) & (lanes < 3 * EXPERTS)).astype(jnp.float32)[None, :]
    weights = (
        dense_gate.T,
        dense_up.T,
        dense_down,
        expert_gate[0],
        expert_up[0],
        expert_down[0],
    )
    own, other = {}, {}
    rows = block.shape[0]
    for group in GROUPS:
        mine, theirs = layers(
            [slots[k] for k in group],
            [swapped[k] for k in group],
            RING * a_rows,
            weights,
            pick,
            cut,
        )
        theirs = swap_cores(theirs)
        for i, k in enumerate(group):
            own[k] = mine[i * rows : (i + 1) * rows]
            other[k] = theirs[i * rows : (i + 1) * rows]
    streams = (0, width * 3 // 7, width)
    total = scatter_ring(own, other, streams)
    both_sum = jnp.concatenate(
        [
            total[: RING * a_rows].reshape(RING, a_rows, width),
            total[RING * a_rows :].reshape(RING, b_rows, width),
        ],
        1,
    )
    back = exchange(both_sum.astype(jnp.bfloat16)).astype(jnp.float32)
    total = jnp.sum(back, axis=0)
    a_out = (a_float + total[:a_rows]).astype(jnp.bfloat16)
    b_out = (b_float + total[a_rows:]).astype(jnp.bfloat16)
    return (a_out, b_out)


def solution(mesh):
    finer = Mesh(
        mesh.devices.reshape(mesh.shape["rep"], RING, RING, CORES),
        ("rep", "exp_0", "exp_1", "exp_2"),
    )
    placed = (
        P(REP_EXP, None),
        P(),
        P(None, EXP),
        P(None, EXP),
        P(EXP, None),
        P(REP_EXP, None),
        P(),
        P(REP_EXP, None),
        P(REP_EXP, None),
        P(EXP, None, None),
        P(EXP, None, None),
        P(EXP, None, None),
    )
    return jax.shard_map(
        shards,
        mesh=finer,
        in_specs=placed,
        out_specs=(P(REP_EXP, None), P(REP_EXP, None)),
        check_vma=False,
    )
```

profile of v0, /device:TPU:528, one launch (start us, length us, event | category | flops | bytes accessed | tf_op | source)
XLA Modules:
  0.0 217.1 jit_solution(4084348732360111025)
XLA Ops:
  0.6 0.8 copy-done.19
  1.5 0.7 copy-done.21
  2.2 0.7 copy-done.23
  3.0 0.7 copy-done.24
  3.7 0.7 copy-done.25
  4.4 0.7 copy-done.26
  5.1 0.3 prepare.1
  5.3 38.2 %all_to_all.10.near_ref = bf16[8,6,7296]{2,1,0:T(8,128)(2,1)S(1)} all-to-all(bf16[8,6,7296]{2,1,0:T(8,128)(2,1)S(1)} %prepare.1), channel_id=1, replica_groups={{0,2,4,6,8,10,12,14},{16,18,20,22,24,26,28,30},{32,34,36,38,40,42,44,46..., dimensions={0} | all-to-all | bytes 1400832 | tf_op jit(solution)/shard_map/all_to_all | solution.py:64
  43.5 0.3 pack.1.refs_0_
  44.2 10.9 %collective-permute-done.2.refs_0_ = bf16[48,7296]{1,0:T(8,128)(2,1)S(1)} collective-permute-done((bf16[48,7296]{1,0:T(8,128)(2,1)S(1)}, bf16[48,7296]{1,0:T(8,128)(2,1)S(1)}, u32[]{:S(2)}, u32[]{:S(2)}) %collective-permute-start.2) | collective-permute-done | bytes 700448 | tf_op jit(solution)/shard_map/ppermute | solution.py:38
  55.1 1.4 collective-permute-done.3.refs_1_
  56.4 0.7 collective-permute-start.7
  57.1 10.3 %collective-permute-done.8.refs_1_ = bf16[48,7296]{1,0:T(8,128)(2,1)S(1)} collective-permute-done((bf16[48,7296]{1,0:T(8,128)(2,1)S(1)}, bf16[48,7296]{1,0:T(8,128)(2,1)S(1)}, u32[]{:S(2)}, u32[]{:S(2)}) %collective-permute-start.8) | collective-permute-done | bytes 700448 | tf_op jit(solution)/shard_map/ppermute | solution.py:42
  67.5 0.7 copy-done.11
  68.2 1.2 collective-permute-start.13
  69.4 9.0 %collective-permute-done.12.refs_0_ = bf16[48,7296]{1,0:T(8,128)(2,1)S(1)} collective-permute-done((bf16[48,7296]{1,0:T(8,128)(2,1)S(1)}, bf16[48,7296]{1,0:T(8,128)(2,1)S(1)}, u32[]{:S(2)}, u32[]{:S(2)}) %collective-permute-start.12) | collective-permute-done | bytes 700448 | tf_op jit(solution)/shard_map/ppermute | solution.py:38
  78.7 1.8 collective-permute-done.13.refs_1_
  80.6 1.0 slice.259
  81.8 5.5 %collective-permute-done.15.refs_3_ = bf16[48,3712]{1,0:T(8,128)(2,1)} collective-permute-done((bf16[48,3712]{1,0:T(8,128)(2,1)S(1)}, bf16[48,3712]{1,0:T(8,128)(2,1)}, u32[]{:S(2)}, u32[]{:S(2)}) %collective-permute-start.15) | collective-permute-done | bytes 356384 | tf_op jit(solution)/shard_map/ppermute | solution.py:42
  87.3 1.8 collective-permute-done.14.refs_2_
  89.1 2.0 collective-permute-done.18.refs_6_
  91.1 1.6 copy-done.1
  92.7 1.6 copy-done.3
  94.2 1.5 copy-done.5
  95.7 1.5 copy-done.7
  97.2 1.5 copy-done.9
  98.8 9.2 %shard_map.134 = (bf16[144,7168]{1,0:T(8,128)(2,1)S(1)}, bf16[144,7168]{1,0:T(8,128)(2,1)S(1)}) custom-call(bf16[48,7296]{1,0:T(8,128)(2,1)S(1)} %collective-permute-done.12.refs_0_, bf16[48,7296]{1,0:T(8,128)(2,1)} %collective-permute-done.13.refs_1_, bf16[48,3584]{1,0:T(8,128)(2,1)} %collective-permute-done.14.refs_2_, ...), custom_call_target="tpu_custom_call" | custom-call | flops 1651507200 | bytes 19955712 | tf_op jit(solution)/shard_map/pallas_call | solution.py:205
  108.0 0.3 collective-permute-start.20
  108.2 0.4 collective-permute-start
  108.8 0.4 collective-permute-start.5
  109.1 0.3 collective-permute-start.10
  109.4 3.8 %collective-permute-done.refs_1_ = bf16[48,7296]{1,0:T(8,128)(2,1)S(1)} collective-permute-done((bf16[48,7296]{1,0:T(8,128)(2,1)S(1)}, bf16[48,7296]{1,0:T(8,128)(2,1)S(1)}, u32[]{:S(2)}, u32[]{:S(2)}) %collective-permute-start) | collective-permute-done | bytes 700448 | tf_op jit(solution)/shard_map/ppermute | solution.py:47
  113.4 6.3 %shard_map.131 = (bf16[48,7168]{1,0:T(8,128)(2,1)S(1)}, bf16[48,7168]{1,0:T(8,128)(2,1)S(1)}) custom-call(bf16[48,7296]{1,0:T(8,128)(2,1)S(1)} %pack.1.refs_0_, bf16[48,7296]{1,0:T(8,128)(2,1)S(1)} %collective-permute-done.refs_1_, bf16[144,7168]{1,0:T(8,128)(2,1)S(1)} %bitcast.8, bf16[144,7168]{1,0:T(8,128)(2,1)S(1)} %bitcast.12, ...), custom_call_target="tpu_custom_call" | custom-call | flops 550502400 | bytes 14450688 | tf_op jit(solution)/shard_map/pallas_call | solution.py:205
  119.7 0.5 collective-permute-start.1
  120.2 8.0 %shard_map.132 = (bf16[96,7168]{1,0:T(8,128)(2,1)S(1)}, bf16[96,7168]{1,0:T(8,128)(2,1)S(1)}) custom-call(bf16[48,7296]{1,0:T(8,128)(2,1)S(1)} %copy-done.14, bf16[48,7296]{1,0:T(8,128)(2,1)S(1)} %copy-done.18, bf16[48,7296]{1,0:T(8,128)(2,1)S(1)} %collective-permute-done.4.refs_2_, bf16[48,7296]{1,0:T(8,128)(2,1)S(1)} %collective-permute-done.5.refs_3_, ...), custom_call_target="tpu_custom_call" | custom-call | flops 1101004800 | bytes 17203200 | tf_op jit(solution)/shard_map/pallas_call | solution.py:205
  128.4 8.0 %shard_map.133 = (bf16[96,7168]{1,0:T(8,128)(2,1)S(1)}, bf16[96,7168]{1,0:T(8,128)(2,1)S(1)}) custom-call(bf16[48,7296]{1,0:T(8,128)(2,1)S(1)} %copy-done.16, bf16[48,7296]{1,0:T(8,128)(2,1)S(1)} %copy-done.12, bf16[48,7296]{1,0:T(8,128)(2,1)S(1)} %collective-permute-done.9.refs_2_, bf16[48,7296]{1,0:T(8,128)(2,1)S(1)} %collective-permute-done.10.refs_3_, ...), custom_call_target="tpu_custom_call" | custom-call | flops 1101004800 | bytes 17203200 | tf_op jit(solution)/shard_map/pallas_call | solution.py:205
  136.4 0.5 collective-permute-start.11
  137.1 1.8 collective-permute-start.25
  139.4 4.2 %collective-permute-done.25 = bf16[48,1536]{1,0:T(8,128)(2,1)S(1)} collective-permute-done((bf16[48,1536]{1,0:T(8,128)(2,1)S(1)}, bf16[48,1536]{1,0:T(8,128)(2,1)S(1)}, u32[]{:S(2)}, u32[]{:S(2)}) %collective-permute-start.25) | collective-permute-done | bytes 147488 | tf_op jit(solution)/shard_map/ppermute | solution.py:42
  143.6 1.7 collective-permute-start.33
  145.6 4.9 %collective-permute-done.33 = bf16[48,2048]{1,0:T(8,128)(2,1)S(1)} collective-permute-done((bf16[48,2048]{1,0:T(8,128)(2,1)S(1)}, bf16[48,2048]{1,0:T(8,128)(2,1)S(1)}, u32[]{:S(2)}, u32[]{:S(2)}) %collective-permute-start.33) | collective-permute-done | bytes 196640 | tf_op jit(solution)/shard_map/ppermute | solution.py:42
  150.5 0.6 collective-permute-done.29
  151.2 1.5 collective-permute-start.22
  152.9 4.2 %collective-permute-done.26 = bf16[48,3072]{1,0:T(8,128)(2,1)S(1)} collective-permute-done((bf16[48,3072]{1,0:T(8,128)(2,1)S(1)}, bf16[48,3072]{1,0:T(8,128)(2,1)S(1)}, u32[]{:S(2)}, u32[]{:S(2)}) %collective-permute-start.26) | collective-permute-done | bytes 294944 | tf_op jit(solution)/shard_map/ppermute | solution.py:38
  157.2 1.7 collective-permute-start.30
  159.3 0.4 collective-permute-start.23
  159.8 1.6 collective-permute-done.34
  161.4 1.7 collective-permute-start.27
  163.1 3.0 %collective-permute-done.30 = bf16[48,4096]{1,0:T(8,128)(2,1)S(1)} collective-permute-done((bf16[48,4096]{1,0:T(8,128)(2,1)S(1)}, bf16[48,4096]{1,0:T(8,128)(2,1)S(1)}, u32[]{:S(2)}, u32[]{:S(2)}) %collective-permute-start.30) | collective-permute-done | bytes 393248 | tf_op jit(solution)/shard_map/ppermute | solution.py:42
  166.2 0.3 add_convert_fusion.3
  166.6 2.1 collective-permute-start.35
  168.7 0.6 collective-permute-done.27
  169.6 1.8 collective-permute-start.24
  171.4 3.0 %collective-permute-done.31 = bf16[48,4096]{1,0:T(8,128)(2,1)S(1)} collective-permute-done((bf16[48,4096]{1,0:T(8,128)(2,1)S(1)}, bf16[48,4096]{1,0:T(8,128)(2,1)S(1)}, u32[]{:S(2)}, u32[]{:S(2)}) %collective-permute-start.31) | collective-permute-done | bytes 393248 | tf_op jit(solution)/shard_map/ppermute | solution.py:38
  174.4 1.6 collective-permute-done.35
  176.0 0.3 add_convert_fusion.2
  176.2 1.8 collective-permute-start.32
  178.1 1.0 collective-permute-done.24
  179.3 6.1 %collective-permute-done.32 = bf16[48,4096]{1,0:T(8,128)(2,1)S(1)} collective-permute-done((bf16[48,4096]{1,0:T(8,128)(2,1)S(1)}, bf16[48,4096]{1,0:T(8,128)(2,1)S(1)}, u32[]{:S(2)}, u32[]{:S(2)}) %collective-permute-start.32) | collective-permute-done | bytes 393248 | tf_op jit(solution)/shard_map/ppermute | solution.py:42
  185.4 2.0 collective-permute-done.36
  187.9 0.4 pad_maximum_fusion.1
  188.4 27.2 %all_to_all.11 = bf16[8,6,7168]{2,1,0:T(8,128)(2,1)S(1)} all-to-all(bf16[8,6,7168]{2,1,0:T(8,128)(2,1)S(1)} %pad_maximum_fusion.1), channel_id=1, replica_groups={{0,2,4,6,8,10,12,14},{16,18,20,22,24,26,28,30},{32,34,36,38,40,42,44,46..., dimensions={0} | all-to-all | bytes 1376256 | tf_op jit(solution)/shard_map/all_to_all | solution.py:64
  215.8 0.7 fusion.5
  216.5 0.6 fusion.6
  (105 shorter events, 4.3 us)
Async XLA Ops:
  0.6 0.8 copy-start.19
  1.5 0.7 copy-start.21
  2.2 0.7 copy-start.23
  3.0 0.7 copy-start.24
  3.7 0.7 copy-start.25
  4.4 0.7 copy-start.26
  43.5 47.5 %copy-start = (bf16[7168,144]{0,1:T(8,128)(2,1)S(1)}, bf16[7168,144]{0,1:T(8,128)(2,1)}, u32[]{:S(2)}) copy-start(bf16[7168,144]{0,1:T(8,128)(2,1)} %param.14) | copy-start | bytes 6193156
  43.9 11.2 %collective-permute-start.2 = (bf16[48,7296]{1,0:T(8,128)(2,1)S(1)}, bf16[48,7296]{1,0:T(8,128)(2,1)S(1)}, u32[]{:S(2)}, u32[]{:S(2)}) collective-permute-start(bf16[48,7296]{1,0:T(8,128)(2,1)S(1)} %pack.1.refs_0_), channel_id=1, source_target_pairs={{0,16},{1,3},{2,18},{3,1},{4,20},{5,7},{6,22},{7,5},{8,24},{9,11},... | collective-permute-start | bytes 2101256 | tf_op jit(solution)/shard_map/ppermute | solution.py:38
  44.0 12.4 %collective-permute-start.3 = (bf16[48,7296]{1,0:T(8,128)(2,1)S(1)}, bf16[48,7296]{1,0:T(8,128)(2,1)S(1)}, u32[]{:S(2)}, u32[]{:S(2)}) collective-permute-start(bf16[48,7296]{1,0:T(8,128)(2,1)S(1)} %pack.1.refs_0_), channel_id=1, source_target_pairs={{0,112},{1,15},{2,114},{3,5},{4,116},{5,3},{6,118},{7,9},{8,120},{... | collective-permute-start | bytes 2101256 | tf_op jit(solution)/shard_map/ppermute | solution.py:42
  55.0 14.3 %copy-start.13 = (bf16[48,7296]{1,0:T(8,128)(2,1)}, bf16[48,7296]{1,0:T(8,128)(2,1)S(1)}, u32[]{:S(2)}) copy-start(bf16[48,7296]{1,0:T(8,128)(2,1)S(1)} %collective-permute-done.2.refs_0_) | copy-start | bytes 2101252
  55.1 12.3 %collective-permute-start.8 = (bf16[48,7296]{1,0:T(8,128)(2,1)S(1)}, bf16[48,7296]{1,0:T(8,128)(2,1)S(1)}, u32[]{:S(2)}, u32[]{:S(2)}) collective-permute-start(bf16[48,7296]{1,0:T(8,128)(2,1)S(1)} %collective-permute-done.2.refs_0_), channel_id=1, source_target_pairs={{0,112},{1,15},{2,114},{3,5},{4,116},{5,3},{6,118},{7,9},{8,120},{... | collective-permute-start | bytes 2101256 | tf_op jit(solution)/shard_map/ppermute | solution.py:42
  56.4 13.0 %copy-start.17 = (bf16[48,7296]{1,0:T(8,128)(2,1)}, bf16[48,7296]{1,0:T(8,128)(2,1)S(1)}, u32[]{:S(2)}) copy-start(bf16[48,7296]{1,0:T(8,128)(2,1)S(1)} %collective-permute-done.3.refs_1_) | copy-start | bytes 2101252
  56.4 11.1 %collective-permute-start.7 = (bf16[48,7296]{1,0:T(8,128)(2,1)S(1)}, bf16[48,7296]{1,0:T(8,128)(2,1)S(1)}, u32[]{:S(2)}, u32[]{:S(2)}) collective-permute-start(bf16[48,7296]{1,0:T(8,128)(2,1)S(1)} %collective-permute-done.3.refs_1_), channel_id=1, source_target_pairs={{0,16},{1,3},{2,18},{3,1},{4,20},{5,7},{6,22},{7,5},{8,24},{9,11},... | collective-permute-start | bytes 2101256 | tf_op jit(solution)/shard_map/ppermute | solution.py:38
  67.3 0.9 copy-start.11
  67.3 11.1 %collective-permute-start.12 = (bf16[48,7296]{1,0:T(8,128)(2,1)S(1)}, bf16[48,7296]{1,0:T(8,128)(2,1)S(1)}, u32[]{:S(2)}, u32[]{:S(2)}) collective-permute-start(bf16[48,7296]{1,0:T(8,128)(2,1)S(1)} %collective-permute-done.8.refs_1_), channel_id=1, source_target_pairs={{0,16},{1,3},{2,18},{3,1},{4,20},{5,7},{6,22},{7,5},{8,24},{9,11},... | collective-permute-start | bytes 2101256 | tf_op jit(solution)/shard_map/ppermute | solution.py:38
  68.2 10.2 %copy-start.15 = (bf16[48,7296]{1,0:T(8,128)(2,1)}, bf16[48,7296]{1,0:T(8,128)(2,1)S(1)}, u32[]{:S(2)}) copy-start(bf16[48,7296]{1,0:T(8,128)(2,1)S(1)} %collective-permute-done.7.refs_0_) | copy-start | bytes 2101252
  68.2 12.4 %collective-permute-start.13 = (bf16[48,7296]{1,0:T(8,128)(2,1)S(1)}, bf16[48,7296]{1,0:T(8,128)(2,1)}, u32[]{:S(2)}, u32[]{:S(2)}) collective-permute-start(bf16[48,7296]{1,0:T(8,128)(2,1)S(1)} %collective-permute-done.7.refs_0_), channel_id=1, source_target_pairs={{0,112},{1,15},{2,114},{3,5},{4,116},{5,3},{6,118},{7,9},{8,120},{... | collective-permute-start | bytes 2101256 | tf_op jit(solution)/shard_map/ppermute | solution.py:42
  78.4 8.8 %collective-permute-start.15 = (bf16[48,3712]{1,0:T(8,128)(2,1)S(1)}, bf16[48,3712]{1,0:T(8,128)(2,1)}, u32[]{:S(2)}, u32[]{:S(2)}) collective-permute-start(bf16[48,3712]{1,0:T(8,128)(2,1)S(1)} %slice.260), channel_id=1, source_target_pairs={{0,112},{1,15},{2,114},{3,5},{4,116},{5,3},{6,118},{7,9},{8,120},{... | collective-permute-start | bytes 1069064 | tf_op jit(solution)/shard_map/ppermute | solution.py:42
  78.6 12.5 %collective-permute-start.16 = (bf16[48,7296]{1,0:T(8,128)(2,1)S(1)}, bf16[48,7296]{1,0:T(8,128)(2,1)}, u32[]{:S(2)}, u32[]{:S(2)}) collective-permute-start(bf16[48,7296]{1,0:T(8,128)(2,1)S(1)} %collective-permute-done.12.refs_0_), channel_id=1, source_target_pairs={{0,1},{1,0},{2,3},{3,2},{4,5},{5,4},{6,7},{7,6},{8,9},{9,8},{10,11... | collective-permute-start | bytes 2101256 | tf_op jit(solution)/shard_map/ppermute | solution.py:47
  80.6 10.5 %collective-permute-start.17 = (bf16[48,7296]{1,0:T(8,128)(2,1)}, bf16[48,7296]{1,0:T(8,128)(2,1)}, u32[]{:S(2)}, u32[]{:S(2)}) collective-permute-start(bf16[48,7296]{1,0:T(8,128)(2,1)} %collective-permute-done.13.refs_1_), channel_id=1, source_target_pairs={{0,1},{1,0},{2,3},{3,2},{4,5},{5,4},{6,7},{7,6},{8,9},{9,8},{10,11... | collective-permute-start | bytes 2101256 | tf_op jit(solution)/shard_map/ppermute | solution.py:47
  81.6 7.5 %collective-permute-start.14 = (bf16[48,3584]{1,0:T(8,128)(2,1)S(1)}, bf16[48,3584]{1,0:T(8,128)(2,1)}, u32[]{:S(2)}, u32[]{:S(2)}) collective-permute-start(bf16[48,3584]{1,0:T(8,128)(2,1)S(1)} %slice.259), channel_id=1, source_target_pairs={{0,16},{1,3},{2,18},{3,1},{4,20},{5,7},{6,22},{7,5},{8,24},{9,11},... | collective-permute-start | bytes 1032200 | tf_op jit(solution)/shard_map/ppermute | solution.py:38
  87.3 3.8 %collective-permute-start.19 = (bf16[48,3712]{1,0:T(8,128)(2,1)}, bf16[48,3712]{1,0:T(8,128)(2,1)}, u32[]{:S(2)}, u32[]{:S(2)}) collective-permute-start(bf16[48,3712]{1,0:T(8,128)(2,1)} %collective-permute-done.15.refs_3_), channel_id=1, source_target_pairs={{0,1},{1,0},{2,3},{3,2},{4,5},{5,4},{6,7},{7,6},{8,9},{9,8},{10,11... | collective-permute-start | bytes 1069064 | tf_op jit(solution)/shard_map/ppermute | solution.py:47
  89.1 2.0 collective-permute-start.18
  91.1 1.6 copy-start.1
  92.7 1.6 copy-start.3
  94.2 1.5 copy-start.5
  95.7 1.5 copy-start.7
  97.2 1.5 copy-start.9
  98.7 9.9 %copy-start.14 = (bf16[48,7296]{1,0:T(8,128)(2,1)S(1)}, bf16[48,7296]{1,0:T(8,128)(2,1)}, u32[]{:S(2)}) copy-start(bf16[48,7296]{1,0:T(8,128)(2,1)} %copy-done.13) | copy-start | bytes 2101252
  98.7 10.0 %copy-start.18 = (bf16[48,7296]{1,0:T(8,128)(2,1)S(1)}, bf16[48,7296]{1,0:T(8,128)(2,1)}, u32[]{:S(2)}) copy-start(bf16[48,7296]{1,0:T(8,128)(2,1)} %copy-done.17) | copy-start | bytes 2101252
  98.7 10.4 %copy-start.12 = (bf16[48,7296]{1,0:T(8,128)(2,1)S(1)}, bf16[48,7296]{1,0:T(8,128)(2,1)}, u32[]{:S(2)}) copy-start(bf16[48,7296]{1,0:T(8,128)(2,1)} %copy-done.11) | copy-start | bytes 2101252
  98.8 14.5 %copy-start.16 = (bf16[48,7296]{1,0:T(8,128)(2,1)S(1)}, bf16[48,7296]{1,0:T(8,128)(2,1)}, u32[]{:S(2)}) copy-start(bf16[48,7296]{1,0:T(8,128)(2,1)} %copy-done.15) | copy-start | bytes 2101252
  98.8 14.6 %copy-start.2 = (bf16[7168,144]{0,1:T(8,128)(2,1)S(1)}, bf16[7168,144]{0,1:T(8,128)(2,1)}, u32[]{:S(2)}) copy-start(bf16[7168,144]{0,1:T(8,128)(2,1)} %param.15) | copy-start | bytes 6193156
  98.8 14.6 %copy-start.4 = (bf16[144,7168]{1,0:T(8,128)(2,1)S(1)}, bf16[144,7168]{1,0:T(8,128)(2,1)}, u32[]{:S(2)}) copy-start(bf16[144,7168]{1,0:T(8,128)(2,1)} %refs_10_.1) | copy-start | bytes 6193156
  98.8 14.6 %copy-start.6 = (bf16[1,7168,128]{2,1,0:T(8,128)(2,1)S(1)}, bf16[1,7168,128]{2,1,0:T(8,128)(2,1)}, u32[]{:S(2)}) copy-start(bf16[1,7168,128]{2,1,0:T(8,128)(2,1)} %param.21) | copy-start | bytes 5505028
  98.8 14.6 %copy-start.8 = (bf16[1,7168,128]{2,1,0:T(8,128)(2,1)S(1)}, bf16[1,7168,128]{2,1,0:T(8,128)(2,1)}, u32[]{:S(2)}) copy-start(bf16[1,7168,128]{2,1,0:T(8,128)(2,1)} %param.22) | copy-start | bytes 5505028
  98.8 14.6 %copy-start.10 = (bf16[1,128,7168]{2,1,0:T(8,128)(2,1)S(1)}, bf16[1,128,7168]{2,1,0:T(8,128)(2,1)}, u32[]{:S(2)}) copy-start(bf16[1,128,7168]{2,1,0:T(8,128)(2,1)} %param.23) | copy-start | bytes 5505028
  108.0 28.9 %collective-permute-start.20 = (bf16[144,7168]{1,0:T(8,128)(2,1)S(1)}, bf16[144,7168]{1,0:T(8,128)(2,1)S(1)}, u32[]{:S(2)}, u32[]{:S(2)}) collective-permute-start(bf16[144,7168]{1,0:T(8,128)(2,1)S(1)} %get-tuple-element.17), channel_id=1, source_target_pairs={{0,1},{1,0},{2,3},{3,2},{4,5},{5,4},{6,7},{7,6},{8,9},{9,8},{10,11... | collective-permute-start | bytes 6193160 | tf_op jit(solution)/shard_map/ppermute | solution.py:47
  108.2 5.0 %collective-permute-start = (bf16[48,7296]{1,0:T(8,128)(2,1)S(1)}, bf16[48,7296]{1,0:T(8,128)(2,1)S(1)}, u32[]{:S(2)}, u32[]{:S(2)}) collective-permute-start(bf16[48,7296]{1,0:T(8,128)(2,1)S(1)} %pack.1.refs_0_), channel_id=1, source_target_pairs={{0,1},{1,0},{2,3},{3,2},{4,5},{5,4},{6,7},{7,6},{8,9},{9,8},{10,11... | collective-permute-start | bytes 2101256 | tf_op jit(solution)/shard_map/ppermute | solution.py:47
  108.6 11.1 %collective-permute-start.4 = (bf16[48,7296]{1,0:T(8,128)(2,1)S(1)}, bf16[48,7296]{1,0:T(8,128)(2,1)S(1)}, u32[]{:S(2)}, u32[]{:S(2)}) collective-permute-start(bf16[48,7296]{1,0:T(8,128)(2,1)S(1)} %copy-done.14), channel_id=1, source_target_pairs={{0,1},{1,0},{2,3},{3,2},{4,5},{5,4},{6,7},{7,6},{8,9},{9,8},{10,11... | collective-permute-start | bytes 2101256 | tf_op jit(solution)/shard_map/ppermute | solution.py:47
  108.8 11.4 %collective-permute-start.5 = (bf16[48,7296]{1,0:T(8,128)(2,1)S(1)}, bf16[48,7296]{1,0:T(8,128)(2,1)S(1)}, u32[]{:S(2)}, u32[]{:S(2)}) collective-permute-start(bf16[48,7296]{1,0:T(8,128)(2,1)S(1)} %copy-done.18), channel_id=1, source_target_pairs={{0,1},{1,0},{2,3},{3,2},{4,5},{5,4},{6,7},{7,6},{8,9},{9,8},{10,11... | collective-permute-start | bytes 2101256 | tf_op jit(solution)/shard_map/ppermute | solution.py:47
  109.1 19.3 %collective-permute-start.10 = (bf16[48,7296]{1,0:T(8,128)(2,1)S(1)}, bf16[48,7296]{1,0:T(8,128)(2,1)S(1)}, u32[]{:S(2)}, u32[]{:S(2)}) collective-permute-start(bf16[48,7296]{1,0:T(8,128)(2,1)S(1)} %copy-done.12), channel_id=1, source_target_pairs={{0,1},{1,0},{2,3},{3,2},{4,5},{5,4},{6,7},{7,6},{8,9},{9,8},{10,11... | collective-permute-start | bytes 2101256 | tf_op jit(solution)/shard_map/ppermute | solution.py:47
  113.2 15.2 %collective-permute-start.9 = (bf16[48,7296]{1,0:T(8,128)(2,1)S(1)}, bf16[48,7296]{1,0:T(8,128)(2,1)S(1)}, u32[]{:S(2)}, u32[]{:S(2)}) collective-permute-start(bf16[48,7296]{1,0:T(8,128)(2,1)S(1)} %copy-done.16), channel_id=1, source_target_pairs={{0,1},{1,0},{2,3},{3,2},{4,5},{5,4},{6,7},{7,6},{8,9},{9,8},{10,11... | collective-permute-start | bytes 2101256 | tf_op jit(solution)/shard_map/ppermute | solution.py:47
  119.7 58.4 %collective-permute-start.1 = (bf16[48,7168]{1,0:T(8,128)(2,1)S(1)}, bf16[48,7168]{1,0:T(8,128)(2,1)S(1)}, u32[]{:S(2)}, u32[]{:S(2)}) collective-permute-start(bf16[48,7168]{1,0:T(8,128)(2,1)S(1)} %get-tuple-element.11), channel_id=1, source_target_pairs={{0,1},{1,0},{2,3},{3,2},{4,5},{5,4},{6,7},{7,6},{8,9},{9,8},{10,11... | collective-permute-start | bytes 2064392 | tf_op jit(solution)/shard_map/ppermute | solution.py:47
  128.2 38.5 %collective-permute-start.6 = (bf16[96,7168]{1,0:T(8,128)(2,1)S(1)}, bf16[96,7168]{1,0:T(8,128)(2,1)S(1)}, u32[]{:S(2)}, u32[]{:S(2)}) collective-permute-start(bf16[96,7168]{1,0:T(8,128)(2,1)S(1)} %get-tuple-element.13), channel_id=1, source_target_pairs={{0,1},{1,0},{2,3},{3,2},{4,5},{5,4},{6,7},{7,6},{8,9},{9,8},{10,11... | collective-permute-start | bytes 4128776 | tf_op jit(solution)/shard_map/ppermute | solution.py:47
  136.4 16.4 %collective-permute-start.11 = (bf16[96,7168]{1,0:T(8,128)(2,1)S(1)}, bf16[96,7168]{1,0:T(8,128)(2,1)S(1)}, u32[]{:S(2)}, u32[]{:S(2)}) collective-permute-start(bf16[96,7168]{1,0:T(8,128)(2,1)S(1)} %get-tuple-element.15), channel_id=1, source_target_pairs={{0,1},{1,0},{2,3},{3,2},{4,5},{5,4},{6,7},{7,6},{8,9},{9,8},{10,11... | collective-permute-start | bytes 4128776 | tf_op jit(solution)/shard_map/ppermute | solution.py:47
  137.1 6.5 %collective-permute-start.25 = (bf16[48,1536]{1,0:T(8,128)(2,1)S(1)}, bf16[48,1536]{1,0:T(8,128)(2,1)S(1)}, u32[]{:S(2)}, u32[]{:S(2)}) collective-permute-start(bf16[48,1536]{1,0:T(8,128)(2,1)S(1)} %get-tuple-element.35), channel_id=1, source_target_pairs={{0,112},{1,15},{2,114},{3,5},{4,116},{5,3},{6,118},{7,9},{8,120},{... | collective-permute-start | bytes 442376 | tf_op jit(solution)/shard_map/ppermute | solution.py:42
  139.0 6.4 %collective-permute-start.21 = (bf16[48,1536]{1,0:T(8,128)(2,1)S(1)}, bf16[48,1536]{1,0:T(8,128)(2,1)S(1)}, u32[]{:S(2)}, u32[]{:S(2)}) collective-permute-start(bf16[48,1536]{1,0:T(8,128)(2,1)S(1)} %get-tuple-element.34), channel_id=1, source_target_pairs={{0,16},{1,3},{2,18},{3,1},{4,20},{5,7},{6,22},{7,5},{8,24},{9,11},... | collective-permute-start | bytes 442376 | tf_op jit(solution)/shard_map/ppermute | solution.py:38
  143.6 6.9 %collective-permute-start.33 = (bf16[48,2048]{1,0:T(8,128)(2,1)S(1)}, bf16[48,2048]{1,0:T(8,128)(2,1)S(1)}, u32[]{:S(2)}, u32[]{:S(2)}) collective-permute-start(bf16[48,2048]{1,0:T(8,128)(2,1)S(1)} %get-tuple-element.33), channel_id=1, source_target_pairs={{0,112},{1,15},{2,114},{3,5},{4,116},{5,3},{6,118},{7,9},{8,120},{... | collective-permute-start | bytes 589832 | tf_op jit(solution)/shard_map/ppermute | solution.py:42
  145.4 5.8 %collective-permute-start.29 = (bf16[48,2048]{1,0:T(8,128)(2,1)S(1)}, bf16[48,2048]{1,0:T(8,128)(2,1)S(1)}, u32[]{:S(2)}, u32[]{:S(2)}) collective-permute-start(bf16[48,2048]{1,0:T(8,128)(2,1)S(1)} %get-tuple-element.32), channel_id=1, source_target_pairs={{0,16},{1,3},{2,18},{3,1},{4,20},{5,7},{6,22},{7,5},{8,24},{9,11},... | collective-permute-start | bytes 589832 | tf_op jit(solution)/shard_map/ppermute | solution.py:38
  150.5 6.7 %collective-permute-start.26 = (bf16[48,3072]{1,0:T(8,128)(2,1)S(1)}, bf16[48,3072]{1,0:T(8,128)(2,1)S(1)}, u32[]{:S(2)}, u32[]{:S(2)}) collective-permute-start(bf16[48,3072]{1,0:T(8,128)(2,1)S(1)} %pad_maximum_fusion.5), channel_id=1, source_target_pairs={{0,16},{1,3},{2,18},{3,1},{4,20},{5,7},{6,22},{7,5},{8,24},{9,11},... | collective-permute-start | bytes 884744 | tf_op jit(solution)/shard_map/ppermute | solution.py:38
  151.2 7.9 %collective-permute-start.22 = (bf16[48,3072]{1,0:T(8,128)(2,1)S(1)}, bf16[48,3072]{1,0:T(8,128)(2,1)S(1)}, u32[]{:S(2)}, u32[]{:S(2)}) collective-permute-start(bf16[48,3072]{1,0:T(8,128)(2,1)S(1)} %pad_maximum_fusion.4), channel_id=1, source_target_pairs={{0,112},{1,15},{2,114},{3,5},{4,116},{5,3},{6,118},{7,9},{8,120},{... | collective-permute-start | bytes 884744 | tf_op jit(solution)/shard_map/ppermute | solution.py:42
  152.8 8.6 %collective-permute-start.34 = (bf16[48,4096]{1,0:T(8,128)(2,1)S(1)}, bf16[48,4096]{1,0:T(8,128)(2,1)S(1)}, u32[]{:S(2)}, u32[]{:S(2)}) collective-permute-start(bf16[48,4096]{1,0:T(8,128)(2,1)S(1)} %pad_maximum_fusion.3), channel_id=1, source_target_pairs={{0,16},{1,3},{2,18},{3,1},{4,20},{5,7},{6,22},{7,5},{8,24},{9,11},... | collective-permute-start | bytes 1179656 | tf_op jit(solution)/shard_map/ppermute | solution.py:38
  157.2 9.0 %collective-permute-start.30 = (bf16[48,4096]{1,0:T(8,128)(2,1)S(1)}, bf16[48,4096]{1,0:T(8,128)(2,1)S(1)}, u32[]{:S(2)}, u32[]{:S(2)}) collective-permute-start(bf16[48,4096]{1,0:T(8,128)(2,1)S(1)} %pad_maximum_fusion.2), channel_id=1, source_target_pairs={{0,112},{1,15},{2,114},{3,5},{4,116},{5,3},{6,118},{7,9},{8,120},{... | collective-permute-start | bytes 1179656 | tf_op jit(solution)/shard_map/ppermute | solution.py:42
  159.3 9.4 %collective-permute-start.23 = (bf16[48,3072]{1,0:T(8,128)(2,1)S(1)}, bf16[48,3072]{1,0:T(8,128)(2,1)S(1)}, u32[]{:S(2)}, u32[]{:S(2)}) collective-permute-start(bf16[48,3072]{1,0:T(8,128)(2,1)S(1)} %get-tuple-element.26), channel_id=1, source_target_pairs={{0,16},{1,3},{2,18},{3,1},{4,20},{5,7},{6,22},{7,5},{8,24},{9,11},... | collective-permute-start | bytes 884744 | tf_op jit(solution)/shard_map/ppermute | solution.py:38
  161.4 7.9 %collective-permute-start.27 = (bf16[48,3072]{1,0:T(8,128)(2,1)S(1)}, bf16[48,3072]{1,0:T(8,128)(2,1)S(1)}, u32[]{:S(2)}, u32[]{:S(2)}) collective-permute-start(bf16[48,3072]{1,0:T(8,128)(2,1)S(1)} %get-tuple-element.27), channel_id=1, source_target_pairs={{0,112},{1,15},{2,114},{3,5},{4,116},{5,3},{6,118},{7,9},{8,120},{... | collective-permute-start | bytes 884744 | tf_op jit(solution)/shard_map/ppermute | solution.py:42
  166.5 7.9 %collective-permute-start.31 = (bf16[48,4096]{1,0:T(8,128)(2,1)S(1)}, bf16[48,4096]{1,0:T(8,128)(2,1)S(1)}, u32[]{:S(2)}, u32[]{:S(2)}) collective-permute-start(bf16[48,4096]{1,0:T(8,128)(2,1)S(1)} %get-tuple-element.30), channel_id=1, source_target_pairs={{0,16},{1,3},{2,18},{3,1},{4,20},{5,7},{6,22},{7,5},{8,24},{9,11},... | collective-permute-start | bytes 1179656 | tf_op jit(solution)/shard_map/ppermute | solution.py:38
  166.6 9.3 %collective-permute-start.35 = (bf16[48,4096]{1,0:T(8,128)(2,1)S(1)}, bf16[48,4096]{1,0:T(8,128)(2,1)S(1)}, u32[]{:S(2)}, u32[]{:S(2)}) collective-permute-start(bf16[48,4096]{1,0:T(8,128)(2,1)S(1)} %get-tuple-element.31), channel_id=1, source_target_pairs={{0,112},{1,15},{2,114},{3,5},{4,116},{5,3},{6,118},{7,9},{8,120},{... | collective-permute-start | bytes 1179656 | tf_op jit(solution)/shard_map/ppermute | solution.py:42
  169.6 9.6 %collective-permute-start.24 = (bf16[48,3072]{1,0:T(8,128)(2,1)S(1)}, bf16[48,3072]{1,0:T(8,128)(2,1)S(1)}, u32[]{:S(2)}, u32[]{:S(2)}) collective-permute-start(bf16[48,3072]{1,0:T(8,128)(2,1)S(1)} %get-tuple-element.24), channel_id=1, source_target_pairs={{0,112},{1,15},{2,114},{3,5},{4,116},{5,3},{6,118},{7,9},{8,120},{... | collective-permute-start | bytes 884744 | tf_op jit(solution)/shard_map/ppermute | solution.py:42
  171.4 7.7 %collective-permute-start.28 = (bf16[48,3072]{1,0:T(8,128)(2,1)S(1)}, bf16[48,3072]{1,0:T(8,128)(2,1)S(1)}, u32[]{:S(2)}, u32[]{:S(2)}) collective-permute-start(bf16[48,3072]{1,0:T(8,128)(2,1)S(1)} %get-tuple-element.25), channel_id=1, source_target_pairs={{0,16},{1,3},{2,18},{3,1},{4,20},{5,7},{6,22},{7,5},{8,24},{9,11},... | collective-permute-start | bytes 884744 | tf_op jit(solution)/shard_map/ppermute | solution.py:38
  176.2 9.1 %collective-permute-start.32 = (bf16[48,4096]{1,0:T(8,128)(2,1)S(1)}, bf16[48,4096]{1,0:T(8,128)(2,1)S(1)}, u32[]{:S(2)}, u32[]{:S(2)}) collective-permute-start(bf16[48,4096]{1,0:T(8,128)(2,1)S(1)} %get-tuple-element.28), channel_id=1, source_target_pairs={{0,112},{1,15},{2,114},{3,5},{4,116},{5,3},{6,118},{7,9},{8,120},{... | collective-permute-start | bytes 1179656 | tf_op jit(solution)/shard_map/ppermute | solution.py:42
  178.1 9.3 %collective-permute-start.36 = (bf16[48,4096]{1,0:T(8,128)(2,1)S(1)}, bf16[48,4096]{1,0:T(8,128)(2,1)S(1)}, u32[]{:S(2)}, u32[]{:S(2)}) collective-permute-start(bf16[48,4096]{1,0:T(8,128)(2,1)S(1)} %get-tuple-element.29), channel_id=1, source_target_pairs={{0,16},{1,3},{2,18},{3,1},{4,20},{5,7},{6,22},{7,5},{8,24},{9,11},... | collective-permute-start | bytes 1179656 | tf_op jit(solution)/shard_map/ppermute | solution.py:38
  188.4 27.4 %copy-start.20 = (bf16[4,7168]{1,0:T(4,128)(2,1)S(1)}, bf16[4,7168]{1,0:T(4,128)(2,1)}, u32[]{:S(2)}) copy-start(bf16[4,7168]{1,0:T(4,128)(2,1)} %b_ref.1) | copy-start | bytes 172036
  188.4 28.1 %copy-start.22 = (bf16[2,7168]{1,0:T(2,128)(2,1)S(1)}, bf16[2,7168]{1,0:T(2,128)(2,1)}, u32[]{:S(2)}) copy-start(bf16[2,7168]{1,0:T(2,128)(2,1)} %a_ref.1) | copy-start | bytes 86020
where the time goes:
time: 218 us; the launch traced here: 217 us
  waiting for transfers between devices  79.7 us (37%)
  blocking collectives  65.4 us (30%)
  Pallas kernels  32 us (15%)
  starting transfers between devices  20.7 us (9%)
  local copies, waits for them, and re-layouts  14.3 us (7%)
  other arithmetic  4.02 us (2%)
    all_to_all x2, blocking collectives, exchange(): lax.all_to_all(blocks, EXP, split_axis=0, concat_axis=0, tiled=True, axis...  65.4 us
    ppermute x12, waiting for transfers between devices, over_odd(): return lax.ppermute(array, EXP, pairs_along(2, odd_partner))  40.6 us
    ppermute x12, waiting for transfers between devices, over_even(): return lax.ppermute(array, EXP, pairs_along(2, even_partner))  33.4 us
    pallas_call x4, Pallas kernels, layers(): pl.pallas_call(body, in_specs=[hbm_spec] * n_blocks + [vmem_spec] * 7, ou...  31.4 us
    ppermute x12, starting transfers between devices, over_odd(): return lax.ppermute(array, EXP, pairs_along(2, odd_partner))  15.8 us
    unnamed x54, local copies, waits for them, and re-layouts  12.8 us
    ppermute x13, waiting for transfers between devices, swap_cores(): return lax.ppermute(array, EXP, [(i, i ^ 1) for i in range(devices)])  5.79 us
  transfers between devices with their start and end apart: 37, of which 23 were waited for; matrix products, arithmetic and copies ran while one was open for 1% of the time, Pallas kernels for 10%

commit v1 on v0

--- a/solution.py
+++ b/solution.py
@@ -51,7 +51,7 @@
     return values * lax.rsqrt(jnp.mean(values * values, axis=-1, keepdims=True) + 1e-06) * gain_vec
 
 
-GROUPS = ((0,), (1, -1), (2, -2), (3, -3, 4))
+GROUPS = ((0, 1, -1), (2, -2), (3, -3), (4,))
 
 
 def stage_1_groups():
@@ -71,7 +71,9 @@
     for k in (1, 2, 3):
         slots[k] = over_even(slots[1 - k])
         slots[-k] = over_odd(slots[k - 1])
-    slots[4] = (over_even(slots[-3][:, :cut]), over_odd(slots[3][:, cut:]))
+    low = over_even(slots[-3][:, :cut])
+    high = over_odd(slots[3][:, cut:])
+    slots[4] = (low, high)
     return slots
 
 
@@ -97,13 +99,13 @@
             one, two = low[i].astype(jnp.bfloat16), high[i].astype(jnp.bfloat16)
             one = over_even(one) if k == 1 else over_odd(one)
             two = over_odd(two) if k == 1 else over_even(two)
-            low[i], high[i] = one.astype(jnp.float32), two.astype(jnp.float32)
+            low[i], high[i] = one, two
         if k:
             side = 1 if k == 2 else -1
             for i in range(count):
-                low[i] = part(side * k, i) + low[i]
-                high[i] = part(-side * k, i) + high[i]
-    return jnp.concatenate([part(0, i) + low[i] + high[i] for i in range(count)], 1)
+                low[i] = part(side * k, i) + low[i].astype(jnp.float32)
+                high[i] = part(-side * k, i) + high[i].astype(jnp.float32)
+    return low, high
 
 
 def layers(own, other, a_count, weights, pick, cut):
@@ -125,7 +127,7 @@
     n_blocks = len(parts)
     inputs = [p[0] for p in parts] + list(weights) + [pick]
     n_in = len(inputs)
-    chunk = 1024
+    chunk = 1792
 
     def body(*refs):
         ins = refs[:n_in]
@@ -223,8 +225,17 @@
     rows = a_rows + b_tokens.shape[0]
     lanes = 128
     full = width + lanes
-
-    def body(a_ref, ag_ref, b_ref, bg_ref, id_ref, w_ref, out_ref, hold):
+    inputs = (a_tokens, a_gain[None], b_tokens, b_gain[None], expert_ids, route_weights)
+
+    def body(*refs):
+        out_ref, hold, value = refs[6:9]
+        held, sems = refs[9:15], refs[15]
+        copies = [pltpu.make_async_copy(refs[i], held[i], sems.at[i]) for i in range(6)]
+        for c in copies:
+            c.start()
+        for c in copies:
+            c.wait()
+        a_ref, ag_ref, b_ref, bg_ref, id_ref, w_ref = held
         hold[:a_rows, :width] = normed(a_ref[...].astype(jnp.float32), ag_ref[...])
         hold[:a_rows, width:] = jnp.zeros((a_rows, lanes), jnp.float32)
         hold[a_rows:rows, :width] = normed(b_ref[...].astype(jnp.float32), bg_ref[...])
@@ -238,21 +249,24 @@
         third = weight - first - second
         part = jnp.where(lane < EXPERTS, first, jnp.where(lane < 2 * EXPERTS, second, third))
         hold[a_rows:rows, width:] = jnp.where(lane < 3 * EXPERTS, part, 0.0)
-        value = hold[:rows, :].astype(jnp.bfloat16)
-        for i in range(RING):
-            out_ref[i] = value
-
-    vmem_spec = pl.BlockSpec(memory_space=pltpu.VMEM)
-    return pl.pallas_call(
-        body,
-        in_specs=[vmem_spec] * 6,
-        out_specs=vmem_spec,
+        value[...] = hold[:rows, :].astype(jnp.bfloat16)
+        copies = [pltpu.make_async_copy(value, out_ref.at[i], sems.at[6 + i]) for i in range(RING)]
+        for c in copies:
+            c.start()
+        for c in copies:
+            c.wait()
+
+    return pl.pallas_call(
+        body,
+        in_specs=[pl.BlockSpec(memory_space=pl.ANY)] * 6,
+        out_specs=pl.BlockSpec(memory_space=pl.ANY),
         out_shape=jax.ShapeDtypeStruct((RING, rows, full), jnp.bfloat16),
-        scratch_shapes=[pltpu.VMEM((8, full), jnp.float32)],
-        cost_estimate=pl.CostEstimate(flops=20_000_000_000, bytes_accessed=1_000_000, transcendentals=0),
-        compiler_params=pltpu.CompilerParams(vmem_limit_bytes=4 * 1024 * 1024),
+        scratch_shapes=[pltpu.VMEM((8, full), jnp.float32), pltpu.VMEM((rows, full), jnp.bfloat16)]
+        + [pltpu.VMEM(x.shape, x.dtype) for x in inputs]
+        + [pltpu.SemaphoreType.DMA((6 + RING,))],
+        compiler_params=pltpu.CompilerParams(vmem_limit_bytes=60 * 1024 * 1024),
         name="prepare",
-    )(a_tokens, a_gain[None], b_tokens, b_gain[None], expert_ids, route_weights)
+    )(*inputs)
 
 
 def pack(near, a_rows):
@@ -276,6 +290,83 @@
         compiler_params=pltpu.CompilerParams(vmem_limit_bytes=6 * 1024 * 1024),
         name="pack",
     )(near)
+
+
+def touch(weights, pick):
+    def body(*refs):
+        refs[-1][...] = refs[-2][...]
+
+    vmem_spec = pl.BlockSpec(memory_space=pltpu.VMEM)
+    return pl.pallas_call(
+        body,
+        in_specs=[vmem_spec] * 7,
+        out_specs=vmem_spec,
+        out_shape=jax.ShapeDtypeStruct(pick.shape, pick.dtype),
+        compiler_params=pltpu.CompilerParams(vmem_limit_bytes=1024 * 1024),
+        name="touch",
+    )(*weights, pick)
+
+
+def unpack(own, other, low, high, streams, a_rows):
+    total, width = own.shape
+    rows = total // RING
+    b_rows = rows - a_rows
+    count = len(streams) - 1
+
+    def body(*refs):
+        own_ref, other_ref = refs[:2]
+        lows, highs = refs[2 : 2 + count], refs[2 + count : 2 + 2 * count]
+        out_ref, hold, one = refs[2 + 2 * count :]
+        for i in range(count):
+            at = slice(streams[i], streams[i + 1])
+            hold[:, at] = (
+                own_ref[:, at].astype(jnp.float32)
+                + other_ref[:, at].astype(jnp.float32)
+                + lows[i][...].astype(jnp.float32)
+                + highs[i][...].astype(jnp.float32)
+            )
+        for j in range(RING):
+            one[:a_rows] = hold[pl.ds(j * a_rows, a_rows), :]
+            one[a_rows:rows] = hold[pl.ds(RING * a_rows + j * b_rows, b_rows), :]
+            out_ref[j] = one[:rows].astype(jnp.bfloat16)
+
+    vmem_spec = pl.BlockSpec(memory_space=pltpu.VMEM)
+    return pl.pallas_call(
+        body,
+        in_specs=[vmem_spec] * (2 + 2 * count),
+        out_specs=vmem_spec,
+        out_shape=jax.ShapeDtypeStruct((RING, rows, width), jnp.bfloat16),
+        scratch_shapes=[pltpu.VMEM((total, width), jnp.float32), pltpu.VMEM((8, width), jnp.float32)],
+        compiler_params=pltpu.CompilerParams(vmem_limit_bytes=6 * 1024 * 1024),
+        name="unpack",
+    )(own, other, *low, *high)
+
+
+def finish(pieces, a_tokens, b_tokens):
+    a_rows, width = a_tokens.shape
+    rows = pieces.shape[1]
+
+    def body(piece_ref, a_ref, b_ref, a_out, b_out, hold):
+        value = piece_ref[0].astype(jnp.float32)
+        for j in range(1, RING):
+            value = value + piece_ref[j].astype(jnp.float32)
+        hold[:rows] = value
+        a_out[...] = (a_ref[...].astype(jnp.float32) + hold[:a_rows]).astype(jnp.bfloat16)
+        b_out[...] = (b_ref[...].astype(jnp.float32) + hold[a_rows:rows]).astype(jnp.bfloat16)
+
+    vmem_spec = pl.BlockSpec(memory_space=pltpu.VMEM)
+    return pl.pallas_call(
+        body,
+        in_specs=[vmem_spec] * 3,
+        out_specs=[vmem_spec] * 2,
+        out_shape=[
+            jax.ShapeDtypeStruct(a_tokens.shape, jnp.bfloat16),
+            jax.ShapeDtypeStruct(b_tokens.shape, jnp.bfloat16),
+        ],
+        scratch_shapes=[pltpu.VMEM((8, width), jnp.float32)],
+        compiler_params=pltpu.CompilerParams(vmem_limit_bytes=2 * 1024 * 1024),
+        name="finish",
+    )(pieces, a_tokens, b_tokens)
 
 
 def shards(
@@ -296,9 +387,6 @@
     group_size = devices // EXPERTS
     width = b_tokens.shape[1]
     a_rows = a_tokens.shape[0]
-    b_rows = b_tokens.shape[0]
-    a_float = a_tokens.astype(jnp.float32)
-    b_float = b_tokens.astype(jnp.float32)
     ready = prepare(a_tokens, a_gain, b_tokens, b_gain, expert_ids, route_weights)
     full = ready.shape[2]
     block = pack(exchange(ready), a_rows)
@@ -319,6 +407,7 @@
         expert_up[0],
         expert_down[0],
     )
+    pick = touch(weights, pick)
     own, other = {}, {}
     rows = block.shape[0]
     for group in GROUPS:
@@ -334,20 +423,10 @@
         for i, k in enumerate(group):
             own[k] = mine[i * rows : (i + 1) * rows]
             other[k] = theirs[i * rows : (i + 1) * rows]
-    streams = (0, width * 3 // 7, width)
-    total = scatter_ring(own, other, streams)
-    both_sum = jnp.concatenate(
-        [
-            total[: RING * a_rows].reshape(RING, a_rows, width),
-            total[RING * a_rows :].reshape(RING, b_rows, width),
-        ],
-        1,
-    )
-    back = exchange(both_sum.astype(jnp.bfloat16)).astype(jnp.float32)
-    total = jnp.sum(back, axis=0)
-    a_out = (a_float + total[:a_rows]).astype(jnp.bfloat16)
-    b_out = (b_float + total[a_rows:]).astype(jnp.bfloat16)
-    return (a_out, b_out)
+    streams = (0, width * 4 // 7, width)
+    low, high = scatter_ring(own, other, streams)
+    pieces = unpack(own[0], other[0], low, high, streams, a_rows)
+    return tuple(finish(exchange(pieces), a_tokens, b_tokens))
 
 
 def solution(mesh):

time: 218 us -> 202 us (0.927)
  the two profiles are of different devices: /device:TPU:528 before, /device:TPU:516 now
where the time goes in v1:
time: 202 us; the launch traced here: 199 us
  starting transfers between devices  54.1 us (27%)
  blocking collectives  52.3 us (26%)
  waiting for transfers between devices  46.5 us (23%)
  Pallas kernels  30.3 us (15%)
  local copies, waits for them, and re-layouts  13.5 us (7%)
    all_to_all x2, blocking collectives, exchange(): lax.all_to_all(blocks, EXP, split_axis=0, concat_axis=0, tiled=True, axis...  52.3 us
    ppermute x12, starting transfers between devices, over_odd(): return lax.ppermute(array, EXP, pairs_along(2, odd_partner))  44.8 us
    pallas_call x4, Pallas kernels, layers(): pl.pallas_call(body, in_specs=[hbm_spec] * n_blocks + [vmem_spec] * 7, ou...  25.9 us
    ppermute x12, waiting for transfers between devices, over_odd(): return lax.ppermute(array, EXP, pairs_along(2, odd_partner))  23.8 us
    ppermute x12, waiting for transfers between devices, over_even(): return lax.ppermute(array, EXP, pairs_along(2, even_partner))  21.9 us
    unnamed x42, local copies, waits for them, and re-layouts  13.2 us
    ppermute x12, starting transfers between devices, over_even(): return lax.ppermute(array, EXP, pairs_along(2, even_partner))  5.8 us
  transfers between devices with their start and end apart: 37, of which 13 were waited for; matrix products, arithmetic and copies ran while one was open for 1% of the time, Pallas kernels for 13%

profile of v1, /device:TPU:516, one launch (start us, length us, event | category | flops | bytes accessed | tf_op | source)
XLA Modules:
  0.0 199.4 jit_solution(18361173711212853565)
XLA Ops:
  0.6 2.2 %prepare.1 = bf16[8,6,7296]{2,1,0:T(8,128)(2,1)} custom-call(bf16[2,7168]{1,0:T(2,128)(2,1)} %a_ref.1, f32[1,7168]{1,0:T(1,128)} %bitcast.32, bf16[4,7168]{1,0:T(4,128)(2,1)} %b_ref.1, f32[1,7168]{1,0:T(1,128)} %bitcast.33, s32[4,8]{1,0:T(4,128)} %refs_4_.1, f32[4,8]{1,0:T(4,128)} %refs_5_.1), custom_call_target="tpu_custom_call" | custom-call | tf_op jit(solution)/shard_map/prepare/pallas_call | solution.py:259
  2.9 30.8 %all_to_all.10.near_ref = bf16[8,6,7296]{2,1,0:T(8,128)(2,1)S(1)} all-to-all(bf16[8,6,7296]{2,1,0:T(8,128)(2,1)} %prepare.1), channel_id=1, replica_groups={{0,2,4,6,8,10,12,14},{16,18,20,22,24,26,28,30},{32,34,36,38,40,42,44,46..., dimensions={0} | all-to-all | bytes 1400832 | tf_op jit(solution)/shard_map/all_to_all | solution.py:64
  33.7 0.3 pack.1.refs_0_
  34.0 1.7 collective-permute-start
  35.8 10.0 %collective-permute-start.1 = (bf16[48,7296]{1,0:T(8,128)(2,1)S(1)}, bf16[48,7296]{1,0:T(8,128)(2,1)S(1)}, u32[]{:S(2)}, u32[]{:S(2)}) collective-permute-start(bf16[48,7296]{1,0:T(8,128)(2,1)S(1)} %pack.1.refs_0_), channel_id=1, source_target_pairs={{0,112},{1,15},{2,114},{3,5},{4,116},{5,3},{6,118},{7,9},{8,120},{... | collective-permute-start | bytes 2101256 | tf_op jit(solution)/shard_map/ppermute | solution.py:42
  45.7 9.2 %collective-permute-start.7 = (bf16[48,7296]{1,0:T(8,128)(2,1)}, bf16[48,7296]{1,0:T(8,128)(2,1)}, u32[]{:S(2)}, u32[]{:S(2)}) collective-permute-start(bf16[48,7296]{1,0:T(8,128)(2,1)} %collective-permute-done.refs_1_), channel_id=1, source_target_pairs={{0,112},{1,15},{2,114},{3,5},{4,116},{5,3},{6,118},{7,9},{8,120},{... | collective-permute-start | bytes 2101256 | tf_op jit(solution)/shard_map/ppermute | solution.py:42
  54.9 9.3 %collective-permute-done.7.refs_1_ = bf16[48,7296]{1,0:T(8,128)(2,1)} collective-permute-done((bf16[48,7296]{1,0:T(8,128)(2,1)}, bf16[48,7296]{1,0:T(8,128)(2,1)}, u32[]{:S(2)}, u32[]{:S(2)}) %collective-permute-start.7) | collective-permute-done | bytes 700448 | tf_op jit(solution)/shard_map/ppermute | solution.py:42
  64.3 1.8 collective-permute-done.6.refs_0_
  66.1 3.4 %collective-permute-start.12 = (bf16[48,7296]{1,0:T(8,128)(2,1)}, bf16[48,7296]{1,0:T(8,128)(2,1)S(1)}, u32[]{:S(2)}, u32[]{:S(2)}) collective-permute-start(bf16[48,7296]{1,0:T(8,128)(2,1)} %collective-permute-done.6.refs_0_), channel_id=1, source_target_pairs={{0,112},{1,15},{2,114},{3,5},{4,116},{5,3},{6,118},{7,9},{8,120},{... | collective-permute-start | bytes 2101256 | tf_op jit(solution)/shard_map/ppermute | solution.py:42
  69.5 0.5 collective-permute-start.4
  70.0 5.5 %collective-permute-done.11.refs_0_ = bf16[48,7296]{1,0:T(8,128)(2,1)S(1)} collective-permute-done((bf16[48,7296]{1,0:T(8,128)(2,1)}, bf16[48,7296]{1,0:T(8,128)(2,1)S(1)}, u32[]{:S(2)}, u32[]{:S(2)}) %collective-permute-start.11) | collective-permute-done | bytes 700448 | tf_op jit(solution)/shard_map/ppermute | solution.py:38
  75.6 3.3 %collective-permute-start.17 = (bf16[48,3712]{1,0:T(8,128)(2,1)S(1)}, bf16[48,3712]{1,0:T(8,128)(2,1)}, u32[]{:S(2)}, u32[]{:S(2)}) collective-permute-start(bf16[48,3712]{1,0:T(8,128)(2,1)S(1)} %slice.230), channel_id=1, source_target_pairs={{0,112},{1,15},{2,114},{3,5},{4,116},{5,3},{6,118},{7,9},{8,120},{... | collective-permute-start | bytes 1069064 | tf_op jit(solution)/shard_map/ppermute | solution.py:42
  79.3 5.1 %collective-permute-done.17.refs_1_ = bf16[48,3712]{1,0:T(8,128)(2,1)} collective-permute-done((bf16[48,3712]{1,0:T(8,128)(2,1)S(1)}, bf16[48,3712]{1,0:T(8,128)(2,1)}, u32[]{:S(2)}, u32[]{:S(2)}) %collective-permute-start.17) | collective-permute-done | bytes 356384 | tf_op jit(solution)/shard_map/ppermute | solution.py:42
  84.4 2.0 %collective-permute-done.16.refs_0_ = bf16[48,3584]{1,0:T(8,128)(2,1)} collective-permute-done((bf16[48,3584]{1,0:T(8,128)(2,1)S(1)}, bf16[48,3584]{1,0:T(8,128)(2,1)}, u32[]{:S(2)}, u32[]{:S(2)}) %collective-permute-start.16) | collective-permute-done | bytes 344096 | tf_op jit(solution)/shard_map/ppermute | solution.py:38
  86.5 0.9 copy-done.15
  87.3 0.5 collective-permute-start.8
  87.8 0.9 copy-done.17
  88.7 0.5 collective-permute-start.14
  89.3 1.6 copy-done.1
  90.9 1.6 copy-done.3
  92.5 1.5 copy-done.5
  94.0 1.5 copy-done.7
  95.5 1.5 copy-done.9
  97.0 1.5 copy-done.2
  98.6 0.6 copy-done.4
  99.2 0.5 copy-done.6
  99.7 0.5 copy-done.8
  100.3 0.5 copy-done.10
  100.8 5.7 %shard_map.134 = (bf16[48,7168]{1,0:T(8,128)(2,1)S(1)}, bf16[48,7168]{1,0:T(8,128)(2,1)S(1)}) custom-call(bf16[48,3584]{1,0:T(8,128)(2,1)} %collective-permute-done.16.refs_0_, bf16[48,3712]{1,0:T(8,128)(2,1)} %collective-permute-done.17.refs_1_, bf16[48,3584]{1,0:T(8,128)(2,1)} %collective-permute-done.18.refs_2_, ...), custom_call_target="tpu_custom_call" | custom-call | flops 550502400 | bytes 14450688 | tf_op jit(solution)/shard_map/pallas_call | solution.py:207
  106.6 0.7 collective-permute-start.20
  107.2 7.5 %shard_map.131 = (bf16[144,7168]{1,0:T(8,128)(2,1)S(1)}, bf16[144,7168]{1,0:T(8,128)(2,1)S(1)}) custom-call(bf16[48,7296]{1,0:T(8,128)(2,1)S(1)} %pack.1.refs_0_, bf16[48,7296]{1,0:T(8,128)(2,1)} %collective-permute-done.refs_1_, bf16[48,7296]{1,0:T(8,128)(2,1)S(1)} %copy-done.14, bf16[48,7296]{1,0:T(8,128)(2,1)S(1)} %copy-done.16, ...), custom_call_target="tpu_custom_call" | custom-call | flops 1651507200 | bytes 19955712 | tf_op jit(solution)/shard_map/pallas_call | solution.py:207
  114.7 0.2 collective-permute-start.5
  115.0 6.2 %shard_map.132 = (bf16[96,7168]{1,0:T(8,128)(2,1)S(1)}, bf16[96,7168]{1,0:T(8,128)(2,1)S(1)}) custom-call(bf16[48,7296]{1,0:T(8,128)(2,1)} %collective-permute-done.6.refs_0_, bf16[48,7296]{1,0:T(8,128)(2,1)} %collective-permute-done.7.refs_1_, bf16[48,7296]{1,0:T(8,128)(2,1)} %collective-permute-done.8.refs_2_, ...), custom_call_target="tpu_custom_call" | custom-call | flops 1101004800 | bytes 17203200 | tf_op jit(solution)/shard_map/pallas_call | solution.py:207
  121.2 0.5 collective-permute-start.10
  121.7 6.5 %shard_map.133 = (bf16[96,7168]{1,0:T(8,128)(2,1)S(1)}, bf16[96,7168]{1,0:T(8,128)(2,1)S(1)}) custom-call(bf16[48,7296]{1,0:T(8,128)(2,1)S(1)} %collective-permute-done.11.refs_0_, bf16[48,7296]{1,0:T(8,128)(2,1)S(1)} %copy-done.12, bf16[48,7296]{1,0:T(8,128)(2,1)S(1)} %collective-permute-done.13.refs_2_, ...), custom_call_target="tpu_custom_call" | custom-call | flops 1101004800 | bytes 17203200 | tf_op jit(solution)/shard_map/pallas_call | solution.py:207
  128.2 0.2 collective-permute-start.15
  128.6 2.0 collective-permute-start.33
  130.7 0.8 collective-permute-done.15
  131.5 2.7 %collective-permute-start.29 = (bf16[48,2048]{1,0:T(8,128)(2,1)S(1)}, bf16[48,2048]{1,0:T(8,128)(2,1)S(1)}, u32[]{:S(2)}, u32[]{:S(2)}) collective-permute-start(bf16[48,2048]{1,0:T(8,128)(2,1)S(1)} %get-tuple-element.30), channel_id=1, source_target_pairs={{0,112},{1,15},{2,114},{3,5},{4,116},{5,3},{6,118},{7,9},{8,120},{... | collective-permute-start | bytes 589832 | tf_op jit(solution)/shard_map/ppermute | solution.py:42
  134.2 0.2 convert_add_fusion
  134.5 1.1 collective-permute-done.25
  135.8 5.6 %collective-permute-done.21 = bf16[48,2048]{1,0:T(8,128)(2,1)S(1)} collective-permute-done((bf16[48,2048]{1,0:T(8,128)(2,1)S(1)}, bf16[48,2048]{1,0:T(8,128)(2,1)S(1)}, u32[]{:S(2)}, u32[]{:S(2)}) %collective-permute-start.21) | collective-permute-done | bytes 196640 | tf_op jit(solution)/shard_map/ppermute | solution.py:38
  141.4 1.4 collective-permute-start.26
  142.8 0.8 collective-permute-start.22
  143.7 1.3 collective-permute-start.30
  145.2 0.9 collective-permute-start.34
  146.1 6.2 %collective-permute-done.22 = bf16[48,4096]{1,0:T(8,128)(2,1)S(1)} collective-permute-done((bf16[48,4096]{1,0:T(8,128)(2,1)S(1)}, bf16[48,4096]{1,0:T(8,128)(2,1)S(1)}, u32[]{:S(2)}, u32[]{:S(2)}) %collective-permute-start.22) | collective-permute-done | bytes 393248 | tf_op jit(solution)/shard_map/ppermute | solution.py:42
  152.3 0.3 add_convert_fusion.1
  152.6 2.1 %collective-permute-start.31 = (bf16[48,4096]{1,0:T(8,128)(2,1)S(1)}, bf16[48,4096]{1,0:T(8,128)(2,1)S(1)}, u32[]{:S(2)}, u32[]{:S(2)}) collective-permute-start(bf16[48,4096]{1,0:T(8,128)(2,1)S(1)} %get-tuple-element.26), channel_id=1, source_target_pairs={{0,112},{1,15},{2,114},{3,5},{4,116},{5,3},{6,118},{7,9},{8,120},{... | collective-permute-start | bytes 1179656 | tf_op jit(solution)/shard_map/ppermute | solution.py:42
  154.6 0.7 collective-permute-start.23
  155.3 0.2 add_convert_fusion.6
  155.6 3.7 %collective-permute-start.35 = (bf16[48,3072]{1,0:T(8,128)(2,1)S(1)}, bf16[48,3072]{1,0:T(8,128)(2,1)S(1)}, u32[]{:S(2)}, u32[]{:S(2)}) collective-permute-start(bf16[48,3072]{1,0:T(8,128)(2,1)S(1)} %get-tuple-element.22), channel_id=1, source_target_pairs={{0,112},{1,15},{2,114},{3,5},{4,116},{5,3},{6,118},{7,9},{8,120},{... | collective-permute-start | bytes 884744 | tf_op jit(solution)/shard_map/ppermute | solution.py:42
  159.3 1.2 collective-permute-done.31
  160.5 1.9 collective-permute-done.23
  162.4 0.3 add_convert_fusion
  162.7 0.8 collective-permute-start.32
  163.5 3.6 %collective-permute-start.24 = (bf16[48,4096]{1,0:T(8,128)(2,1)S(1)}, bf16[48,4096]{1,0:T(8,128)(2,1)S(1)}, u32[]{:S(2)}, u32[]{:S(2)}) collective-permute-start(bf16[48,4096]{1,0:T(8,128)(2,1)S(1)} %get-tuple-element.21), channel_id=1, source_target_pairs={{0,112},{1,15},{2,114},{3,5},{4,116},{5,3},{6,118},{7,9},{8,120},{... | collective-permute-start | bytes 1179656 | tf_op jit(solution)/shard_map/ppermute | solution.py:42
  167.1 0.2 add_convert_fusion.5
  167.5 2.7 %collective-permute-start.28 = (bf16[48,3072]{1,0:T(8,128)(2,1)S(1)}, bf16[48,3072]{1,0:T(8,128)(2,1)S(1)}, u32[]{:S(2)}, u32[]{:S(2)}) collective-permute-start(bf16[48,3072]{1,0:T(8,128)(2,1)S(1)} %get-tuple-element.19), channel_id=1, source_target_pairs={{0,112},{1,15},{2,114},{3,5},{4,116},{5,3},{6,118},{7,9},{8,120},{... | collective-permute-start | bytes 884744 | tf_op jit(solution)/shard_map/ppermute | solution.py:42
  170.3 3.9 %collective-permute-done.36.refs_5_ = bf16[48,3072]{1,0:T(8,128)(2,1)S(1)} collective-permute-done((bf16[48,3072]{1,0:T(8,128)(2,1)S(1)}, bf16[48,3072]{1,0:T(8,128)(2,1)S(1)}, u32[]{:S(2)}, u32[]{:S(2)}) %collective-permute-start.36) | collective-permute-done | bytes 294944 | tf_op jit(solution)/shard_map/ppermute | solution.py:38
  174.2 1.8 collective-permute-done.28.refs_3_
  176.0 1.0 unpack.1
  177.1 21.5 %all_to_all.11.piece_ref = bf16[8,6,7168]{2,1,0:T(8,128)(2,1)S(1)} all-to-all(bf16[8,6,7168]{2,1,0:T(8,128)(2,1)S(1)} %unpack.1), channel_id=1, replica_groups={{0,2,4,6,8,10,12,14},{16,18,20,22,24,26,28,30},{32,34,36,38,40,42,44,46..., dimensions={0} | all-to-all | bytes 1376256 | tf_op jit(solution)/shard_map/all_to_all | solution.py:64
  198.5 0.9 finish.1
  (90 shorter events, 1.5 us)
Async XLA Ops:
  33.7 55.6 %copy-start = (bf16[7168,144]{0,1:T(8,128)(2,1)S(1)}, bf16[7168,144]{0,1:T(8,128)(2,1)}, u32[]{:S(2)}) copy-start(bf16[7168,144]{0,1:T(8,128)(2,1)} %param.14) | copy-start | bytes 6193156
  34.0 11.7 %collective-permute-start = (bf16[48,7296]{1,0:T(8,128)(2,1)S(1)}, bf16[48,7296]{1,0:T(8,128)(2,1)}, u32[]{:S(2)}, u32[]{:S(2)}) collective-permute-start(bf16[48,7296]{1,0:T(8,128)(2,1)S(1)} %pack.1.refs_0_), channel_id=1, source_target_pairs={{0,16},{1,3},{2,18},{3,1},{4,20},{5,7},{6,22},{7,5},{8,24},{9,11},... | collective-permute-start | bytes 2101256 | tf_op jit(solution)/shard_map/ppermute | solution.py:38
  35.8 19.1 %collective-permute-start.1 = (bf16[48,7296]{1,0:T(8,128)(2,1)S(1)}, bf16[48,7296]{1,0:T(8,128)(2,1)S(1)}, u32[]{:S(2)}, u32[]{:S(2)}) collective-permute-start(bf16[48,7296]{1,0:T(8,128)(2,1)S(1)} %pack.1.refs_0_), channel_id=1, source_target_pairs={{0,112},{1,15},{2,114},{3,5},{4,116},{5,3},{6,118},{7,9},{8,120},{... | collective-permute-start | bytes 2101256 | tf_op jit(solution)/shard_map/ppermute | solution.py:42
  45.7 18.5 %collective-permute-start.7 = (bf16[48,7296]{1,0:T(8,128)(2,1)}, bf16[48,7296]{1,0:T(8,128)(2,1)}, u32[]{:S(2)}, u32[]{:S(2)}) collective-permute-start(bf16[48,7296]{1,0:T(8,128)(2,1)} %collective-permute-done.refs_1_), channel_id=1, source_target_pairs={{0,112},{1,15},{2,114},{3,5},{4,116},{5,3},{6,118},{7,9},{8,120},{... | collective-permute-start | bytes 2101256 | tf_op jit(solution)/shard_map/ppermute | solution.py:42
  54.9 32.9 %copy-start.13 = (bf16[48,7296]{1,0:T(8,128)(2,1)}, bf16[48,7296]{1,0:T(8,128)(2,1)S(1)}, u32[]{:S(2)}) copy-start(bf16[48,7296]{1,0:T(8,128)(2,1)S(1)} %collective-permute-done.1.refs_2_) | copy-start | bytes 2101252
  54.9 11.2 %collective-permute-start.6 = (bf16[48,7296]{1,0:T(8,128)(2,1)S(1)}, bf16[48,7296]{1,0:T(8,128)(2,1)}, u32[]{:S(2)}, u32[]{:S(2)}) collective-permute-start(bf16[48,7296]{1,0:T(8,128)(2,1)S(1)} %collective-permute-done.1.refs_2_), channel_id=1, source_target_pairs={{0,16},{1,3},{2,18},{3,1},{4,20},{5,7},{6,22},{7,5},{8,24},{9,11},... | collective-permute-start | bytes 2101256 | tf_op jit(solution)/shard_map/ppermute | solution.py:38
  64.3 11.3 %collective-permute-start.11 = (bf16[48,7296]{1,0:T(8,128)(2,1)}, bf16[48,7296]{1,0:T(8,128)(2,1)S(1)}, u32[]{:S(2)}, u32[]{:S(2)}) collective-permute-start(bf16[48,7296]{1,0:T(8,128)(2,1)} %collective-permute-done.7.refs_1_), channel_id=1, source_target_pairs={{0,16},{1,3},{2,18},{3,1},{4,20},{5,7},{6,22},{7,5},{8,24},{9,11},... | collective-permute-start | bytes 2101256 | tf_op jit(solution)/shard_map/ppermute | solution.py:38
  66.1 12.8 %collective-permute-start.12 = (bf16[48,7296]{1,0:T(8,128)(2,1)}, bf16[48,7296]{1,0:T(8,128)(2,1)S(1)}, u32[]{:S(2)}, u32[]{:S(2)}) collective-permute-start(bf16[48,7296]{1,0:T(8,128)(2,1)} %collective-permute-done.6.refs_0_), channel_id=1, source_target_pairs={{0,112},{1,15},{2,114},{3,5},{4,116},{5,3},{6,118},{7,9},{8,120},{... | collective-permute-start | bytes 2101256 | tf_op jit(solution)/shard_map/ppermute | solution.py:42
  69.5 16.9 %collective-permute-start.2 = (bf16[48,7296]{1,0:T(8,128)(2,1)S(1)}, bf16[48,7296]{1,0:T(8,128)(2,1)S(1)}, u32[]{:S(2)}, u32[]{:S(2)}) collective-permute-start(bf16[48,7296]{1,0:T(8,128)(2,1)S(1)} %pack.1.refs_0_), channel_id=1, source_target_pairs={{0,1},{1,0},{2,3},{3,2},{4,5},{5,4},{6,7},{7,6},{8,9},{9,8},{10,11... | collective-permute-start | bytes 2101256 | tf_op jit(solution)/shard_map/ppermute | solution.py:47
  69.5 18.3 %collective-permute-start.4 = (bf16[48,7296]{1,0:T(8,128)(2,1)S(1)}, bf16[48,7296]{1,0:T(8,128)(2,1)S(1)}, u32[]{:S(2)}, u32[]{:S(2)}) collective-permute-start(bf16[48,7296]{1,0:T(8,128)(2,1)S(1)} %collective-permute-done.1.refs_2_), channel_id=1, source_target_pairs={{0,1},{1,0},{2,3},{3,2},{4,5},{5,4},{6,7},{7,6},{8,9},{9,8},{10,11... | collective-permute-start | bytes 2101256 | tf_op jit(solution)/shard_map/ppermute | solution.py:47
  75.6 8.8 %collective-permute-start.17 = (bf16[48,3712]{1,0:T(8,128)(2,1)S(1)}, bf16[48,3712]{1,0:T(8,128)(2,1)}, u32[]{:S(2)}, u32[]{:S(2)}) collective-permute-start(bf16[48,3712]{1,0:T(8,128)(2,1)S(1)} %slice.230), channel_id=1, source_target_pairs={{0,112},{1,15},{2,114},{3,5},{4,116},{5,3},{6,118},{7,9},{8,120},{... | collective-permute-start | bytes 1069064 | tf_op jit(solution)/shard_map/ppermute | solution.py:42
  78.9 7.5 %copy-start.11 = (bf16[48,7296]{1,0:T(8,128)(2,1)}, bf16[48,7296]{1,0:T(8,128)(2,1)S(1)}, u32[]{:S(2)}) copy-start(bf16[48,7296]{1,0:T(8,128)(2,1)S(1)} %collective-permute-done.12.refs_1_) | copy-start | bytes 2101252
  79.0 7.5 %collective-permute-start.16 = (bf16[48,3584]{1,0:T(8,128)(2,1)S(1)}, bf16[48,3584]{1,0:T(8,128)(2,1)}, u32[]{:S(2)}, u32[]{:S(2)}) collective-permute-start(bf16[48,3584]{1,0:T(8,128)(2,1)S(1)} %slice.229), channel_id=1, source_target_pairs={{0,16},{1,3},{2,18},{3,1},{4,20},{5,7},{6,22},{7,5},{8,24},{9,11},... | collective-permute-start | bytes 1032200 | tf_op jit(solution)/shard_map/ppermute | solution.py:38
  79.1 27.4 %collective-permute-start.3 = (bf16[48,7296]{1,0:T(8,128)(2,1)}, bf16[48,7296]{1,0:T(8,128)(2,1)}, u32[]{:S(2)}, u32[]{:S(2)}) collective-permute-start(bf16[48,7296]{1,0:T(8,128)(2,1)} %collective-permute-done.refs_1_), channel_id=1, source_target_pairs={{0,1},{1,0},{2,3},{3,2},{4,5},{5,4},{6,7},{7,6},{8,9},{9,8},{10,11... | collective-permute-start | bytes 2101256 | tf_op jit(solution)/shard_map/ppermute | solution.py:47
  84.4 4.8 %collective-permute-start.19 = (bf16[48,3712]{1,0:T(8,128)(2,1)}, bf16[48,3712]{1,0:T(8,128)(2,1)}, u32[]{:S(2)}, u32[]{:S(2)}) collective-permute-start(bf16[48,3712]{1,0:T(8,128)(2,1)} %collective-permute-done.17.refs_1_), channel_id=1, source_target_pairs={{0,1},{1,0},{2,3},{3,2},{4,5},{5,4},{6,7},{7,6},{8,9},{9,8},{10,11... | collective-permute-start | bytes 1069064 | tf_op jit(solution)/shard_map/ppermute | solution.py:47
  86.4 2.3 %collective-permute-start.18 = (bf16[48,3584]{1,0:T(8,128)(2,1)}, bf16[48,3584]{1,0:T(8,128)(2,1)}, u32[]{:S(2)}, u32[]{:S(2)}) collective-permute-start(bf16[48,3584]{1,0:T(8,128)(2,1)} %collective-permute-done.16.refs_0_), channel_id=1, source_target_pairs={{0,1},{1,0},{2,3},{3,2},{4,5},{5,4},{6,7},{7,6},{8,9},{9,8},{10,11... | collective-permute-start | bytes 1032200 | tf_op jit(solution)/shard_map/ppermute | solution.py:47
  86.4 0.9 copy-start.15
  87.3 27.4 %collective-permute-start.8 = (bf16[48,7296]{1,0:T(8,128)(2,1)}, bf16[48,7296]{1,0:T(8,128)(2,1)}, u32[]{:S(2)}, u32[]{:S(2)}) collective-permute-start(bf16[48,7296]{1,0:T(8,128)(2,1)} %collective-permute-done.6.refs_0_), channel_id=1, source_target_pairs={{0,1},{1,0},{2,3},{3,2},{4,5},{5,4},{6,7},{7,6},{8,9},{9,8},{10,11... | collective-permute-start | bytes 2101256 | tf_op jit(solution)/shard_map/ppermute | solution.py:47
  87.8 0.9 copy-start.17
  88.7 26.3 %collective-permute-start.9 = (bf16[48,7296]{1,0:T(8,128)(2,1)}, bf16[48,7296]{1,0:T(8,128)(2,1)}, u32[]{:S(2)}, u32[]{:S(2)}) collective-permute-start(bf16[48,7296]{1,0:T(8,128)(2,1)} %collective-permute-done.7.refs_1_), channel_id=1, source_target_pairs={{0,1},{1,0},{2,3},{3,2},{4,5},{5,4},{6,7},{7,6},{8,9},{9,8},{10,11... | collective-permute-start | bytes 2101256 | tf_op jit(solution)/shard_map/ppermute | solution.py:47
  88.7 33.0 %collective-permute-start.14 = (bf16[48,7296]{1,0:T(8,128)(2,1)}, bf16[48,7296]{1,0:T(8,128)(2,1)S(1)}, u32[]{:S(2)}, u32[]{:S(2)}) collective-permute-start(bf16[48,7296]{1,0:T(8,128)(2,1)} %copy-done.11), channel_id=1, source_target_pairs={{0,1},{1,0},{2,3},{3,2},{4,5},{5,4},{6,7},{7,6},{8,9},{9,8},{10,11... | collective-permute-start | bytes 2101256 | tf_op jit(solution)/shard_map/ppermute | solution.py:47
  89.2 32.5 %collective-permute-start.13 = (bf16[48,7296]{1,0:T(8,128)(2,1)S(1)}, bf16[48,7296]{1,0:T(8,128)(2,1)S(1)}, u32[]{:S(2)}, u32[]{:S(2)}) collective-permute-start(bf16[48,7296]{1,0:T(8,128)(2,1)S(1)} %collective-permute-done.11.refs_0_), channel_id=1, source_target_pairs={{0,1},{1,0},{2,3},{3,2},{4,5},{5,4},{6,7},{7,6},{8,9},{9,8},{10,11... | collective-permute-start | bytes 2101256 | tf_op jit(solution)/shard_map/ppermute | solution.py:47
  89.3 1.6 copy-start.1
  90.9 1.6 copy-start.3
  92.5 1.5 copy-start.5
  94.0 1.5 copy-start.7
  95.5 1.5 copy-start.9
  97.0 1.6 copy-start.2
  97.0 2.2 %copy-start.4 = (bf16[144,7168]{1,0:T(8,128)(2,1)S(1)}, bf16[144,7168]{1,0:T(8,128)(2,1)}, u32[]{:S(2)}) copy-start(bf16[144,7168]{1,0:T(8,128)(2,1)} %refs_6_.5) | copy-start | bytes 6193156
  97.0 2.7 %copy-start.6 = (bf16[1,7168,128]{2,1,0:T(8,128)(2,1)S(1)}, bf16[1,7168,128]{2,1,0:T(8,128)(2,1)}, u32[]{:S(2)}) copy-start(bf16[1,7168,128]{2,1,0:T(8,128)(2,1)} %param.21) | copy-start | bytes 5505028
  97.0 3.3 %copy-start.8 = (bf16[1,7168,128]{2,1,0:T(8,128)(2,1)S(1)}, bf16[1,7168,128]{2,1,0:T(8,128)(2,1)}, u32[]{:S(2)}) copy-start(bf16[1,7168,128]{2,1,0:T(8,128)(2,1)} %param.22) | copy-start | bytes 5505028
  97.0 3.8 %copy-start.10 = (bf16[1,128,7168]{2,1,0:T(8,128)(2,1)S(1)}, bf16[1,128,7168]{2,1,0:T(8,128)(2,1)}, u32[]{:S(2)}) copy-start(bf16[1,128,7168]{2,1,0:T(8,128)(2,1)} %param.23) | copy-start | bytes 5505028
  100.8 6.4 %copy-start.14 = (bf16[48,7296]{1,0:T(8,128)(2,1)S(1)}, bf16[48,7296]{1,0:T(8,128)(2,1)}, u32[]{:S(2)}) copy-start(bf16[48,7296]{1,0:T(8,128)(2,1)} %copy-done.13) | copy-start | bytes 2101252
  100.8 6.4 %copy-start.16 = (bf16[48,7296]{1,0:T(8,128)(2,1)S(1)}, bf16[48,7296]{1,0:T(8,128)(2,1)}, u32[]{:S(2)}) copy-start(bf16[48,7296]{1,0:T(8,128)(2,1)} %copy-done.15) | copy-start | bytes 2101252
  100.8 6.4 %copy-start.18 = (bf16[48,7296]{1,0:T(8,128)(2,1)S(1)}, bf16[48,7296]{1,0:T(8,128)(2,1)}, u32[]{:S(2)}) copy-start(bf16[48,7296]{1,0:T(8,128)(2,1)} %copy-done.17) | copy-start | bytes 2101252
  106.6 21.9 %collective-permute-start.20 = (bf16[48,7168]{1,0:T(8,128)(2,1)S(1)}, bf16[48,7168]{1,0:T(8,128)(2,1)S(1)}, u32[]{:S(2)}, u32[]{:S(2)}) collective-permute-start(bf16[48,7168]{1,0:T(8,128)(2,1)S(1)} %get-tuple-element.17), channel_id=1, source_target_pairs={{0,1},{1,0},{2,3},{3,2},{4,5},{5,4},{6,7},{7,6},{8,9},{9,8},{10,11... | collective-permute-start | bytes 2064392 | tf_op jit(solution)/shard_map/ppermute | solution.py:47
  114.7 7.0 %copy-start.12 = (bf16[48,7296]{1,0:T(8,128)(2,1)S(1)}, bf16[48,7296]{1,0:T(8,128)(2,1)}, u32[]{:S(2)}) copy-start(bf16[48,7296]{1,0:T(8,128)(2,1)} %copy-done.11) | copy-start | bytes 2101252
  114.7 44.5 %collective-permute-start.5 = (bf16[144,7168]{1,0:T(8,128)(2,1)S(1)}, bf16[144,7168]{1,0:T(8,128)(2,1)S(1)}, u32[]{:S(2)}, u32[]{:S(2)}) collective-permute-start(bf16[144,7168]{1,0:T(8,128)(2,1)S(1)} %get-tuple-element.11), channel_id=1, source_target_pairs={{0,1},{1,0},{2,3},{3,2},{4,5},{5,4},{6,7},{7,6},{8,9},{9,8},{10,11... | collective-permute-start | bytes 6193160 | tf_op jit(solution)/shard_map/ppermute | solution.py:47
  121.2 24.0 %collective-permute-start.10 = (bf16[96,7168]{1,0:T(8,128)(2,1)S(1)}, bf16[96,7168]{1,0:T(8,128)(2,1)S(1)}, u32[]{:S(2)}, u32[]{:S(2)}) collective-permute-start(bf16[96,7168]{1,0:T(8,128)(2,1)S(1)} %get-tuple-element.13), channel_id=1, source_target_pairs={{0,1},{1,0},{2,3},{3,2},{4,5},{5,4},{6,7},{7,6},{8,9},{9,8},{10,11... | collective-permute-start | bytes 4128776 | tf_op jit(solution)/shard_map/ppermute | solution.py:47
  128.2 3.3 %collective-permute-start.15 = (bf16[96,7168]{1,0:T(8,128)(2,1)S(1)}, bf16[96,7168]{1,0:T(8,128)(2,1)S(1)}, u32[]{:S(2)}, u32[]{:S(2)}) collective-permute-start(bf16[96,7168]{1,0:T(8,128)(2,1)S(1)} %get-tuple-element.15), channel_id=1, source_target_pairs={{0,1},{1,0},{2,3},{3,2},{4,5},{5,4},{6,7},{7,6},{8,9},{9,8},{10,11... | collective-permute-start | bytes 4128776 | tf_op jit(solution)/shard_map/ppermute | solution.py:47
  128.6 15.2 %collective-permute-start.33 = (bf16[48,1536]{1,0:T(8,128)(2,1)S(1)}, bf16[48,1536]{1,0:T(8,128)(2,1)S(1)}, u32[]{:S(2)}, u32[]{:S(2)}) collective-permute-start(bf16[48,1536]{1,0:T(8,128)(2,1)S(1)} %get-tuple-element.32), channel_id=1, source_target_pairs={{0,112},{1,15},{2,114},{3,5},{4,116},{5,3},{6,118},{7,9},{8,120},{... | collective-permute-start | bytes 442376 | tf_op jit(solution)/shard_map/ppermute | solution.py:42
  130.5 5.1 %collective-permute-start.25 = (bf16[48,1536]{1,0:T(8,128)(2,1)S(1)}, bf16[48,1536]{1,0:T(8,128)(2,1)S(1)}, u32[]{:S(2)}, u32[]{:S(2)}) collective-permute-start(bf16[48,1536]{1,0:T(8,128)(2,1)S(1)} %get-tuple-element.33), channel_id=1, source_target_pairs={{0,16},{1,3},{2,18},{3,1},{4,20},{5,7},{6,22},{7,5},{8,24},{9,11},... | collective-permute-start | bytes 442376 | tf_op jit(solution)/shard_map/ppermute | solution.py:38
  131.5 11.4 %collective-permute-start.29 = (bf16[48,2048]{1,0:T(8,128)(2,1)S(1)}, bf16[48,2048]{1,0:T(8,128)(2,1)S(1)}, u32[]{:S(2)}, u32[]{:S(2)}) collective-permute-start(bf16[48,2048]{1,0:T(8,128)(2,1)S(1)} %get-tuple-element.30), channel_id=1, source_target_pairs={{0,112},{1,15},{2,114},{3,5},{4,116},{5,3},{6,118},{7,9},{8,120},{... | collective-permute-start | bytes 589832 | tf_op jit(solution)/shard_map/ppermute | solution.py:42
  135.7 5.7 %collective-permute-start.21 = (bf16[48,2048]{1,0:T(8,128)(2,1)S(1)}, bf16[48,2048]{1,0:T(8,128)(2,1)S(1)}, u32[]{:S(2)}, u32[]{:S(2)}) collective-permute-start(bf16[48,2048]{1,0:T(8,128)(2,1)S(1)} %get-tuple-element.31), channel_id=1, source_target_pairs={{0,16},{1,3},{2,18},{3,1},{4,20},{5,7},{6,22},{7,5},{8,24},{9,11},... | collective-permute-start | bytes 589832 | tf_op jit(solution)/shard_map/ppermute | solution.py:38
  141.4 14.0 %collective-permute-start.26 = (bf16[48,3072]{1,0:T(8,128)(2,1)S(1)}, bf16[48,3072]{1,0:T(8,128)(2,1)S(1)}, u32[]{:S(2)}, u32[]{:S(2)}) collective-permute-start(bf16[48,3072]{1,0:T(8,128)(2,1)S(1)} %pad_maximum_fusion.2), channel_id=1, source_target_pairs={{0,112},{1,15},{2,114},{3,5},{4,116},{5,3},{6,118},{7,9},{8,120},{... | collective-permute-start | bytes 884744 | tf_op jit(solution)/shard_map/ppermute | solution.py:42
  142.8 9.5 %collective-permute-start.22 = (bf16[48,4096]{1,0:T(8,128)(2,1)S(1)}, bf16[48,4096]{1,0:T(8,128)(2,1)S(1)}, u32[]{:S(2)}, u32[]{:S(2)}) collective-permute-start(bf16[48,4096]{1,0:T(8,128)(2,1)S(1)} %pad_maximum_fusion), channel_id=1, source_target_pairs={{0,112},{1,15},{2,114},{3,5},{4,116},{5,3},{6,118},{7,9},{8,120},{... | collective-permute-start | bytes 1179656 | tf_op jit(solution)/shard_map/ppermute | solution.py:42
  143.7 8.6 %collective-permute-start.30 = (bf16[48,4096]{1,0:T(8,128)(2,1)S(1)}, bf16[48,4096]{1,0:T(8,128)(2,1)S(1)}, u32[]{:S(2)}, u32[]{:S(2)}) collective-permute-start(bf16[48,4096]{1,0:T(8,128)(2,1)S(1)} %pad_maximum_fusion.1), channel_id=1, source_target_pairs={{0,16},{1,3},{2,18},{3,1},{4,20},{5,7},{6,22},{7,5},{8,24},{9,11},... | collective-permute-start | bytes 1179656 | tf_op jit(solution)/shard_map/ppermute | solution.py:38
  145.2 10.2 %collective-permute-start.34 = (bf16[48,3072]{1,0:T(8,128)(2,1)S(1)}, bf16[48,3072]{1,0:T(8,128)(2,1)S(1)}, u32[]{:S(2)}, u32[]{:S(2)}) collective-permute-start(bf16[48,3072]{1,0:T(8,128)(2,1)S(1)} %pad_maximum_fusion.3), channel_id=1, source_target_pairs={{0,16},{1,3},{2,18},{3,1},{4,20},{5,7},{6,22},{7,5},{8,24},{9,11},... | collective-permute-start | bytes 884744 | tf_op jit(solution)/shard_map/ppermute | solution.py:38
  152.6 7.9 %collective-permute-start.31 = (bf16[48,4096]{1,0:T(8,128)(2,1)S(1)}, bf16[48,4096]{1,0:T(8,128)(2,1)S(1)}, u32[]{:S(2)}, u32[]{:S(2)}) collective-permute-start(bf16[48,4096]{1,0:T(8,128)(2,1)S(1)} %get-tuple-element.26), channel_id=1, source_target_pairs={{0,112},{1,15},{2,114},{3,5},{4,116},{5,3},{6,118},{7,9},{8,120},{... | collective-permute-start | bytes 1179656 | tf_op jit(solution)/shard_map/ppermute | solution.py:42
  154.6 7.8 %collective-permute-start.23 = (bf16[48,4096]{1,0:T(8,128)(2,1)S(1)}, bf16[48,4096]{1,0:T(8,128)(2,1)S(1)}, u32[]{:S(2)}, u32[]{:S(2)}) collective-permute-start(bf16[48,4096]{1,0:T(8,128)(2,1)S(1)} %get-tuple-element.27), channel_id=1, source_target_pairs={{0,16},{1,3},{2,18},{3,1},{4,20},{5,7},{6,22},{7,5},{8,24},{9,11},... | collective-permute-start | bytes 1179656 | tf_op jit(solution)/shard_map/ppermute | solution.py:38
  155.6 11.5 %collective-permute-start.35 = (bf16[48,3072]{1,0:T(8,128)(2,1)S(1)}, bf16[48,3072]{1,0:T(8,128)(2,1)S(1)}, u32[]{:S(2)}, u32[]{:S(2)}) collective-permute-start(bf16[48,3072]{1,0:T(8,128)(2,1)S(1)} %get-tuple-element.22), channel_id=1, source_target_pairs={{0,112},{1,15},{2,114},{3,5},{4,116},{5,3},{6,118},{7,9},{8,120},{... | collective-permute-start | bytes 884744 | tf_op jit(solution)/shard_map/ppermute | solution.py:42
  159.3 7.8 %collective-permute-start.27 = (bf16[48,3072]{1,0:T(8,128)(2,1)S(1)}, bf16[48,3072]{1,0:T(8,128)(2,1)S(1)}, u32[]{:S(2)}, u32[]{:S(2)}) collective-permute-start(bf16[48,3072]{1,0:T(8,128)(2,1)S(1)} %get-tuple-element.23), channel_id=1, source_target_pairs={{0,16},{1,3},{2,18},{3,1},{4,20},{5,7},{6,22},{7,5},{8,24},{9,11},... | collective-permute-start | bytes 884744 | tf_op jit(solution)/shard_map/ppermute | solution.py:38
  162.7 13.3 %collective-permute-start.32 = (bf16[48,4096]{1,0:T(8,128)(2,1)S(1)}, bf16[48,4096]{1,0:T(8,128)(2,1)S(1)}, u32[]{:S(2)}, u32[]{:S(2)}) collective-permute-start(bf16[48,4096]{1,0:T(8,128)(2,1)S(1)} %get-tuple-element.20), channel_id=1, source_target_pairs={{0,16},{1,3},{2,18},{3,1},{4,20},{5,7},{6,22},{7,5},{8,24},{9,11},... | collective-permute-start | bytes 1179656 | tf_op jit(solution)/shard_map/ppermute | solution.py:38
  163.5 12.5 %collective-permute-start.24 = (bf16[48,4096]{1,0:T(8,128)(2,1)S(1)}, bf16[48,4096]{1,0:T(8,128)(2,1)S(1)}, u32[]{:S(2)}, u32[]{:S(2)}) collective-permute-start(bf16[48,4096]{1,0:T(8,128)(2,1)S(1)} %get-tuple-element.21), channel_id=1, source_target_pairs={{0,112},{1,15},{2,114},{3,5},{4,116},{5,3},{6,118},{7,9},{8,120},{... | collective-permute-start | bytes 1179656 | tf_op jit(solution)/shard_map/ppermute | solution.py:42
  167.3 6.8 %collective-permute-start.36 = (bf16[48,3072]{1,0:T(8,128)(2,1)S(1)}, bf16[48,3072]{1,0:T(8,128)(2,1)S(1)}, u32[]{:S(2)}, u32[]{:S(2)}) collective-permute-start(bf16[48,3072]{1,0:T(8,128)(2,1)S(1)} %get-tuple-element.18), channel_id=1, source_target_pairs={{0,16},{1,3},{2,18},{3,1},{4,20},{5,7},{6,22},{7,5},{8,24},{9,11},... | collective-permute-start | bytes 884744 | tf_op jit(solution)/shard_map/ppermute | solution.py:38
  167.5 8.5 %collective-permute-start.28 = (bf16[48,3072]{1,0:T(8,128)(2,1)S(1)}, bf16[48,3072]{1,0:T(8,128)(2,1)S(1)}, u32[]{:S(2)}, u32[]{:S(2)}) collective-permute-start(bf16[48,3072]{1,0:T(8,128)(2,1)S(1)} %get-tuple-element.19), channel_id=1, source_target_pairs={{0,112},{1,15},{2,114},{3,5},{4,116},{5,3},{6,118},{7,9},{8,120},{... | collective-permute-start | bytes 884744 | tf_op jit(solution)/shard_map/ppermute | solution.py:42
  177.0 21.5 %copy-start.19 = (bf16[4,7168]{1,0:T(4,128)(2,1)S(1)}, bf16[4,7168]{1,0:T(4,128)(2,1)}, u32[]{:S(2)}) copy-start(bf16[4,7168]{1,0:T(4,128)(2,1)} %b_ref.1) | copy-start | bytes 172036
  177.1 21.5 %copy-start.20 = (bf16[2,7168]{1,0:T(2,128)(2,1)S(1)}, bf16[2,7168]{1,0:T(2,128)(2,1)}, u32[]{:S(2)}) copy-start(bf16[2,7168]{1,0:T(2,128)(2,1)} %a_ref.1) | copy-start | bytes 86020

commit v2 on v1

--- a/solution.py
+++ b/solution.py
@@ -220,16 +220,29 @@
     )(*inputs)
 
 
+def fine_size(a_rows, b_rows, a_width, b_width):
+    return -(-(a_rows * a_width + b_rows * b_width) // (128 * 16)) * 16
+
+
+def fine_parts(a_rows, b_rows, a_width, b_width):
+    a_tiles = a_width // 128
+    parts = [(t * a_rows, 0, a_rows, t) for t in range(a_tiles)]
+    return parts + [
+        (a_tiles * a_rows + t * b_rows, a_rows, b_rows, t) for t in range(b_width // 128)
+    ]
+
+
 def prepare(a_tokens, a_gain, b_tokens, b_gain, expert_ids, route_weights):
     a_rows, width = a_tokens.shape
     rows = a_rows + b_tokens.shape[0]
     lanes = 128
     full = width + lanes
+    fine_rows = fine_size(a_rows, rows - a_rows, width, full)
     inputs = (a_tokens, a_gain[None], b_tokens, b_gain[None], expert_ids, route_weights)
 
     def body(*refs):
-        out_ref, hold, value = refs[6:9]
-        held, sems = refs[9:15], refs[15]
+        out_ref, hold, fine, value = refs[6:10]
+        held, sems = refs[10:16], refs[16]
         copies = [pltpu.make_async_copy(refs[i], held[i], sems.at[i]) for i in range(6)]
         for c in copies:
             c.start()
@@ -237,7 +250,6 @@
             c.wait()
         a_ref, ag_ref, b_ref, bg_ref, id_ref, w_ref = held
         hold[:a_rows, :width] = normed(a_ref[...].astype(jnp.float32), ag_ref[...])
-        hold[:a_rows, width:] = jnp.zeros((a_rows, lanes), jnp.float32)
         hold[a_rows:rows, :width] = normed(b_ref[...].astype(jnp.float32), bg_ref[...])
         lane = lax.broadcasted_iota(jnp.int32, (rows - a_rows, lanes), 1)
         expert = lane & (EXPERTS - 1)
@@ -249,7 +261,10 @@
         third = weight - first - second
         part = jnp.where(lane < EXPERTS, first, jnp.where(lane < 2 * EXPERTS, second, third))
         hold[a_rows:rows, width:] = jnp.where(lane < 3 * EXPERTS, part, 0.0)
-        value[...] = hold[:rows, :].astype(jnp.bfloat16)
+        fine[pl.ds(fine_rows - 16, 16), :] = jnp.zeros((16, lanes), jnp.float32)
+        for to, lo, n, t in fine_parts(a_rows, rows - a_rows, width, full):
+            fine[pl.ds(to, n), :] = hold[pl.ds(lo, n), pl.ds(t * lanes, lanes)]
+        value[...] = fine[...].astype(jnp.bfloat16)
         copies = [pltpu.make_async_copy(value, out_ref.at[i], sems.at[6 + i]) for i in range(RING)]
         for c in copies:
             c.start()
@@ -260,8 +275,9 @@
         body,
         in_specs=[pl.BlockSpec(memory_space=pl.ANY)] * 6,
         out_specs=pl.BlockSpec(memory_space=pl.ANY),
-        out_shape=jax.ShapeDtypeStruct((RING, rows, full), jnp.bfloat16),
-        scratch_shapes=[pltpu.VMEM((8, full), jnp.float32), pltpu.VMEM((rows, full), jnp.bfloat16)]
+        out_shape=jax.ShapeDtypeStruct((RING, fine_rows, lanes), jnp.bfloat16),
+        scratch_shapes=[pltpu.VMEM((8, full), jnp.float32), pltpu.VMEM((fine_rows, lanes), jnp.float32)]
+        + [pltpu.VMEM((fine_rows, lanes), jnp.bfloat16)]
         + [pltpu.VMEM(x.shape, x.dtype) for x in inputs]
         + [pltpu.SemaphoreType.DMA((6 + RING,))],
         compiler_params=pltpu.CompilerParams(vmem_limit_bytes=60 * 1024 * 1024),
@@ -269,15 +285,20 @@
     )(*inputs)
 
 
-def pack(near, a_rows):
-    places, rows, full = near.shape
-    b_rows = rows - a_rows
-
-    def body(near_ref, out_ref, hold):
+def pack(near, a_rows, b_rows, width):
+    places, fine_rows, lanes = near.shape
+    full = width + lanes
+    rows = a_rows + b_rows
+
+    def body(near_ref, out_ref, fine, hold):
+        hold[pl.ds(0, places * a_rows), pl.ds(width, lanes)] = jnp.zeros(
+            (places * a_rows, lanes), jnp.float32
+        )
         for i in range(places):
-            value = near_ref[i].astype(jnp.float32)
-            hold[pl.ds(i * a_rows, a_rows), :] = value[:a_rows]
-            hold[pl.ds(places * a_rows + i * b_rows, b_rows), :] = value[a_rows:]
+            fine[...] = near_ref[i].astype(jnp.float32)
+            for at, lo, n, t in fine_parts(a_rows, b_rows, width, full):
+                to = i * a_rows if lo == 0 else places * a_rows + i * b_rows
+                hold[pl.ds(to, n), pl.ds(t * lanes, lanes)] = fine[pl.ds(at, n), :]
         out_ref[...] = hold[...].astype(jnp.bfloat16)
 
     vmem_spec = pl.BlockSpec(memory_space=pltpu.VMEM)
@@ -286,7 +307,10 @@
         in_specs=[vmem_spec],
         out_specs=vmem_spec,
         out_shape=jax.ShapeDtypeStruct((places * rows, full), jnp.bfloat16),
-        scratch_shapes=[pltpu.VMEM((places * rows, full), jnp.float32)],
+        scratch_shapes=[
+            pltpu.VMEM((fine_rows, lanes), jnp.float32),
+            pltpu.VMEM((places * rows, full), jnp.float32),
+        ],
         compiler_params=pltpu.CompilerParams(vmem_limit_bytes=6 * 1024 * 1024),
         name="pack",
     )(near)
@@ -312,6 +336,8 @@
     rows = total // RING
     b_rows = rows - a_rows
     count = len(streams) - 1
+    lanes = 128
+    fine_rows = fine_size(a_rows, b_rows, width, width)
 
     def body(*refs):
         own_ref, other_ref = refs[:2]
@@ -326,17 +352,18 @@
                 + highs[i][...].astype(jnp.float32)
             )
         for j in range(RING):
-            one[:a_rows] = hold[pl.ds(j * a_rows, a_rows), :]
-            one[a_rows:rows] = hold[pl.ds(RING * a_rows + j * b_rows, b_rows), :]
-            out_ref[j] = one[:rows].astype(jnp.bfloat16)
+            for to, lo, n, t in fine_parts(a_rows, b_rows, width, width):
+                at = j * a_rows if lo == 0 else RING * a_rows + j * b_rows
+                one[pl.ds(to, n), :] = hold[pl.ds(at, n), pl.ds(t * lanes, lanes)]
+            out_ref[j] = one[...].astype(jnp.bfloat16)
 
     vmem_spec = pl.BlockSpec(memory_space=pltpu.VMEM)
     return pl.pallas_call(
         body,
         in_specs=[vmem_spec] * (2 + 2 * count),
         out_specs=vmem_spec,
-        out_shape=jax.ShapeDtypeStruct((RING, rows, width), jnp.bfloat16),
-        scratch_shapes=[pltpu.VMEM((total, width), jnp.float32), pltpu.VMEM((8, width), jnp.float32)],
+        out_shape=jax.ShapeDtypeStruct((RING, fine_rows, lanes), jnp.bfloat16),
+        scratch_shapes=[pltpu.VMEM((total, width), jnp.float32), pltpu.VMEM((fine_rows, lanes), jnp.float32)],
         compiler_params=pltpu.CompilerParams(vmem_limit_bytes=6 * 1024 * 1024),
         name="unpack",
     )(own, other, *low, *high)
@@ -344,13 +371,17 @@
 
 def finish(pieces, a_tokens, b_tokens):
     a_rows, width = a_tokens.shape
-    rows = pieces.shape[1]
-
-    def body(piece_ref, a_ref, b_ref, a_out, b_out, hold):
+    b_rows = b_tokens.shape[0]
+    rows = a_rows + b_rows
+    fine_rows, lanes = pieces.shape[1:]
+
+    def body(piece_ref, a_ref, b_ref, a_out, b_out, fine, hold):
         value = piece_ref[0].astype(jnp.float32)
         for j in range(1, RING):
             value = value + piece_ref[j].astype(jnp.float32)
-        hold[:rows] = value
+        fine[...] = value
+        for at, lo, n, t in fine_parts(a_rows, b_rows, width, width):
+            hold[pl.ds(lo, n), pl.ds(t * lanes, lanes)] = fine[pl.ds(at, n), :]
         a_out[...] = (a_ref[...].astype(jnp.float32) + hold[:a_rows]).astype(jnp.bfloat16)
         b_out[...] = (b_ref[...].astype(jnp.float32) + hold[a_rows:rows]).astype(jnp.bfloat16)
 
@@ -363,7 +394,7 @@
             jax.ShapeDtypeStruct(a_tokens.shape, jnp.bfloat16),
             jax.ShapeDtypeStruct(b_tokens.shape, jnp.bfloat16),
         ],
-        scratch_shapes=[pltpu.VMEM((8, width), jnp.float32)],
+        scratch_shapes=[pltpu.VMEM((fine_rows, lanes), jnp.float32), pltpu.VMEM((8, width), jnp.float32)],
         compiler_params=pltpu.CompilerParams(vmem_limit_bytes=2 * 1024 * 1024),
         name="finish",
     )(pieces, a_tokens, b_tokens)
@@ -388,8 +419,8 @@
     width = b_tokens.shape[1]
     a_rows = a_tokens.shape[0]
     ready = prepare(a_tokens, a_gain, b_tokens, b_gain, expert_ids, route_weights)
-    full = ready.shape[2]
-    block = pack(exchange(ready), a_rows)
+    full = width + ready.shape[2]
+    block = pack(exchange(ready), a_rows, b_tokens.shape[0], width)
     cut = width // 2
     slots = gather_ring(block, cut)
     swapped = {

time: 202 us -> 197 us (0.975)
  blocking collectives: 52.3 us -> 48 us
    all_to_all x2, blocking collectives: 52.3 us -> 48 us  [exchange(): lax.all_to_all(blocks, EXP, split_axis=0, concat_axis=0, tiled=True, axis...]
where the time goes in v2:
time: 197 us; the launch traced here: 195 us
  starting transfers between devices  53.9 us (27%)
  blocking collectives  48 us (24%)
  waiting for transfers between devices  46.3 us (24%)
  Pallas kernels  30.2 us (15%)
  local copies, waits for them, and re-layouts  13.5 us (7%)
    all_to_all x2, blocking collectives, exchange(): lax.all_to_all(blocks, EXP, split_axis=0, concat_axis=0, tiled=True, axis...  48 us
    ppermute x12, starting transfers between devices, over_odd(): return lax.ppermute(array, EXP, pairs_along(2, odd_partner))  44.4 us
    pallas_call x4, Pallas kernels, layers(): pl.pallas_call(body, in_specs=[hbm_spec] * n_blocks + [vmem_spec] * 7, ou...  25.8 us
    ppermute x12, waiting for transfers between devices, over_odd(): return lax.ppermute(array, EXP, pairs_along(2, odd_partner))  23.7 us
    ppermute x12, waiting for transfers between devices, over_even(): return lax.ppermute(array, EXP, pairs_along(2, even_partner))  21.9 us
    unnamed x42, local copies, waits for them, and re-layouts  13.2 us
    ppermute x12, starting transfers between devices, over_even(): return lax.ppermute(array, EXP, pairs_along(2, even_partner))  6.01 us
  transfers between devices with their start and end apart: 37, of which 13 were waited for; matrix products, arithmetic and copies ran while one was open for 1% of the time, Pallas kernels for 13%

profile of v2, /device:TPU:516, one launch (start us, length us, event | category | flops | bytes accessed | tf_op | source)
XLA Modules:
  0.0 194.6 jit_solution(11289343537678489110)
XLA Ops:
  0.6 2.1 %prepare.1 = bf16[8,352,128]{2,1,0:T(8,128)(2,1)} custom-call(bf16[2,7168]{1,0:T(2,128)(2,1)} %a_ref.1, f32[1,7168]{1,0:T(1,128)} %bitcast.32, bf16[4,7168]{1,0:T(4,128)(2,1)} %b_ref.1, f32[1,7168]{1,0:T(1,128)} %bitcast.33, s32[4,8]{1,0:T(4,128)} %refs_4_.1, f32[4,8]{1,0:T(4,128)} %refs_5_.1), custom_call_target="tpu_custom_call" | custom-call | tf_op jit(solution)/shard_map/prepare/pallas_call | solution.py:274
  2.8 28.6 %all_to_all.10.near_ref = bf16[8,352,128]{2,1,0:T(8,128)(2,1)S(1)} all-to-all(bf16[8,352,128]{2,1,0:T(8,128)(2,1)} %prepare.1), channel_id=1, replica_groups={{0,2,4,6,8,10,12,14},{16,18,20,22,24,26,28,30},{32,34,36,38,40,42,44,46..., dimensions={0} | all-to-all | bytes 1441792 | tf_op jit(solution)/shard_map/all_to_all | solution.py:64
  31.3 0.5 pack.1.refs_0_
  31.8 1.7 collective-permute-start
  33.6 9.7 %collective-permute-start.1 = (bf16[48,7296]{1,0:T(8,128)(2,1)S(1)}, bf16[48,7296]{1,0:T(8,128)(2,1)S(1)}, u32[]{:S(2)}, u32[]{:S(2)}) collective-permute-start(bf16[48,7296]{1,0:T(8,128)(2,1)S(1)} %pack.1.refs_0_), channel_id=1, source_target_pairs={{0,112},{1,15},{2,114},{3,5},{4,116},{5,3},{6,118},{7,9},{8,120},{... | collective-permute-start | bytes 2101256 | tf_op jit(solution)/shard_map/ppermute | solution.py:42
  43.3 9.2 %collective-permute-start.7 = (bf16[48,7296]{1,0:T(8,128)(2,1)}, bf16[48,7296]{1,0:T(8,128)(2,1)}, u32[]{:S(2)}, u32[]{:S(2)}) collective-permute-start(bf16[48,7296]{1,0:T(8,128)(2,1)} %collective-permute-done.refs_1_), channel_id=1, source_target_pairs={{0,112},{1,15},{2,114},{3,5},{4,116},{5,3},{6,118},{7,9},{8,120},{... | collective-permute-start | bytes 2101256 | tf_op jit(solution)/shard_map/ppermute | solution.py:42
  52.5 9.3 %collective-permute-done.7.refs_1_ = bf16[48,7296]{1,0:T(8,128)(2,1)} collective-permute-done((bf16[48,7296]{1,0:T(8,128)(2,1)}, bf16[48,7296]{1,0:T(8,128)(2,1)}, u32[]{:S(2)}, u32[]{:S(2)}) %collective-permute-start.7) | collective-permute-done | bytes 700448 | tf_op jit(solution)/shard_map/ppermute | solution.py:42
  61.8 1.8 collective-permute-done.6.refs_0_
  63.6 3.4 %collective-permute-start.12 = (bf16[48,7296]{1,0:T(8,128)(2,1)}, bf16[48,7296]{1,0:T(8,128)(2,1)S(1)}, u32[]{:S(2)}, u32[]{:S(2)}) collective-permute-start(bf16[48,7296]{1,0:T(8,128)(2,1)} %collective-permute-done.6.refs_0_), channel_id=1, source_target_pairs={{0,112},{1,15},{2,114},{3,5},{4,116},{5,3},{6,118},{7,9},{8,120},{... | collective-permute-start | bytes 2101256 | tf_op jit(solution)/shard_map/ppermute | solution.py:42
  67.1 0.5 collective-permute-start.4
  67.6 5.5 %collective-permute-done.11.refs_0_ = bf16[48,7296]{1,0:T(8,128)(2,1)S(1)} collective-permute-done((bf16[48,7296]{1,0:T(8,128)(2,1)}, bf16[48,7296]{1,0:T(8,128)(2,1)S(1)}, u32[]{:S(2)}, u32[]{:S(2)}) %collective-permute-start.11) | collective-permute-done | bytes 700448 | tf_op jit(solution)/shard_map/ppermute | solution.py:38
  73.1 3.3 %collective-permute-start.17 = (bf16[48,3712]{1,0:T(8,128)(2,1)S(1)}, bf16[48,3712]{1,0:T(8,128)(2,1)}, u32[]{:S(2)}, u32[]{:S(2)}) collective-permute-start(bf16[48,3712]{1,0:T(8,128)(2,1)S(1)} %slice.230), channel_id=1, source_target_pairs={{0,112},{1,15},{2,114},{3,5},{4,116},{5,3},{6,118},{7,9},{8,120},{... | collective-permute-start | bytes 1069064 | tf_op jit(solution)/shard_map/ppermute | solution.py:42
  76.8 5.1 %collective-permute-done.17.refs_1_ = bf16[48,3712]{1,0:T(8,128)(2,1)} collective-permute-done((bf16[48,3712]{1,0:T(8,128)(2,1)S(1)}, bf16[48,3712]{1,0:T(8,128)(2,1)}, u32[]{:S(2)}, u32[]{:S(2)}) %collective-permute-start.17) | collective-permute-done | bytes 356384 | tf_op jit(solution)/shard_map/ppermute | solution.py:42
  82.0 2.0 %collective-permute-done.16.refs_0_ = bf16[48,3584]{1,0:T(8,128)(2,1)} collective-permute-done((bf16[48,3584]{1,0:T(8,128)(2,1)S(1)}, bf16[48,3584]{1,0:T(8,128)(2,1)}, u32[]{:S(2)}, u32[]{:S(2)}) %collective-permute-start.16) | collective-permute-done | bytes 344096 | tf_op jit(solution)/shard_map/ppermute | solution.py:38
  84.0 0.9 copy-done.15
  84.9 0.5 collective-permute-start.8
  85.4 0.9 copy-done.17
  86.3 0.5 collective-permute-start.14
  86.8 0.3 collective-permute-start.13
  87.1 1.6 copy-done.1
  88.7 1.6 copy-done.3
  90.2 1.5 copy-done.5
  91.7 1.5 copy-done.7
  93.2 1.5 copy-done.9
  94.8 1.5 copy-done.2
  96.3 0.6 copy-done.4
  96.9 0.5 copy-done.6
  97.5 0.5 copy-done.8
  98.0 0.5 copy-done.10
  98.5 5.7 %shard_map.134 = (bf16[48,7168]{1,0:T(8,128)(2,1)S(1)}, bf16[48,7168]{1,0:T(8,128)(2,1)S(1)}) custom-call(bf16[48,3584]{1,0:T(8,128)(2,1)} %collective-permute-done.16.refs_0_, bf16[48,3712]{1,0:T(8,128)(2,1)} %collective-permute-done.17.refs_1_, bf16[48,3584]{1,0:T(8,128)(2,1)} %collective-permute-done.18.refs_2_, ...), custom_call_target="tpu_custom_call" | custom-call | flops 550502400 | bytes 14450688 | tf_op jit(solution)/shard_map/pallas_call | solution.py:207
  104.3 0.3 collective-permute-start.20
  104.6 7.4 %shard_map.131 = (bf16[144,7168]{1,0:T(8,128)(2,1)S(1)}, bf16[144,7168]{1,0:T(8,128)(2,1)S(1)}) custom-call(bf16[48,7296]{1,0:T(8,128)(2,1)S(1)} %pack.1.refs_0_, bf16[48,7296]{1,0:T(8,128)(2,1)} %collective-permute-done.refs_1_, bf16[48,7296]{1,0:T(8,128)(2,1)S(1)} %copy-done.14, bf16[48,7296]{1,0:T(8,128)(2,1)S(1)} %copy-done.16, ...), custom_call_target="tpu_custom_call" | custom-call | flops 1651507200 | bytes 19955712 | tf_op jit(solution)/shard_map/pallas_call | solution.py:207
  112.1 0.4 collective-permute-start.5
  112.5 6.2 %shard_map.132 = (bf16[96,7168]{1,0:T(8,128)(2,1)S(1)}, bf16[96,7168]{1,0:T(8,128)(2,1)S(1)}) custom-call(bf16[48,7296]{1,0:T(8,128)(2,1)} %collective-permute-done.6.refs_0_, bf16[48,7296]{1,0:T(8,128)(2,1)} %collective-permute-done.7.refs_1_, bf16[48,7296]{1,0:T(8,128)(2,1)} %collective-permute-done.8.refs_2_, ...), custom_call_target="tpu_custom_call" | custom-call | flops 1101004800 | bytes 17203200 | tf_op jit(solution)/shard_map/pallas_call | solution.py:207
  118.7 0.3 collective-permute-start.10
  119.1 6.5 %shard_map.133 = (bf16[96,7168]{1,0:T(8,128)(2,1)S(1)}, bf16[96,7168]{1,0:T(8,128)(2,1)S(1)}) custom-call(bf16[48,7296]{1,0:T(8,128)(2,1)S(1)} %collective-permute-done.11.refs_0_, bf16[48,7296]{1,0:T(8,128)(2,1)S(1)} %copy-done.12, bf16[48,7296]{1,0:T(8,128)(2,1)S(1)} %collective-permute-done.13.refs_2_, ...), custom_call_target="tpu_custom_call" | custom-call | flops 1101004800 | bytes 17203200 | tf_op jit(solution)/shard_map/pallas_call | solution.py:207
  125.6 0.4 collective-permute-start.15
  126.1 2.0 %collective-permute-start.33 = (bf16[48,1536]{1,0:T(8,128)(2,1)S(1)}, bf16[48,1536]{1,0:T(8,128)(2,1)S(1)}, u32[]{:S(2)}, u32[]{:S(2)}) collective-permute-start(bf16[48,1536]{1,0:T(8,128)(2,1)S(1)} %get-tuple-element.32), channel_id=1, source_target_pairs={{0,112},{1,15},{2,114},{3,5},{4,116},{5,3},{6,118},{7,9},{8,120},{... | collective-permute-start | bytes 442376 | tf_op jit(solution)/shard_map/ppermute | solution.py:42
  128.2 0.6 collective-permute-done.15
  128.8 2.9 %collective-permute-start.29 = (bf16[48,2048]{1,0:T(8,128)(2,1)S(1)}, bf16[48,2048]{1,0:T(8,128)(2,1)S(1)}, u32[]{:S(2)}, u32[]{:S(2)}) collective-permute-start(bf16[48,2048]{1,0:T(8,128)(2,1)S(1)} %get-tuple-element.30), channel_id=1, source_target_pairs={{0,112},{1,15},{2,114},{3,5},{4,116},{5,3},{6,118},{7,9},{8,120},{... | collective-permute-start | bytes 589832 | tf_op jit(solution)/shard_map/ppermute | solution.py:42
  132.1 1.1 collective-permute-done.25
  133.3 5.6 %collective-permute-done.21 = bf16[48,2048]{1,0:T(8,128)(2,1)S(1)} collective-permute-done((bf16[48,2048]{1,0:T(8,128)(2,1)S(1)}, bf16[48,2048]{1,0:T(8,128)(2,1)S(1)}, u32[]{:S(2)}, u32[]{:S(2)}) %collective-permute-start.21) | collective-permute-done | bytes 196640 | tf_op jit(solution)/shard_map/ppermute | solution.py:38
  138.9 1.4 collective-permute-start.26
  140.4 0.8 collective-permute-start.22
  141.3 1.3 collective-permute-start.30
  142.7 1.2 collective-permute-start.34
  143.9 6.0 %collective-permute-done.22 = bf16[48,4096]{1,0:T(8,128)(2,1)S(1)} collective-permute-done((bf16[48,4096]{1,0:T(8,128)(2,1)S(1)}, bf16[48,4096]{1,0:T(8,128)(2,1)S(1)}, u32[]{:S(2)}, u32[]{:S(2)}) %collective-permute-start.22) | collective-permute-done | bytes 393248 | tf_op jit(solution)/shard_map/ppermute | solution.py:42
  149.8 0.3 add_convert_fusion.1
  150.1 2.1 %collective-permute-start.31 = (bf16[48,4096]{1,0:T(8,128)(2,1)S(1)}, bf16[48,4096]{1,0:T(8,128)(2,1)S(1)}, u32[]{:S(2)}, u32[]{:S(2)}) collective-permute-start(bf16[48,4096]{1,0:T(8,128)(2,1)S(1)} %get-tuple-element.26), channel_id=1, source_target_pairs={{0,112},{1,15},{2,114},{3,5},{4,116},{5,3},{6,118},{7,9},{8,120},{... | collective-permute-start | bytes 1179656 | tf_op jit(solution)/shard_map/ppermute | solution.py:42
  152.2 0.7 collective-permute-start.23
  152.9 0.2 add_convert_fusion.6
  153.1 3.5 %collective-permute-start.35 = (bf16[48,3072]{1,0:T(8,128)(2,1)S(1)}, bf16[48,3072]{1,0:T(8,128)(2,1)S(1)}, u32[]{:S(2)}, u32[]{:S(2)}) collective-permute-start(bf16[48,3072]{1,0:T(8,128)(2,1)S(1)} %get-tuple-element.22), channel_id=1, source_target_pairs={{0,112},{1,15},{2,114},{3,5},{4,116},{5,3},{6,118},{7,9},{8,120},{... | collective-permute-start | bytes 884744 | tf_op jit(solution)/shard_map/ppermute | solution.py:42
  156.6 1.4 collective-permute-done.31
  158.0 1.9 collective-permute-done.23
  160.0 0.3 add_convert_fusion
  160.3 0.8 collective-permute-start.32
  161.1 3.4 %collective-permute-start.24 = (bf16[48,4096]{1,0:T(8,128)(2,1)S(1)}, bf16[48,4096]{1,0:T(8,128)(2,1)S(1)}, u32[]{:S(2)}, u32[]{:S(2)}) collective-permute-start(bf16[48,4096]{1,0:T(8,128)(2,1)S(1)} %get-tuple-element.21), channel_id=1, source_target_pairs={{0,112},{1,15},{2,114},{3,5},{4,116},{5,3},{6,118},{7,9},{8,120},{... | collective-permute-start | bytes 1179656 | tf_op jit(solution)/shard_map/ppermute | solution.py:42
  164.5 0.2 add_convert_fusion.5
  164.8 2.7 %collective-permute-start.28 = (bf16[48,3072]{1,0:T(8,128)(2,1)S(1)}, bf16[48,3072]{1,0:T(8,128)(2,1)S(1)}, u32[]{:S(2)}, u32[]{:S(2)}) collective-permute-start(bf16[48,3072]{1,0:T(8,128)(2,1)S(1)} %get-tuple-element.19), channel_id=1, source_target_pairs={{0,112},{1,15},{2,114},{3,5},{4,116},{5,3},{6,118},{7,9},{8,120},{... | collective-permute-start | bytes 884744 | tf_op jit(solution)/shard_map/ppermute | solution.py:42
  167.6 3.9 %collective-permute-done.36.refs_5_ = bf16[48,3072]{1,0:T(8,128)(2,1)S(1)} collective-permute-done((bf16[48,3072]{1,0:T(8,128)(2,1)S(1)}, bf16[48,3072]{1,0:T(8,128)(2,1)S(1)}, u32[]{:S(2)}, u32[]{:S(2)}) %collective-permute-start.36) | collective-permute-done | bytes 294944 | tf_op jit(solution)/shard_map/ppermute | solution.py:38
  171.5 1.8 collective-permute-done.28.refs_3_
  173.4 0.9 unpack.1
  174.3 19.4 %all_to_all.11.piece_ref = bf16[8,336,128]{2,1,0:T(8,128)(2,1)S(1)} all-to-all(bf16[8,336,128]{2,1,0:T(8,128)(2,1)S(1)} %unpack.1), channel_id=1, replica_groups={{0,2,4,6,8,10,12,14},{16,18,20,22,24,26,28,30},{32,34,36,38,40,42,44,46..., dimensions={0} | all-to-all | bytes 1376256 | tf_op jit(solution)/shard_map/all_to_all | solution.py:64
  193.7 0.9 finish.1
  (90 shorter events, 1.6 us)
Async XLA Ops:
  31.3 55.7 %copy-start = (bf16[7168,144]{0,1:T(8,128)(2,1)S(1)}, bf16[7168,144]{0,1:T(8,128)(2,1)}, u32[]{:S(2)}) copy-start(bf16[7168,144]{0,1:T(8,128)(2,1)} %param.14) | copy-start | bytes 6193156
  31.8 11.5 %collective-permute-start = (bf16[48,7296]{1,0:T(8,128)(2,1)S(1)}, bf16[48,7296]{1,0:T(8,128)(2,1)}, u32[]{:S(2)}, u32[]{:S(2)}) collective-permute-start(bf16[48,7296]{1,0:T(8,128)(2,1)S(1)} %pack.1.refs_0_), channel_id=1, source_target_pairs={{0,16},{1,3},{2,18},{3,1},{4,20},{5,7},{6,22},{7,5},{8,24},{9,11},... | collective-permute-start | bytes 2101256 | tf_op jit(solution)/shard_map/ppermute | solution.py:38
  33.6 18.9 %collective-permute-start.1 = (bf16[48,7296]{1,0:T(8,128)(2,1)S(1)}, bf16[48,7296]{1,0:T(8,128)(2,1)S(1)}, u32[]{:S(2)}, u32[]{:S(2)}) collective-permute-start(bf16[48,7296]{1,0:T(8,128)(2,1)S(1)} %pack.1.refs_0_), channel_id=1, source_target_pairs={{0,112},{1,15},{2,114},{3,5},{4,116},{5,3},{6,118},{7,9},{8,120},{... | collective-permute-start | bytes 2101256 | tf_op jit(solution)/shard_map/ppermute | solution.py:42
  43.3 18.5 %collective-permute-start.7 = (bf16[48,7296]{1,0:T(8,128)(2,1)}, bf16[48,7296]{1,0:T(8,128)(2,1)}, u32[]{:S(2)}, u32[]{:S(2)}) collective-permute-start(bf16[48,7296]{1,0:T(8,128)(2,1)} %collective-permute-done.refs_1_), channel_id=1, source_target_pairs={{0,112},{1,15},{2,114},{3,5},{4,116},{5,3},{6,118},{7,9},{8,120},{... | collective-permute-start | bytes 2101256 | tf_op jit(solution)/shard_map/ppermute | solution.py:42
  52.5 32.9 %copy-start.13 = (bf16[48,7296]{1,0:T(8,128)(2,1)}, bf16[48,7296]{1,0:T(8,128)(2,1)S(1)}, u32[]{:S(2)}) copy-start(bf16[48,7296]{1,0:T(8,128)(2,1)S(1)} %collective-permute-done.1.refs_2_) | copy-start | bytes 2101252
  52.5 11.2 %collective-permute-start.6 = (bf16[48,7296]{1,0:T(8,128)(2,1)S(1)}, bf16[48,7296]{1,0:T(8,128)(2,1)}, u32[]{:S(2)}, u32[]{:S(2)}) collective-permute-start(bf16[48,7296]{1,0:T(8,128)(2,1)S(1)} %collective-permute-done.1.refs_2_), channel_id=1, source_target_pairs={{0,16},{1,3},{2,18},{3,1},{4,20},{5,7},{6,22},{7,5},{8,24},{9,11},... | collective-permute-start | bytes 2101256 | tf_op jit(solution)/shard_map/ppermute | solution.py:38
  61.8 11.3 %collective-permute-start.11 = (bf16[48,7296]{1,0:T(8,128)(2,1)}, bf16[48,7296]{1,0:T(8,128)(2,1)S(1)}, u32[]{:S(2)}, u32[]{:S(2)}) collective-permute-start(bf16[48,7296]{1,0:T(8,128)(2,1)} %collective-permute-done.7.refs_1_), channel_id=1, source_target_pairs={{0,16},{1,3},{2,18},{3,1},{4,20},{5,7},{6,22},{7,5},{8,24},{9,11},... | collective-permute-start | bytes 2101256 | tf_op jit(solution)/shard_map/ppermute | solution.py:38
  63.6 12.8 %collective-permute-start.12 = (bf16[48,7296]{1,0:T(8,128)(2,1)}, bf16[48,7296]{1,0:T(8,128)(2,1)S(1)}, u32[]{:S(2)}, u32[]{:S(2)}) collective-permute-start(bf16[48,7296]{1,0:T(8,128)(2,1)} %collective-permute-done.6.refs_0_), channel_id=1, source_target_pairs={{0,112},{1,15},{2,114},{3,5},{4,116},{5,3},{6,118},{7,9},{8,120},{... | collective-permute-start | bytes 2101256 | tf_op jit(solution)/shard_map/ppermute | solution.py:42
  67.1 16.9 %collective-permute-start.2 = (bf16[48,7296]{1,0:T(8,128)(2,1)S(1)}, bf16[48,7296]{1,0:T(8,128)(2,1)S(1)}, u32[]{:S(2)}, u32[]{:S(2)}) collective-permute-start(bf16[48,7296]{1,0:T(8,128)(2,1)S(1)} %pack.1.refs_0_), channel_id=1, source_target_pairs={{0,1},{1,0},{2,3},{3,2},{4,5},{5,4},{6,7},{7,6},{8,9},{9,8},{10,11... | collective-permute-start | bytes 2101256 | tf_op jit(solution)/shard_map/ppermute | solution.py:47
  67.1 18.3 %collective-permute-start.4 = (bf16[48,7296]{1,0:T(8,128)(2,1)S(1)}, bf16[48,7296]{1,0:T(8,128)(2,1)S(1)}, u32[]{:S(2)}, u32[]{:S(2)}) collective-permute-start(bf16[48,7296]{1,0:T(8,128)(2,1)S(1)} %collective-permute-done.1.refs_2_), channel_id=1, source_target_pairs={{0,1},{1,0},{2,3},{3,2},{4,5},{5,4},{6,7},{7,6},{8,9},{9,8},{10,11... | collective-permute-start | bytes 2101256 | tf_op jit(solution)/shard_map/ppermute | solution.py:47
  73.1 8.8 %collective-permute-start.17 = (bf16[48,3712]{1,0:T(8,128)(2,1)S(1)}, bf16[48,3712]{1,0:T(8,128)(2,1)}, u32[]{:S(2)}, u32[]{:S(2)}) collective-permute-start(bf16[48,3712]{1,0:T(8,128)(2,1)S(1)} %slice.230), channel_id=1, source_target_pairs={{0,112},{1,15},{2,114},{3,5},{4,116},{5,3},{6,118},{7,9},{8,120},{... | collective-permute-start | bytes 1069064 | tf_op jit(solution)/shard_map/ppermute | solution.py:42
  76.5 7.5 %copy-start.11 = (bf16[48,7296]{1,0:T(8,128)(2,1)}, bf16[48,7296]{1,0:T(8,128)(2,1)S(1)}, u32[]{:S(2)}) copy-start(bf16[48,7296]{1,0:T(8,128)(2,1)S(1)} %collective-permute-done.12.refs_1_) | copy-start | bytes 2101252
  76.5 7.5 %collective-permute-start.16 = (bf16[48,3584]{1,0:T(8,128)(2,1)S(1)}, bf16[48,3584]{1,0:T(8,128)(2,1)}, u32[]{:S(2)}, u32[]{:S(2)}) collective-permute-start(bf16[48,3584]{1,0:T(8,128)(2,1)S(1)} %slice.229), channel_id=1, source_target_pairs={{0,16},{1,3},{2,18},{3,1},{4,20},{5,7},{6,22},{7,5},{8,24},{9,11},... | collective-permute-start | bytes 1032200 | tf_op jit(solution)/shard_map/ppermute | solution.py:38
  76.7 27.6 %collective-permute-start.3 = (bf16[48,7296]{1,0:T(8,128)(2,1)}, bf16[48,7296]{1,0:T(8,128)(2,1)}, u32[]{:S(2)}, u32[]{:S(2)}) collective-permute-start(bf16[48,7296]{1,0:T(8,128)(2,1)} %collective-permute-done.refs_1_), channel_id=1, source_target_pairs={{0,1},{1,0},{2,3},{3,2},{4,5},{5,4},{6,7},{7,6},{8,9},{9,8},{10,11... | collective-permute-start | bytes 2101256 | tf_op jit(solution)/shard_map/ppermute | solution.py:47
  82.0 4.8 %collective-permute-start.19 = (bf16[48,3712]{1,0:T(8,128)(2,1)}, bf16[48,3712]{1,0:T(8,128)(2,1)}, u32[]{:S(2)}, u32[]{:S(2)}) collective-permute-start(bf16[48,3712]{1,0:T(8,128)(2,1)} %collective-permute-done.17.refs_1_), channel_id=1, source_target_pairs={{0,1},{1,0},{2,3},{3,2},{4,5},{5,4},{6,7},{7,6},{8,9},{9,8},{10,11... | collective-permute-start | bytes 1069064 | tf_op jit(solution)/shard_map/ppermute | solution.py:47
  84.0 2.3 %collective-permute-start.18 = (bf16[48,3584]{1,0:T(8,128)(2,1)}, bf16[48,3584]{1,0:T(8,128)(2,1)}, u32[]{:S(2)}, u32[]{:S(2)}) collective-permute-start(bf16[48,3584]{1,0:T(8,128)(2,1)} %collective-permute-done.16.refs_0_), channel_id=1, source_target_pairs={{0,1},{1,0},{2,3},{3,2},{4,5},{5,4},{6,7},{7,6},{8,9},{9,8},{10,11... | collective-permute-start | bytes 1032200 | tf_op jit(solution)/shard_map/ppermute | solution.py:47
  84.0 0.9 copy-start.15
  84.9 27.2 %collective-permute-start.8 = (bf16[48,7296]{1,0:T(8,128)(2,1)}, bf16[48,7296]{1,0:T(8,128)(2,1)}, u32[]{:S(2)}, u32[]{:S(2)}) collective-permute-start(bf16[48,7296]{1,0:T(8,128)(2,1)} %collective-permute-done.6.refs_0_), channel_id=1, source_target_pairs={{0,1},{1,0},{2,3},{3,2},{4,5},{5,4},{6,7},{7,6},{8,9},{9,8},{10,11... | collective-permute-start | bytes 2101256 | tf_op jit(solution)/shard_map/ppermute | solution.py:47
  85.4 0.9 copy-start.17
  86.2 26.3 %collective-permute-start.9 = (bf16[48,7296]{1,0:T(8,128)(2,1)}, bf16[48,7296]{1,0:T(8,128)(2,1)}, u32[]{:S(2)}, u32[]{:S(2)}) collective-permute-start(bf16[48,7296]{1,0:T(8,128)(2,1)} %collective-permute-done.7.refs_1_), channel_id=1, source_target_pairs={{0,1},{1,0},{2,3},{3,2},{4,5},{5,4},{6,7},{7,6},{8,9},{9,8},{10,11... | collective-permute-start | bytes 2101256 | tf_op jit(solution)/shard_map/ppermute | solution.py:47
  86.3 32.8 %collective-permute-start.14 = (bf16[48,7296]{1,0:T(8,128)(2,1)}, bf16[48,7296]{1,0:T(8,128)(2,1)S(1)}, u32[]{:S(2)}, u32[]{:S(2)}) collective-permute-start(bf16[48,7296]{1,0:T(8,128)(2,1)} %copy-done.11), channel_id=1, source_target_pairs={{0,1},{1,0},{2,3},{3,2},{4,5},{5,4},{6,7},{7,6},{8,9},{9,8},{10,11... | collective-permute-start | bytes 2101256 | tf_op jit(solution)/shard_map/ppermute | solution.py:47
  86.8 32.3 %collective-permute-start.13 = (bf16[48,7296]{1,0:T(8,128)(2,1)S(1)}, bf16[48,7296]{1,0:T(8,128)(2,1)S(1)}, u32[]{:S(2)}, u32[]{:S(2)}) collective-permute-start(bf16[48,7296]{1,0:T(8,128)(2,1)S(1)} %collective-permute-done.11.refs_0_), channel_id=1, source_target_pairs={{0,1},{1,0},{2,3},{3,2},{4,5},{5,4},{6,7},{7,6},{8,9},{9,8},{10,11... | collective-permute-start | bytes 2101256 | tf_op jit(solution)/shard_map/ppermute | solution.py:47
  87.1 1.6 copy-start.1
  88.7 1.6 copy-start.3
  90.2 1.5 copy-start.5
  91.7 1.5 copy-start.7
  93.2 1.5 copy-start.9
  94.7 1.6 copy-start.2
  94.7 2.2 %copy-start.4 = (bf16[144,7168]{1,0:T(8,128)(2,1)S(1)}, bf16[144,7168]{1,0:T(8,128)(2,1)}, u32[]{:S(2)}) copy-start(bf16[144,7168]{1,0:T(8,128)(2,1)} %refs_6_.5) | copy-start | bytes 6193156
  94.7 2.7 %copy-start.6 = (bf16[1,7168,128]{2,1,0:T(8,128)(2,1)S(1)}, bf16[1,7168,128]{2,1,0:T(8,128)(2,1)}, u32[]{:S(2)}) copy-start(bf16[1,7168,128]{2,1,0:T(8,128)(2,1)} %param.21) | copy-start | bytes 5505028
  94.7 3.3 %copy-start.8 = (bf16[1,7168,128]{2,1,0:T(8,128)(2,1)S(1)}, bf16[1,7168,128]{2,1,0:T(8,128)(2,1)}, u32[]{:S(2)}) copy-start(bf16[1,7168,128]{2,1,0:T(8,128)(2,1)} %param.22) | copy-start | bytes 5505028
  94.7 3.8 %copy-start.10 = (bf16[1,128,7168]{2,1,0:T(8,128)(2,1)S(1)}, bf16[1,128,7168]{2,1,0:T(8,128)(2,1)}, u32[]{:S(2)}) copy-start(bf16[1,128,7168]{2,1,0:T(8,128)(2,1)} %param.23) | copy-start | bytes 5505028
  98.5 6.1 %copy-start.14 = (bf16[48,7296]{1,0:T(8,128)(2,1)S(1)}, bf16[48,7296]{1,0:T(8,128)(2,1)}, u32[]{:S(2)}) copy-start(bf16[48,7296]{1,0:T(8,128)(2,1)} %copy-done.13) | copy-start | bytes 2101252
  98.5 6.1 %copy-start.16 = (bf16[48,7296]{1,0:T(8,128)(2,1)S(1)}, bf16[48,7296]{1,0:T(8,128)(2,1)}, u32[]{:S(2)}) copy-start(bf16[48,7296]{1,0:T(8,128)(2,1)} %copy-done.15) | copy-start | bytes 2101252
  98.5 6.1 %copy-start.18 = (bf16[48,7296]{1,0:T(8,128)(2,1)S(1)}, bf16[48,7296]{1,0:T(8,128)(2,1)}, u32[]{:S(2)}) copy-start(bf16[48,7296]{1,0:T(8,128)(2,1)} %copy-done.17) | copy-start | bytes 2101252
  104.3 21.7 %collective-permute-start.20 = (bf16[48,7168]{1,0:T(8,128)(2,1)S(1)}, bf16[48,7168]{1,0:T(8,128)(2,1)S(1)}, u32[]{:S(2)}, u32[]{:S(2)}) collective-permute-start(bf16[48,7168]{1,0:T(8,128)(2,1)S(1)} %get-tuple-element.17), channel_id=1, source_target_pairs={{0,1},{1,0},{2,3},{3,2},{4,5},{5,4},{6,7},{7,6},{8,9},{9,8},{10,11... | collective-permute-start | bytes 2064392 | tf_op jit(solution)/shard_map/ppermute | solution.py:47
  112.1 7.0 %copy-start.12 = (bf16[48,7296]{1,0:T(8,128)(2,1)S(1)}, bf16[48,7296]{1,0:T(8,128)(2,1)}, u32[]{:S(2)}) copy-start(bf16[48,7296]{1,0:T(8,128)(2,1)} %copy-done.11) | copy-start | bytes 2101252
  112.1 44.5 %collective-permute-start.5 = (bf16[144,7168]{1,0:T(8,128)(2,1)S(1)}, bf16[144,7168]{1,0:T(8,128)(2,1)S(1)}, u32[]{:S(2)}, u32[]{:S(2)}) collective-permute-start(bf16[144,7168]{1,0:T(8,128)(2,1)S(1)} %get-tuple-element.11), channel_id=1, source_target_pairs={{0,1},{1,0},{2,3},{3,2},{4,5},{5,4},{6,7},{7,6},{8,9},{9,8},{10,11... | collective-permute-start | bytes 6193160 | tf_op jit(solution)/shard_map/ppermute | solution.py:47
  118.7 24.0 %collective-permute-start.10 = (bf16[96,7168]{1,0:T(8,128)(2,1)S(1)}, bf16[96,7168]{1,0:T(8,128)(2,1)S(1)}, u32[]{:S(2)}, u32[]{:S(2)}) collective-permute-start(bf16[96,7168]{1,0:T(8,128)(2,1)S(1)} %get-tuple-element.13), channel_id=1, source_target_pairs={{0,1},{1,0},{2,3},{3,2},{4,5},{5,4},{6,7},{7,6},{8,9},{9,8},{10,11... | collective-permute-start | bytes 4128776 | tf_op jit(solution)/shard_map/ppermute | solution.py:47
  125.6 3.3 %collective-permute-start.15 = (bf16[96,7168]{1,0:T(8,128)(2,1)S(1)}, bf16[96,7168]{1,0:T(8,128)(2,1)S(1)}, u32[]{:S(2)}, u32[]{:S(2)}) collective-permute-start(bf16[96,7168]{1,0:T(8,128)(2,1)S(1)} %get-tuple-element.15), channel_id=1, source_target_pairs={{0,1},{1,0},{2,3},{3,2},{4,5},{5,4},{6,7},{7,6},{8,9},{9,8},{10,11... | collective-permute-start | bytes 4128776 | tf_op jit(solution)/shard_map/ppermute | solution.py:47
  126.1 15.2 %collective-permute-start.33 = (bf16[48,1536]{1,0:T(8,128)(2,1)S(1)}, bf16[48,1536]{1,0:T(8,128)(2,1)S(1)}, u32[]{:S(2)}, u32[]{:S(2)}) collective-permute-start(bf16[48,1536]{1,0:T(8,128)(2,1)S(1)} %get-tuple-element.32), channel_id=1, source_target_pairs={{0,112},{1,15},{2,114},{3,5},{4,116},{5,3},{6,118},{7,9},{8,120},{... | collective-permute-start | bytes 442376 | tf_op jit(solution)/shard_map/ppermute | solution.py:42
  128.1 5.1 %collective-permute-start.25 = (bf16[48,1536]{1,0:T(8,128)(2,1)S(1)}, bf16[48,1536]{1,0:T(8,128)(2,1)S(1)}, u32[]{:S(2)}, u32[]{:S(2)}) collective-permute-start(bf16[48,1536]{1,0:T(8,128)(2,1)S(1)} %get-tuple-element.33), channel_id=1, source_target_pairs={{0,16},{1,3},{2,18},{3,1},{4,20},{5,7},{6,22},{7,5},{8,24},{9,11},... | collective-permute-start | bytes 442376 | tf_op jit(solution)/shard_map/ppermute | solution.py:38
  128.8 11.5 %collective-permute-start.29 = (bf16[48,2048]{1,0:T(8,128)(2,1)S(1)}, bf16[48,2048]{1,0:T(8,128)(2,1)S(1)}, u32[]{:S(2)}, u32[]{:S(2)}) collective-permute-start(bf16[48,2048]{1,0:T(8,128)(2,1)S(1)} %get-tuple-element.30), channel_id=1, source_target_pairs={{0,112},{1,15},{2,114},{3,5},{4,116},{5,3},{6,118},{7,9},{8,120},{... | collective-permute-start | bytes 589832 | tf_op jit(solution)/shard_map/ppermute | solution.py:42
  133.2 5.7 %collective-permute-start.21 = (bf16[48,2048]{1,0:T(8,128)(2,1)S(1)}, bf16[48,2048]{1,0:T(8,128)(2,1)S(1)}, u32[]{:S(2)}, u32[]{:S(2)}) collective-permute-start(bf16[48,2048]{1,0:T(8,128)(2,1)S(1)} %get-tuple-element.31), channel_id=1, source_target_pairs={{0,16},{1,3},{2,18},{3,1},{4,20},{5,7},{6,22},{7,5},{8,24},{9,11},... | collective-permute-start | bytes 589832 | tf_op jit(solution)/shard_map/ppermute | solution.py:38
  138.9 14.0 %collective-permute-start.26 = (bf16[48,3072]{1,0:T(8,128)(2,1)S(1)}, bf16[48,3072]{1,0:T(8,128)(2,1)S(1)}, u32[]{:S(2)}, u32[]{:S(2)}) collective-permute-start(bf16[48,3072]{1,0:T(8,128)(2,1)S(1)} %pad_maximum_fusion.2), channel_id=1, source_target_pairs={{0,112},{1,15},{2,114},{3,5},{4,116},{5,3},{6,118},{7,9},{8,120},{... | collective-permute-start | bytes 884744 | tf_op jit(solution)/shard_map/ppermute | solution.py:42
  140.4 9.5 %collective-permute-start.22 = (bf16[48,4096]{1,0:T(8,128)(2,1)S(1)}, bf16[48,4096]{1,0:T(8,128)(2,1)S(1)}, u32[]{:S(2)}, u32[]{:S(2)}) collective-permute-start(bf16[48,4096]{1,0:T(8,128)(2,1)S(1)} %pad_maximum_fusion), channel_id=1, source_target_pairs={{0,112},{1,15},{2,114},{3,5},{4,116},{5,3},{6,118},{7,9},{8,120},{... | collective-permute-start | bytes 1179656 | tf_op jit(solution)/shard_map/ppermute | solution.py:42
  141.3 8.6 %collective-permute-start.30 = (bf16[48,4096]{1,0:T(8,128)(2,1)S(1)}, bf16[48,4096]{1,0:T(8,128)(2,1)S(1)}, u32[]{:S(2)}, u32[]{:S(2)}) collective-permute-start(bf16[48,4096]{1,0:T(8,128)(2,1)S(1)} %pad_maximum_fusion.1), channel_id=1, source_target_pairs={{0,16},{1,3},{2,18},{3,1},{4,20},{5,7},{6,22},{7,5},{8,24},{9,11},... | collective-permute-start | bytes 1179656 | tf_op jit(solution)/shard_map/ppermute | solution.py:38
  142.7 10.2 %collective-permute-start.34 = (bf16[48,3072]{1,0:T(8,128)(2,1)S(1)}, bf16[48,3072]{1,0:T(8,128)(2,1)S(1)}, u32[]{:S(2)}, u32[]{:S(2)}) collective-permute-start(bf16[48,3072]{1,0:T(8,128)(2,1)S(1)} %pad_maximum_fusion.3), channel_id=1, source_target_pairs={{0,16},{1,3},{2,18},{3,1},{4,20},{5,7},{6,22},{7,5},{8,24},{9,11},... | collective-permute-start | bytes 884744 | tf_op jit(solution)/shard_map/ppermute | solution.py:38
  150.1 7.9 %collective-permute-start.31 = (bf16[48,4096]{1,0:T(8,128)(2,1)S(1)}, bf16[48,4096]{1,0:T(8,128)(2,1)S(1)}, u32[]{:S(2)}, u32[]{:S(2)}) collective-permute-start(bf16[48,4096]{1,0:T(8,128)(2,1)S(1)} %get-tuple-element.26), channel_id=1, source_target_pairs={{0,112},{1,15},{2,114},{3,5},{4,116},{5,3},{6,118},{7,9},{8,120},{... | collective-permute-start | bytes 1179656 | tf_op jit(solution)/shard_map/ppermute | solution.py:42
  152.2 7.8 %collective-permute-start.23 = (bf16[48,4096]{1,0:T(8,128)(2,1)S(1)}, bf16[48,4096]{1,0:T(8,128)(2,1)S(1)}, u32[]{:S(2)}, u32[]{:S(2)}) collective-permute-start(bf16[48,4096]{1,0:T(8,128)(2,1)S(1)} %get-tuple-element.27), channel_id=1, source_target_pairs={{0,16},{1,3},{2,18},{3,1},{4,20},{5,7},{6,22},{7,5},{8,24},{9,11},... | collective-permute-start | bytes 1179656 | tf_op jit(solution)/shard_map/ppermute | solution.py:38
  153.1 11.4 %collective-permute-start.35 = (bf16[48,3072]{1,0:T(8,128)(2,1)S(1)}, bf16[48,3072]{1,0:T(8,128)(2,1)S(1)}, u32[]{:S(2)}, u32[]{:S(2)}) collective-permute-start(bf16[48,3072]{1,0:T(8,128)(2,1)S(1)} %get-tuple-element.22), channel_id=1, source_target_pairs={{0,112},{1,15},{2,114},{3,5},{4,116},{5,3},{6,118},{7,9},{8,120},{... | collective-permute-start | bytes 884744 | tf_op jit(solution)/shard_map/ppermute | solution.py:42
  156.6 7.8 %collective-permute-start.27 = (bf16[48,3072]{1,0:T(8,128)(2,1)S(1)}, bf16[48,3072]{1,0:T(8,128)(2,1)S(1)}, u32[]{:S(2)}, u32[]{:S(2)}) collective-permute-start(bf16[48,3072]{1,0:T(8,128)(2,1)S(1)} %get-tuple-element.23), channel_id=1, source_target_pairs={{0,16},{1,3},{2,18},{3,1},{4,20},{5,7},{6,22},{7,5},{8,24},{9,11},... | collective-permute-start | bytes 884744 | tf_op jit(solution)/shard_map/ppermute | solution.py:38
  160.3 13.1 %collective-permute-start.32 = (bf16[48,4096]{1,0:T(8,128)(2,1)S(1)}, bf16[48,4096]{1,0:T(8,128)(2,1)S(1)}, u32[]{:S(2)}, u32[]{:S(2)}) collective-permute-start(bf16[48,4096]{1,0:T(8,128)(2,1)S(1)} %get-tuple-element.20), channel_id=1, source_target_pairs={{0,16},{1,3},{2,18},{3,1},{4,20},{5,7},{6,22},{7,5},{8,24},{9,11},... | collective-permute-start | bytes 1179656 | tf_op jit(solution)/shard_map/ppermute | solution.py:38
  161.1 12.3 %collective-permute-start.24 = (bf16[48,4096]{1,0:T(8,128)(2,1)S(1)}, bf16[48,4096]{1,0:T(8,128)(2,1)S(1)}, u32[]{:S(2)}, u32[]{:S(2)}) collective-permute-start(bf16[48,4096]{1,0:T(8,128)(2,1)S(1)} %get-tuple-element.21), channel_id=1, source_target_pairs={{0,112},{1,15},{2,114},{3,5},{4,116},{5,3},{6,118},{7,9},{8,120},{... | collective-permute-start | bytes 1179656 | tf_op jit(solution)/shard_map/ppermute | solution.py:42
  164.7 6.8 %collective-permute-start.36 = (bf16[48,3072]{1,0:T(8,128)(2,1)S(1)}, bf16[48,3072]{1,0:T(8,128)(2,1)S(1)}, u32[]{:S(2)}, u32[]{:S(2)}) collective-permute-start(bf16[48,3072]{1,0:T(8,128)(2,1)S(1)} %get-tuple-element.18), channel_id=1, source_target_pairs={{0,16},{1,3},{2,18},{3,1},{4,20},{5,7},{6,22},{7,5},{8,24},{9,11},... | collective-permute-start | bytes 884744 | tf_op jit(solution)/shard_map/ppermute | solution.py:38
  164.8 8.5 %collective-permute-start.28 = (bf16[48,3072]{1,0:T(8,128)(2,1)S(1)}, bf16[48,3072]{1,0:T(8,128)(2,1)S(1)}, u32[]{:S(2)}, u32[]{:S(2)}) collective-permute-start(bf16[48,3072]{1,0:T(8,128)(2,1)S(1)} %get-tuple-element.19), channel_id=1, source_target_pairs={{0,112},{1,15},{2,114},{3,5},{4,116},{5,3},{6,118},{7,9},{8,120},{... | collective-permute-start | bytes 884744 | tf_op jit(solution)/shard_map/ppermute | solution.py:42
  174.3 19.5 %copy-start.19 = (bf16[4,7168]{1,0:T(4,128)(2,1)S(1)}, bf16[4,7168]{1,0:T(4,128)(2,1)}, u32[]{:S(2)}) copy-start(bf16[4,7168]{1,0:T(4,128)(2,1)} %b_ref.1) | copy-start | bytes 172036
  174.3 19.5 %copy-start.20 = (bf16[2,7168]{1,0:T(2,128)(2,1)S(1)}, bf16[2,7168]{1,0:T(2,128)(2,1)}, u32[]{:S(2)}) copy-start(bf16[2,7168]{1,0:T(2,128)(2,1)} %a_ref.1) | copy-start | bytes 86020

commit v3 on v2

--- a/solution.py
+++ b/solution.py
@@ -77,35 +77,33 @@
     return slots
 
 
-def scatter_ring(own, other, streams):
-    count = len(streams) - 1
-    cuts = [(hi - lo) // 2 for lo, hi in zip(streams, streams[1:])]
-
-    def part(k, i):
-        at = slice(streams[i], streams[i + 1])
-        return own[k][:, at].astype(jnp.float32) + other[k][:, at].astype(jnp.float32)
-
-    low, high = [None] * count, [None] * count
-    for i in range(count):
-        far = part(4, i).astype(jnp.bfloat16)
-        low[i] = over_even(far[:, : cuts[i]])
-        high[i] = over_odd(far[:, cuts[i] :])
-    for i in range(count):
-        first, second = low[i].astype(jnp.float32), high[i].astype(jnp.float32)
-        low[i] = jnp.concatenate([part(-3, i)[:, : cuts[i]] + first, part(-3, i)[:, cuts[i] :]], 1)
-        high[i] = jnp.concatenate([part(3, i)[:, : cuts[i]], part(3, i)[:, cuts[i] :] + second], 1)
-    for k in (2, 1, 0):
-        for i in range(count):
-            one, two = low[i].astype(jnp.bfloat16), high[i].astype(jnp.bfloat16)
-            one = over_even(one) if k == 1 else over_odd(one)
-            two = over_odd(two) if k == 1 else over_even(two)
-            low[i], high[i] = one, two
+def scatter_ring(own, other, cut):
+    width = own[0].shape[1]
+    head, tail = (0, cut), (cut, width)
+
+    def part(k, cols):
+        lo, hi = cols
+        return own[k][:, lo:hi].astype(jnp.float32) + other[k][:, lo:hi].astype(jnp.float32)
+
+    def add(k, cols, piece):
+        return (part(k, cols) + piece.astype(jnp.float32)).astype(jnp.bfloat16)
+
+    short_head = over_even(part(3, head).astype(jnp.bfloat16))
+    short_tail = over_odd(part(-3, tail).astype(jnp.bfloat16))
+    long_head = over_even(part(4, head).astype(jnp.bfloat16))
+    long_tail = over_odd(part(4, tail).astype(jnp.bfloat16))
+    for step, k in enumerate((2, 1, 0)):
+        side = -1 if step == 0 else 1
+        even, odd = (over_odd, over_even) if step == 0 else (over_even, over_odd)
         if k:
-            side = 1 if k == 2 else -1
-            for i in range(count):
-                low[i] = part(side * k, i) + low[i].astype(jnp.float32)
-                high[i] = part(-side * k, i) + high[i].astype(jnp.float32)
-    return low, high
+            short = add(side * k, head, short_head), add(-side * k, tail, short_tail)
+            long_head, long_tail, *short = lax.optimization_barrier((long_head, long_tail, *short))
+            short_head, short_tail = even(short[0]), odd(short[1])
+        side = 1 if step == 1 else -1
+        even, odd = (over_even, over_odd) if step == 1 else (over_odd, over_even)
+        long_head = even(add(side * (k + 1), head, long_head))
+        long_tail = odd(add(-side * (k + 1), tail, long_tail))
+    return (long_head, short_tail), (short_head, long_tail)
 
 
 def layers(own, other, a_count, weights, pick, cut):
@@ -454,8 +452,8 @@
         for i, k in enumerate(group):
             own[k] = mine[i * rows : (i + 1) * rows]
             other[k] = theirs[i * rows : (i + 1) * rows]
-    streams = (0, width * 4 // 7, width)
-    low, high = scatter_ring(own, other, streams)
+    streams = (0, cut, width)
+    low, high = scatter_ring(own, other, cut)
     pieces = unpack(own[0], other[0], low, high, streams, a_rows)
     return tuple(finish(exchange(pieces), a_tokens, b_tokens))
 

time: 197 us -> 192 us (0.975)
  starting transfers between devices: 53.9 us -> 50.8 us
    ppermute x12 -> x11, starting transfers between devices: 44.4 us -> 37.3 us  [over_odd(): return lax.ppermute(array, EXP, pairs_along(2, odd_partner))]
    ppermute x12 -> x11, waiting for transfers between devices: 23.7 us -> 29.5 us  [over_odd(): return lax.ppermute(array, EXP, pairs_along(2, odd_partner))]
    ppermute x12 -> x11, waiting for transfers between devices: 21.9 us -> 17.1 us  [over_even(): return lax.ppermute(array, EXP, pairs_along(2, even_partner))]
    ppermute x12 -> x11, starting transfers between devices: 6.01 us -> 10 us  [over_even(): return lax.ppermute(array, EXP, pairs_along(2, even_partner))]
  transfers between devices with their start and end apart: 37 -> 35, of which waited for: 13 -> 17; matrix products, arithmetic and copies ran while one was open for 1% -> 1% of each run, Pallas kernels for 13% -> 14%
where the time goes in v3:
time: 192 us; the launch traced here: 190 us
  starting transfers between devices  50.8 us (26%)
  waiting for transfers between devices  46.8 us (24%)
  blocking collectives  46.5 us (24%)
  Pallas kernels  30.3 us (16%)
  local copies, waits for them, and re-layouts  12.6 us (7%)
    all_to_all x2, blocking collectives, exchange(): lax.all_to_all(blocks, EXP, split_axis=0, concat_axis=0, tiled=True, axis...  46.5 us
    ppermute x11, starting transfers between devices, over_odd(): return lax.ppermute(array, EXP, pairs_along(2, odd_partner))  37.3 us
    ppermute x11, waiting for transfers between devices, over_odd(): return lax.ppermute(array, EXP, pairs_along(2, odd_partner))  29.5 us
    pallas_call x4, Pallas kernels, layers(): pl.pallas_call(body, in_specs=[hbm_spec] * n_blocks + [vmem_spec] * 7, ou...  25.9 us
    ppermute x11, waiting for transfers between devices, over_even(): return lax.ppermute(array, EXP, pairs_along(2, even_partner))  17.1 us
    unnamed x42, local copies, waits for them, and re-layouts  11.5 us
    ppermute x11, starting transfers between devices, over_even(): return lax.ppermute(array, EXP, pairs_along(2, even_partner))  10 us
  transfers between devices with their start and end apart: 35, of which 17 were waited for; matrix products, arithmetic and copies ran while one was open for 1% of the time, Pallas kernels for 14%

profile of v3, /device:TPU:516, one launch (start us, length us, event | category | flops | bytes accessed | tf_op | source)
XLA Modules:
  0.0 189.8 jit_solution(16488409812347280065)
XLA Ops:
  0.6 2.1 %prepare.1 = bf16[8,352,128]{2,1,0:T(8,128)(2,1)} custom-call(bf16[2,7168]{1,0:T(2,128)(2,1)} %a_ref.1, f32[1,7168]{1,0:T(1,128)} %bitcast.32, bf16[4,7168]{1,0:T(4,128)(2,1)} %b_ref.1, f32[1,7168]{1,0:T(1,128)} %bitcast.33, s32[4,8]{1,0:T(4,128)} %refs_4_.1, f32[4,8]{1,0:T(4,128)} %refs_5_.1), custom_call_target="tpu_custom_call" | custom-call | tf_op jit(solution)/shard_map/prepare/pallas_call | solution.py:272
  2.8 28.7 %all_to_all.10.near_ref = bf16[8,352,128]{2,1,0:T(8,128)(2,1)S(1)} all-to-all(bf16[8,352,128]{2,1,0:T(8,128)(2,1)} %prepare.1), channel_id=1, replica_groups={{0,2,4,6,8,10,12,14},{16,18,20,22,24,26,28,30},{32,34,36,38,40,42,44,46..., dimensions={0} | all-to-all | bytes 1441792 | tf_op jit(solution)/shard_map/all_to_all | solution.py:64
  31.5 0.5 pack.1.refs_0_
  32.0 0.5 collective-permute-start.1
  32.5 4.1 %collective-permute-start = (bf16[48,7296]{1,0:T(8,128)(2,1)S(1)}, bf16[48,7296]{1,0:T(8,128)(2,1)S(1)}, u32[]{:S(2)}, u32[]{:S(2)}) collective-permute-start(bf16[48,7296]{1,0:T(8,128)(2,1)S(1)} %pack.1.refs_0_), channel_id=1, source_target_pairs={{0,16},{1,3},{2,18},{3,1},{4,20},{5,7},{6,22},{7,5},{8,24},{9,11},... | collective-permute-start | bytes 2101256 | tf_op jit(solution)/shard_map/ppermute | solution.py:38
  36.6 6.6 %collective-permute-done.1.refs_2_ = bf16[48,7296]{1,0:T(8,128)(2,1)S(1)} collective-permute-done((bf16[48,7296]{1,0:T(8,128)(2,1)S(1)}, bf16[48,7296]{1,0:T(8,128)(2,1)S(1)}, u32[]{:S(2)}, u32[]{:S(2)}) %collective-permute-start.1) | collective-permute-done | bytes 700448 | tf_op jit(solution)/shard_map/ppermute | solution.py:42
  43.2 2.8 %collective-permute-start.6 = (bf16[48,7296]{1,0:T(8,128)(2,1)S(1)}, bf16[48,7296]{1,0:T(8,128)(2,1)S(1)}, u32[]{:S(2)}, u32[]{:S(2)}) collective-permute-start(bf16[48,7296]{1,0:T(8,128)(2,1)S(1)} %collective-permute-done.1.refs_2_), channel_id=1, source_target_pairs={{0,16},{1,3},{2,18},{3,1},{4,20},{5,7},{6,22},{7,5},{8,24},{9,11},... | collective-permute-start | bytes 2101256 | tf_op jit(solution)/shard_map/ppermute | solution.py:38
  46.0 9.0 %collective-permute-start.7 = (bf16[48,7296]{1,0:T(8,128)(2,1)S(1)}, bf16[48,7296]{1,0:T(8,128)(2,1)S(1)}, u32[]{:S(2)}, u32[]{:S(2)}) collective-permute-start(bf16[48,7296]{1,0:T(8,128)(2,1)S(1)} %collective-permute-done.refs_1_), channel_id=1, source_target_pairs={{0,112},{1,15},{2,114},{3,5},{4,116},{5,3},{6,118},{7,9},{8,120},{... | collective-permute-start | bytes 2101256 | tf_op jit(solution)/shard_map/ppermute | solution.py:42
  55.1 9.0 %collective-permute-start.12 = (bf16[48,7296]{1,0:T(8,128)(2,1)S(1)}, bf16[48,7296]{1,0:T(8,128)(2,1)}, u32[]{:S(2)}, u32[]{:S(2)}) collective-permute-start(bf16[48,7296]{1,0:T(8,128)(2,1)S(1)} %collective-permute-done.6.refs_0_), channel_id=1, source_target_pairs={{0,112},{1,15},{2,114},{3,5},{4,116},{5,3},{6,118},{7,9},{8,120},{... | collective-permute-start | bytes 2101256 | tf_op jit(solution)/shard_map/ppermute | solution.py:42
  64.1 9.1 %collective-permute-done.12.refs_1_ = bf16[48,7296]{1,0:T(8,128)(2,1)} collective-permute-done((bf16[48,7296]{1,0:T(8,128)(2,1)S(1)}, bf16[48,7296]{1,0:T(8,128)(2,1)}, u32[]{:S(2)}, u32[]{:S(2)}) %collective-permute-start.12) | collective-permute-done | bytes 700448 | tf_op jit(solution)/shard_map/ppermute | solution.py:42
  73.2 1.9 %collective-permute-done.11.refs_0_ = bf16[48,7296]{1,0:T(8,128)(2,1)S(1)} collective-permute-done((bf16[48,7296]{1,0:T(8,128)(2,1)S(1)}, bf16[48,7296]{1,0:T(8,128)(2,1)S(1)}, u32[]{:S(2)}, u32[]{:S(2)}) %collective-permute-start.11) | collective-permute-done | bytes 700448 | tf_op jit(solution)/shard_map/ppermute | solution.py:38
  75.2 0.6 collective-permute-start.2
  75.8 1.6 copy-done.1
  77.4 1.6 copy-done.3
  79.0 1.5 copy-done.5
  80.5 1.5 copy-done.7
  82.0 1.5 copy-done.9
  83.5 1.1 copy-done.16
  84.8 0.3 collective-permute-start.3
  85.1 0.4 copy-done.2
  85.5 0.6 copy-done.4
  86.1 0.5 copy-done.6
  86.6 0.5 copy-done.8
  87.2 0.5 copy-done.10
  87.7 6.3 %shard_map.133 = (bf16[96,7168]{1,0:T(8,128)(2,1)S(1)}, bf16[96,7168]{1,0:T(8,128)(2,1)S(1)}) custom-call(bf16[48,7296]{1,0:T(8,128)(2,1)S(1)} %collective-permute-done.11.refs_0_, bf16[48,7296]{1,0:T(8,128)(2,1)} %collective-permute-done.12.refs_1_, bf16[48,7296]{1,0:T(8,128)(2,1)} %collective-permute-done.13.refs_2_, ...), custom_call_target="tpu_custom_call" | custom-call | flops 1101004800 | bytes 17203200 | tf_op jit(solution)/shard_map/pallas_call | solution.py:205
  94.2 0.5 collective-permute-start.8
  94.9 2.1 %collective-permute-start.17 = (bf16[48,3712]{1,0:T(8,128)(2,1)S(1)}, bf16[48,3712]{1,0:T(8,128)(2,1)S(1)}, u32[]{:S(2)}, u32[]{:S(2)}) collective-permute-start(bf16[48,3712]{1,0:T(8,128)(2,1)S(1)} %slice.169), channel_id=1, source_target_pairs={{0,112},{1,15},{2,114},{3,5},{4,116},{5,3},{6,118},{7,9},{8,120},{... | collective-permute-start | bytes 1069064 | tf_op jit(solution)/shard_map/ppermute | solution.py:42
  97.0 1.0 slice.168
  98.2 4.2 %collective-permute-done.17.refs_1_ = bf16[48,3712]{1,0:T(8,128)(2,1)S(1)} collective-permute-done((bf16[48,3712]{1,0:T(8,128)(2,1)S(1)}, bf16[48,3712]{1,0:T(8,128)(2,1)S(1)}, u32[]{:S(2)}, u32[]{:S(2)}) %collective-permute-start.17) | collective-permute-done | bytes 356384 | tf_op jit(solution)/shard_map/ppermute | solution.py:42
  102.4 0.4 collective-permute-start.19
  102.8 2.6 %collective-permute-done.16.refs_0_ = bf16[48,3584]{1,0:T(8,128)(2,1)S(1)} collective-permute-done((bf16[48,3584]{1,0:T(8,128)(2,1)S(1)}, bf16[48,3584]{1,0:T(8,128)(2,1)S(1)}, u32[]{:S(2)}, u32[]{:S(2)}) %collective-permute-start.16) | collective-permute-done | bytes 344096 | tf_op jit(solution)/shard_map/ppermute | solution.py:38
  105.4 8.1 %shard_map.131 = (bf16[144,7168]{1,0:T(8,128)(2,1)S(1)}, bf16[144,7168]{1,0:T(8,128)(2,1)S(1)}) custom-call(bf16[48,7296]{1,0:T(8,128)(2,1)S(1)} %pack.1.refs_0_, bf16[48,7296]{1,0:T(8,128)(2,1)S(1)} %copy-done.18, bf16[48,7296]{1,0:T(8,128)(2,1)S(1)} %copy-done.16, bf16[48,7296]{1,0:T(8,128)(2,1)S(1)} %collective-permute-done.2.refs_3_, ...), custom_call_target="tpu_custom_call" | custom-call | flops 1651507200 | bytes 19955712 | tf_op jit(solution)/shard_map/pallas_call | solution.py:205
  113.6 0.6 collective-permute-start.5
  114.2 6.5 %shard_map.132 = (bf16[96,7168]{1,0:T(8,128)(2,1)S(1)}, bf16[96,7168]{1,0:T(8,128)(2,1)S(1)}) custom-call(bf16[48,7296]{1,0:T(8,128)(2,1)S(1)} %copy-done.12, bf16[48,7296]{1,0:T(8,128)(2,1)S(1)} %copy-done.14, bf16[48,7296]{1,0:T(8,128)(2,1)S(1)} %collective-permute-done.8.refs_2_, bf16[48,7296]{1,0:T(8,128)(2,1)S(1)} %collective-permute-done.9.refs_3_, ...), custom_call_target="tpu_custom_call" | custom-call | flops 1101004800 | bytes 17203200 | tf_op jit(solution)/shard_map/pallas_call | solution.py:205
  120.9 4.9 %shard_map.134 = (bf16[48,7168]{1,0:T(8,128)(2,1)S(1)}, bf16[48,7168]{1,0:T(8,128)(2,1)S(1)}) custom-call(bf16[48,3584]{1,0:T(8,128)(2,1)S(1)} %collective-permute-done.16.refs_0_, bf16[48,3712]{1,0:T(8,128)(2,1)S(1)} %collective-permute-done.17.refs_1_, bf16[48,3584]{1,0:T(8,128)(2,1)S(1)} %collective-permute-done.18.refs_2_, ...), custom_call_target="tpu_custom_call" | custom-call | flops 550502400 | bytes 14450688 | tf_op jit(solution)/shard_map/pallas_call | solution.py:205
  125.8 0.6 collective-permute-start.20
  126.5 1.4 collective-permute-start.24
  128.3 3.6 %collective-permute-start.22 = (bf16[48,3584]{1,0:T(8,128)(2,1)S(1)}, bf16[48,3584]{1,0:T(8,128)(2,1)S(1)}, u32[]{:S(2)}, u32[]{:S(2)}) collective-permute-start(bf16[48,3584]{1,0:T(8,128)(2,1)S(1)} %get-tuple-element.46), channel_id=1, source_target_pairs={{0,112},{1,15},{2,114},{3,5},{4,116},{5,3},{6,118},{7,9},{8,120},{... | collective-permute-start | bytes 1032200 | tf_op jit(solution)/shard_map/ppermute | solution.py:42
  131.9 2.0 %collective-permute-done.24 = bf16[48,3584]{1,0:T(8,128)(2,1)S(1)} collective-permute-done((bf16[48,3584]{1,0:T(8,128)(2,1)S(1)}, bf16[48,3584]{1,0:T(8,128)(2,1)S(1)}, u32[]{:S(2)}, u32[]{:S(2)}) %collective-permute-start.24) | collective-permute-done | bytes 344096 | tf_op jit(solution)/shard_map/ppermute | solution.py:42
  133.9 1.2 collective-permute-done.23
  135.1 0.3 add_convert_fusion.8
  135.5 2.1 %collective-permute-done.22 = bf16[48,3584]{1,0:T(8,128)(2,1)S(1)} collective-permute-done((bf16[48,3584]{1,0:T(8,128)(2,1)S(1)}, bf16[48,3584]{1,0:T(8,128)(2,1)S(1)}, u32[]{:S(2)}, u32[]{:S(2)}) %collective-permute-start.22) | collective-permute-done | bytes 344096 | tf_op jit(solution)/shard_map/ppermute | solution.py:42
  137.6 1.5 collective-permute-done.21
  139.1 1.4 collective-permute-start.27
  140.5 0.4 collective-permute-start.28
  140.8 0.3 add_convert_fusion.6
  141.1 1.8 collective-permute-start.26
  142.9 1.7 collective-permute-start.25
  144.6 1.7 collective-permute-done.27
  146.4 1.4 collective-permute-done.28
  148.0 3.4 %collective-permute-done.26 = bf16[48,3584]{1,0:T(8,128)(2,1)S(1)} collective-permute-done((bf16[48,3584]{1,0:T(8,128)(2,1)S(1)}, bf16[48,3584]{1,0:T(8,128)(2,1)S(1)}, u32[]{:S(2)}, u32[]{:S(2)}) %collective-permute-start.26) | collective-permute-done | bytes 344096 | tf_op jit(solution)/shard_map/ppermute | solution.py:38
  151.4 0.3 add_convert_fusion.1
  151.7 1.9 %collective-permute-start.33 = (bf16[48,3584]{1,0:T(8,128)(2,1)S(1)}, bf16[48,3584]{1,0:T(8,128)(2,1)S(1)}, u32[]{:S(2)}, u32[]{:S(2)}) collective-permute-start(bf16[48,3584]{1,0:T(8,128)(2,1)S(1)} %get-tuple-element.38), channel_id=1, source_target_pairs={{0,112},{1,15},{2,114},{3,5},{4,116},{5,3},{6,118},{7,9},{8,120},{... | collective-permute-start | bytes 1032200 | tf_op jit(solution)/shard_map/ppermute | solution.py:42
  153.6 0.3 collective-permute-start.29
  154.0 3.4 %collective-permute-start.31 = (bf16[48,3584]{1,0:T(8,128)(2,1)S(1)}, bf16[48,3584]{1,0:T(8,128)(2,1)S(1)}, u32[]{:S(2)}, u32[]{:S(2)}) collective-permute-start(bf16[48,3584]{1,0:T(8,128)(2,1)S(1)} %get-tuple-element.31), channel_id=1, source_target_pairs={{0,112},{1,15},{2,114},{3,5},{4,116},{5,3},{6,118},{7,9},{8,120},{... | collective-permute-start | bytes 1032200 | tf_op jit(solution)/shard_map/ppermute | solution.py:42
  157.3 2.0 %collective-permute-done.33 = bf16[48,3584]{1,0:T(8,128)(2,1)S(1)} collective-permute-done((bf16[48,3584]{1,0:T(8,128)(2,1)S(1)}, bf16[48,3584]{1,0:T(8,128)(2,1)S(1)}, u32[]{:S(2)}, u32[]{:S(2)}) %collective-permute-start.33) | collective-permute-done | bytes 344096 | tf_op jit(solution)/shard_map/ppermute | solution.py:42
  159.3 1.6 collective-permute-done.29
  161.2 0.4 collective-permute-start.34
  161.6 3.4 %collective-permute-start.30 = (bf16[48,3584]{1,0:T(8,128)(2,1)S(1)}, bf16[48,3584]{1,0:T(8,128)(2,1)S(1)}, u32[]{:S(2)}, u32[]{:S(2)}) collective-permute-start(bf16[48,3584]{1,0:T(8,128)(2,1)S(1)} %get-tuple-element.35), channel_id=1, source_target_pairs={{0,112},{1,15},{2,114},{3,5},{4,116},{5,3},{6,118},{7,9},{8,120},{... | collective-permute-start | bytes 1032200 | tf_op jit(solution)/shard_map/ppermute | solution.py:42
  165.1 3.4 %collective-permute-done.34.refs_5_ = bf16[48,3584]{1,0:T(8,128)(2,1)S(1)} collective-permute-done((bf16[48,3584]{1,0:T(8,128)(2,1)S(1)}, bf16[48,3584]{1,0:T(8,128)(2,1)S(1)}, u32[]{:S(2)}, u32[]{:S(2)}) %collective-permute-start.34) | collective-permute-done | bytes 344096 | tf_op jit(solution)/shard_map/ppermute | solution.py:38
  168.6 1.7 collective-permute-done.30.refs_2_
  170.2 0.9 unpack.1
  171.1 17.8 %all_to_all.11.piece_ref = bf16[8,336,128]{2,1,0:T(8,128)(2,1)S(1)} all-to-all(bf16[8,336,128]{2,1,0:T(8,128)(2,1)S(1)} %unpack.1), channel_id=1, replica_groups={{0,2,4,6,8,10,12,14},{16,18,20,22,24,26,28,30},{32,34,36,38,40,42,44,46..., dimensions={0} | all-to-all | bytes 1376256 | tf_op jit(solution)/shard_map/all_to_all | solution.py:64
  188.9 0.9 finish.1
  (71 shorter events, 2.3 us)
Async XLA Ops:
  2.8 73.0 %copy-start = (bf16[7168,144]{0,1:T(8,128)(2,1)S(1)}, bf16[7168,144]{0,1:T(8,128)(2,1)}, u32[]{:S(2)}) copy-start(bf16[7168,144]{0,1:T(8,128)(2,1)} %param.14) | copy-start | bytes 6193156
  32.0 11.2 %collective-permute-start.1 = (bf16[48,7296]{1,0:T(8,128)(2,1)S(1)}, bf16[48,7296]{1,0:T(8,128)(2,1)S(1)}, u32[]{:S(2)}, u32[]{:S(2)}) collective-permute-start(bf16[48,7296]{1,0:T(8,128)(2,1)S(1)} %pack.1.refs_0_), channel_id=1, source_target_pairs={{0,112},{1,15},{2,114},{3,5},{4,116},{5,3},{6,118},{7,9},{8,120},{... | collective-permute-start | bytes 2101256 | tf_op jit(solution)/shard_map/ppermute | solution.py:42
  32.5 13.5 %collective-permute-start = (bf16[48,7296]{1,0:T(8,128)(2,1)S(1)}, bf16[48,7296]{1,0:T(8,128)(2,1)S(1)}, u32[]{:S(2)}, u32[]{:S(2)}) collective-permute-start(bf16[48,7296]{1,0:T(8,128)(2,1)S(1)} %pack.1.refs_0_), channel_id=1, source_target_pairs={{0,16},{1,3},{2,18},{3,1},{4,20},{5,7},{6,22},{7,5},{8,24},{9,11},... | collective-permute-start | bytes 2101256 | tf_op jit(solution)/shard_map/ppermute | solution.py:38
  43.2 32.0 %copy-start.15 = (bf16[48,7296]{1,0:T(8,128)(2,1)}, bf16[48,7296]{1,0:T(8,128)(2,1)S(1)}, u32[]{:S(2)}) copy-start(bf16[48,7296]{1,0:T(8,128)(2,1)S(1)} %collective-permute-done.1.refs_2_) | copy-start | bytes 2101252
  43.2 11.9 %collective-permute-start.6 = (bf16[48,7296]{1,0:T(8,128)(2,1)S(1)}, bf16[48,7296]{1,0:T(8,128)(2,1)S(1)}, u32[]{:S(2)}, u32[]{:S(2)}) collective-permute-start(bf16[48,7296]{1,0:T(8,128)(2,1)S(1)} %collective-permute-done.1.refs_2_), channel_id=1, source_target_pairs={{0,16},{1,3},{2,18},{3,1},{4,20},{5,7},{6,22},{7,5},{8,24},{9,11},... | collective-permute-start | bytes 2101256 | tf_op jit(solution)/shard_map/ppermute | solution.py:38
  46.0 29.1 %copy-start.17 = (bf16[48,7296]{1,0:T(8,128)(2,1)}, bf16[48,7296]{1,0:T(8,128)(2,1)S(1)}, u32[]{:S(2)}) copy-start(bf16[48,7296]{1,0:T(8,128)(2,1)S(1)} %collective-permute-done.refs_1_) | copy-start | bytes 2101252
  46.0 18.1 %collective-permute-start.7 = (bf16[48,7296]{1,0:T(8,128)(2,1)S(1)}, bf16[48,7296]{1,0:T(8,128)(2,1)S(1)}, u32[]{:S(2)}, u32[]{:S(2)}) collective-permute-start(bf16[48,7296]{1,0:T(8,128)(2,1)S(1)} %collective-permute-done.refs_1_), channel_id=1, source_target_pairs={{0,112},{1,15},{2,114},{3,5},{4,116},{5,3},{6,118},{7,9},{8,120},{... | collective-permute-start | bytes 2101256 | tf_op jit(solution)/shard_map/ppermute | solution.py:42
  55.1 20.1 %copy-start.11 = (bf16[48,7296]{1,0:T(8,128)(2,1)}, bf16[48,7296]{1,0:T(8,128)(2,1)S(1)}, u32[]{:S(2)}) copy-start(bf16[48,7296]{1,0:T(8,128)(2,1)S(1)} %collective-permute-done.6.refs_0_) | copy-start | bytes 2101252
  55.1 18.2 %collective-permute-start.12 = (bf16[48,7296]{1,0:T(8,128)(2,1)S(1)}, bf16[48,7296]{1,0:T(8,128)(2,1)}, u32[]{:S(2)}, u32[]{:S(2)}) collective-permute-start(bf16[48,7296]{1,0:T(8,128)(2,1)S(1)} %collective-permute-done.6.refs_0_), channel_id=1, source_target_pairs={{0,112},{1,15},{2,114},{3,5},{4,116},{5,3},{6,118},{7,9},{8,120},{... | collective-permute-start | bytes 2101256 | tf_op jit(solution)/shard_map/ppermute | solution.py:42
  64.1 11.1 %copy-start.13 = (bf16[48,7296]{1,0:T(8,128)(2,1)}, bf16[48,7296]{1,0:T(8,128)(2,1)S(1)}, u32[]{:S(2)}) copy-start(bf16[48,7296]{1,0:T(8,128)(2,1)S(1)} %collective-permute-done.7.refs_1_) | copy-start | bytes 2101252
  64.1 11.1 %collective-permute-start.11 = (bf16[48,7296]{1,0:T(8,128)(2,1)S(1)}, bf16[48,7296]{1,0:T(8,128)(2,1)S(1)}, u32[]{:S(2)}, u32[]{:S(2)}) collective-permute-start(bf16[48,7296]{1,0:T(8,128)(2,1)S(1)} %collective-permute-done.7.refs_1_), channel_id=1, source_target_pairs={{0,16},{1,3},{2,18},{3,1},{4,20},{5,7},{6,22},{7,5},{8,24},{9,11},... | collective-permute-start | bytes 2101256 | tf_op jit(solution)/shard_map/ppermute | solution.py:38
  73.2 11.9 %collective-permute-start.14 = (bf16[48,7296]{1,0:T(8,128)(2,1)}, bf16[48,7296]{1,0:T(8,128)(2,1)}, u32[]{:S(2)}, u32[]{:S(2)}) collective-permute-start(bf16[48,7296]{1,0:T(8,128)(2,1)} %collective-permute-done.12.refs_1_), channel_id=1, source_target_pairs={{0,1},{1,0},{2,3},{3,2},{4,5},{5,4},{6,7},{7,6},{8,9},{9,8},{10,11... | collective-permute-start | bytes 2101256 | tf_op jit(solution)/shard_map/ppermute | solution.py:47
  75.2 9.9 %collective-permute-start.13 = (bf16[48,7296]{1,0:T(8,128)(2,1)S(1)}, bf16[48,7296]{1,0:T(8,128)(2,1)}, u32[]{:S(2)}, u32[]{:S(2)}) collective-permute-start(bf16[48,7296]{1,0:T(8,128)(2,1)S(1)} %collective-permute-done.11.refs_0_), channel_id=1, source_target_pairs={{0,1},{1,0},{2,3},{3,2},{4,5},{5,4},{6,7},{7,6},{8,9},{9,8},{10,11... | collective-permute-start | bytes 2101256 | tf_op jit(solution)/shard_map/ppermute | solution.py:47
  75.2 19.5 %collective-permute-start.2 = (bf16[48,7296]{1,0:T(8,128)(2,1)S(1)}, bf16[48,7296]{1,0:T(8,128)(2,1)S(1)}, u32[]{:S(2)}, u32[]{:S(2)}) collective-permute-start(bf16[48,7296]{1,0:T(8,128)(2,1)S(1)} %pack.1.refs_0_), channel_id=1, source_target_pairs={{0,1},{1,0},{2,3},{3,2},{4,5},{5,4},{6,7},{7,6},{8,9},{9,8},{10,11... | collective-permute-start | bytes 2101256 | tf_op jit(solution)/shard_map/ppermute | solution.py:47
  75.8 1.6 copy-start.1
  77.4 1.6 copy-start.3
  79.0 1.5 copy-start.5
  80.5 1.5 copy-start.7
  82.0 1.5 copy-start.9
  83.5 1.1 copy-start.16
  83.5 1.3 copy-start.18
  83.5 2.0 %copy-start.2 = (bf16[7168,144]{0,1:T(8,128)(2,1)S(1)}, bf16[7168,144]{0,1:T(8,128)(2,1)}, u32[]{:S(2)}) copy-start(bf16[7168,144]{0,1:T(8,128)(2,1)} %param.15) | copy-start | bytes 6193156
  83.5 2.6 %copy-start.4 = (bf16[144,7168]{1,0:T(8,128)(2,1)S(1)}, bf16[144,7168]{1,0:T(8,128)(2,1)}, u32[]{:S(2)}) copy-start(bf16[144,7168]{1,0:T(8,128)(2,1)} %refs_6_.5) | copy-start | bytes 6193156
  83.5 3.2 %copy-start.6 = (bf16[1,7168,128]{2,1,0:T(8,128)(2,1)S(1)}, bf16[1,7168,128]{2,1,0:T(8,128)(2,1)}, u32[]{:S(2)}) copy-start(bf16[1,7168,128]{2,1,0:T(8,128)(2,1)} %param.21) | copy-start | bytes 5505028
  83.5 3.7 %copy-start.8 = (bf16[1,7168,128]{2,1,0:T(8,128)(2,1)S(1)}, bf16[1,7168,128]{2,1,0:T(8,128)(2,1)}, u32[]{:S(2)}) copy-start(bf16[1,7168,128]{2,1,0:T(8,128)(2,1)} %param.22) | copy-start | bytes 5505028
  83.5 4.2 %copy-start.10 = (bf16[1,128,7168]{2,1,0:T(8,128)(2,1)S(1)}, bf16[1,128,7168]{2,1,0:T(8,128)(2,1)}, u32[]{:S(2)}) copy-start(bf16[1,128,7168]{2,1,0:T(8,128)(2,1)} %param.23) | copy-start | bytes 5505028
  84.6 9.6 %copy-start.12 = (bf16[48,7296]{1,0:T(8,128)(2,1)S(1)}, bf16[48,7296]{1,0:T(8,128)(2,1)}, u32[]{:S(2)}) copy-start(bf16[48,7296]{1,0:T(8,128)(2,1)} %copy-done.11) | copy-start | bytes 2101252
  84.6 10.1 %copy-start.14 = (bf16[48,7296]{1,0:T(8,128)(2,1)S(1)}, bf16[48,7296]{1,0:T(8,128)(2,1)}, u32[]{:S(2)}) copy-start(bf16[48,7296]{1,0:T(8,128)(2,1)} %copy-done.13) | copy-start | bytes 2101252
  84.6 10.3 %collective-permute-start.4 = (bf16[48,7296]{1,0:T(8,128)(2,1)S(1)}, bf16[48,7296]{1,0:T(8,128)(2,1)S(1)}, u32[]{:S(2)}, u32[]{:S(2)}) collective-permute-start(bf16[48,7296]{1,0:T(8,128)(2,1)S(1)} %copy-done.16), channel_id=1, source_target_pairs={{0,1},{1,0},{2,3},{3,2},{4,5},{5,4},{6,7},{7,6},{8,9},{9,8},{10,11... | collective-permute-start | bytes 2101256 | tf_op jit(solution)/shard_map/ppermute | solution.py:47
  84.8 13.2 %collective-permute-start.3 = (bf16[48,7296]{1,0:T(8,128)(2,1)S(1)}, bf16[48,7296]{1,0:T(8,128)(2,1)S(1)}, u32[]{:S(2)}, u32[]{:S(2)}) collective-permute-start(bf16[48,7296]{1,0:T(8,128)(2,1)S(1)} %copy-done.18), channel_id=1, source_target_pairs={{0,1},{1,0},{2,3},{3,2},{4,5},{5,4},{6,7},{7,6},{8,9},{9,8},{10,11... | collective-permute-start | bytes 2101256 | tf_op jit(solution)/shard_map/ppermute | solution.py:47
  94.0 32.3 %collective-permute-start.15 = (bf16[96,7168]{1,0:T(8,128)(2,1)S(1)}, bf16[96,7168]{1,0:T(8,128)(2,1)S(1)}, u32[]{:S(2)}, u32[]{:S(2)}) collective-permute-start(bf16[96,7168]{1,0:T(8,128)(2,1)S(1)} %get-tuple-element.23), channel_id=1, source_target_pairs={{0,1},{1,0},{2,3},{3,2},{4,5},{5,4},{6,7},{7,6},{8,9},{9,8},{10,11... | collective-permute-start | bytes 4128776 | tf_op jit(solution)/shard_map/ppermute | solution.py:47
  94.2 19.3 %collective-permute-start.8 = (bf16[48,7296]{1,0:T(8,128)(2,1)S(1)}, bf16[48,7296]{1,0:T(8,128)(2,1)S(1)}, u32[]{:S(2)}, u32[]{:S(2)}) collective-permute-start(bf16[48,7296]{1,0:T(8,128)(2,1)S(1)} %copy-done.12), channel_id=1, source_target_pairs={{0,1},{1,0},{2,3},{3,2},{4,5},{5,4},{6,7},{7,6},{8,9},{9,8},{10,11... | collective-permute-start | bytes 2101256 | tf_op jit(solution)/shard_map/ppermute | solution.py:47
  94.7 19.5 %collective-permute-start.9 = (bf16[48,7296]{1,0:T(8,128)(2,1)S(1)}, bf16[48,7296]{1,0:T(8,128)(2,1)S(1)}, u32[]{:S(2)}, u32[]{:S(2)}) collective-permute-start(bf16[48,7296]{1,0:T(8,128)(2,1)S(1)} %copy-done.14), channel_id=1, source_target_pairs={{0,1},{1,0},{2,3},{3,2},{4,5},{5,4},{6,7},{7,6},{8,9},{9,8},{10,11... | collective-permute-start | bytes 2101256 | tf_op jit(solution)/shard_map/ppermute | solution.py:47
  94.9 7.5 %collective-permute-start.17 = (bf16[48,3712]{1,0:T(8,128)(2,1)S(1)}, bf16[48,3712]{1,0:T(8,128)(2,1)S(1)}, u32[]{:S(2)}, u32[]{:S(2)}) collective-permute-start(bf16[48,3712]{1,0:T(8,128)(2,1)S(1)} %slice.169), channel_id=1, source_target_pairs={{0,112},{1,15},{2,114},{3,5},{4,116},{5,3},{6,118},{7,9},{8,120},{... | collective-permute-start | bytes 1069064 | tf_op jit(solution)/shard_map/ppermute | solution.py:42
  98.0 7.4 %collective-permute-start.16 = (bf16[48,3584]{1,0:T(8,128)(2,1)S(1)}, bf16[48,3584]{1,0:T(8,128)(2,1)S(1)}, u32[]{:S(2)}, u32[]{:S(2)}) collective-permute-start(bf16[48,3584]{1,0:T(8,128)(2,1)S(1)} %slice.168), channel_id=1, source_target_pairs={{0,16},{1,3},{2,18},{3,1},{4,20},{5,7},{6,22},{7,5},{8,24},{9,11},... | collective-permute-start | bytes 1032200 | tf_op jit(solution)/shard_map/ppermute | solution.py:38
  102.4 18.5 %collective-permute-start.19 = (bf16[48,3712]{1,0:T(8,128)(2,1)S(1)}, bf16[48,3712]{1,0:T(8,128)(2,1)S(1)}, u32[]{:S(2)}, u32[]{:S(2)}) collective-permute-start(bf16[48,3712]{1,0:T(8,128)(2,1)S(1)} %collective-permute-done.17.refs_1_), channel_id=1, source_target_pairs={{0,1},{1,0},{2,3},{3,2},{4,5},{5,4},{6,7},{7,6},{8,9},{9,8},{10,11... | collective-permute-start | bytes 1069064 | tf_op jit(solution)/shard_map/ppermute | solution.py:47
  105.4 15.5 %collective-permute-start.18 = (bf16[48,3584]{1,0:T(8,128)(2,1)S(1)}, bf16[48,3584]{1,0:T(8,128)(2,1)S(1)}, u32[]{:S(2)}, u32[]{:S(2)}) collective-permute-start(bf16[48,3584]{1,0:T(8,128)(2,1)S(1)} %collective-permute-done.16.refs_0_), channel_id=1, source_target_pairs={{0,1},{1,0},{2,3},{3,2},{4,5},{5,4},{6,7},{7,6},{8,9},{9,8},{10,11... | collective-permute-start | bytes 1032200 | tf_op jit(solution)/shard_map/ppermute | solution.py:47
  113.6 31.1 %collective-permute-start.5 = (bf16[144,7168]{1,0:T(8,128)(2,1)S(1)}, bf16[144,7168]{1,0:T(8,128)(2,1)S(1)}, u32[]{:S(2)}, u32[]{:S(2)}) collective-permute-start(bf16[144,7168]{1,0:T(8,128)(2,1)S(1)} %get-tuple-element.19), channel_id=1, source_target_pairs={{0,1},{1,0},{2,3},{3,2},{4,5},{5,4},{6,7},{7,6},{8,9},{9,8},{10,11... | collective-permute-start | bytes 6193160 | tf_op jit(solution)/shard_map/ppermute | solution.py:47
  120.7 11.2 %collective-permute-start.10 = (bf16[96,7168]{1,0:T(8,128)(2,1)S(1)}, bf16[96,7168]{1,0:T(8,128)(2,1)S(1)}, u32[]{:S(2)}, u32[]{:S(2)}) collective-permute-start(bf16[96,7168]{1,0:T(8,128)(2,1)S(1)} %get-tuple-element.21), channel_id=1, source_target_pairs={{0,1},{1,0},{2,3},{3,2},{4,5},{5,4},{6,7},{7,6},{8,9},{9,8},{10,11... | collective-permute-start | bytes 4128776 | tf_op jit(solution)/shard_map/ppermute | solution.py:47
  125.8 2.4 %collective-permute-start.20 = (bf16[48,7168]{1,0:T(8,128)(2,1)S(1)}, bf16[48,7168]{1,0:T(8,128)(2,1)S(1)}, u32[]{:S(2)}, u32[]{:S(2)}) collective-permute-start(bf16[48,7168]{1,0:T(8,128)(2,1)S(1)} %get-tuple-element.25), channel_id=1, source_target_pairs={{0,1},{1,0},{2,3},{3,2},{4,5},{5,4},{6,7},{7,6},{8,9},{9,8},{10,11... | collective-permute-start | bytes 2064392 | tf_op jit(solution)/shard_map/ppermute | solution.py:47
  126.5 7.4 %collective-permute-start.24 = (bf16[48,3584]{1,0:T(8,128)(2,1)S(1)}, bf16[48,3584]{1,0:T(8,128)(2,1)S(1)}, u32[]{:S(2)}, u32[]{:S(2)}) collective-permute-start(bf16[48,3584]{1,0:T(8,128)(2,1)S(1)} %get-tuple-element.44), channel_id=1, source_target_pairs={{0,112},{1,15},{2,114},{3,5},{4,116},{5,3},{6,118},{7,9},{8,120},{... | collective-permute-start | bytes 1032200 | tf_op jit(solution)/shard_map/ppermute | solution.py:42
  127.9 7.2 %collective-permute-start.23 = (bf16[48,3584]{1,0:T(8,128)(2,1)S(1)}, bf16[48,3584]{1,0:T(8,128)(2,1)S(1)}, u32[]{:S(2)}, u32[]{:S(2)}) collective-permute-start(bf16[48,3584]{1,0:T(8,128)(2,1)S(1)} %get-tuple-element.45), channel_id=1, source_target_pairs={{0,16},{1,3},{2,18},{3,1},{4,20},{5,7},{6,22},{7,5},{8,24},{9,11},... | collective-permute-start | bytes 1032200 | tf_op jit(solution)/shard_map/ppermute | solution.py:38
  128.3 9.3 %collective-permute-start.22 = (bf16[48,3584]{1,0:T(8,128)(2,1)S(1)}, bf16[48,3584]{1,0:T(8,128)(2,1)S(1)}, u32[]{:S(2)}, u32[]{:S(2)}) collective-permute-start(bf16[48,3584]{1,0:T(8,128)(2,1)S(1)} %get-tuple-element.46), channel_id=1, source_target_pairs={{0,112},{1,15},{2,114},{3,5},{4,116},{5,3},{6,118},{7,9},{8,120},{... | collective-permute-start | bytes 1032200 | tf_op jit(solution)/shard_map/ppermute | solution.py:42
  131.9 7.3 %collective-permute-start.21 = (bf16[48,3584]{1,0:T(8,128)(2,1)S(1)}, bf16[48,3584]{1,0:T(8,128)(2,1)S(1)}, u32[]{:S(2)}, u32[]{:S(2)}) collective-permute-start(bf16[48,3584]{1,0:T(8,128)(2,1)S(1)} %get-tuple-element.47), channel_id=1, source_target_pairs={{0,16},{1,3},{2,18},{3,1},{4,20},{5,7},{6,22},{7,5},{8,24},{9,11},... | collective-permute-start | bytes 1032200 | tf_op jit(solution)/shard_map/ppermute | solution.py:38
  139.1 7.2 %collective-permute-start.27 = (bf16[48,3584]{1,0:T(8,128)(2,1)S(1)}, bf16[48,3584]{1,0:T(8,128)(2,1)S(1)}, u32[]{:S(2)}, u32[]{:S(2)}) collective-permute-start(bf16[48,3584]{1,0:T(8,128)(2,1)S(1)} %get-tuple-element.28), channel_id=1, source_target_pairs={{0,112},{1,15},{2,114},{3,5},{4,116},{5,3},{6,118},{7,9},{8,120},{... | collective-permute-start | bytes 1032200 | tf_op jit(solution)/shard_map/ppermute | solution.py:42
  140.5 7.2 %collective-permute-start.28 = (bf16[48,3584]{1,0:T(8,128)(2,1)S(1)}, bf16[48,3584]{1,0:T(8,128)(2,1)S(1)}, u32[]{:S(2)}, u32[]{:S(2)}) collective-permute-start(bf16[48,3584]{1,0:T(8,128)(2,1)S(1)} %get-tuple-element.29), channel_id=1, source_target_pairs={{0,16},{1,3},{2,18},{3,1},{4,20},{5,7},{6,22},{7,5},{8,24},{9,11},... | collective-permute-start | bytes 1032200 | tf_op jit(solution)/shard_map/ppermute | solution.py:38
  141.1 10.3 %collective-permute-start.26 = (bf16[48,3584]{1,0:T(8,128)(2,1)S(1)}, bf16[48,3584]{1,0:T(8,128)(2,1)S(1)}, u32[]{:S(2)}, u32[]{:S(2)}) collective-permute-start(bf16[48,3584]{1,0:T(8,128)(2,1)S(1)} %get-tuple-element.40), channel_id=1, source_target_pairs={{0,16},{1,3},{2,18},{3,1},{4,20},{5,7},{6,22},{7,5},{8,24},{9,11},... | collective-permute-start | bytes 1032200 | tf_op jit(solution)/shard_map/ppermute | solution.py:38
  142.9 8.5 %collective-permute-start.25 = (bf16[48,3584]{1,0:T(8,128)(2,1)S(1)}, bf16[48,3584]{1,0:T(8,128)(2,1)S(1)}, u32[]{:S(2)}, u32[]{:S(2)}) collective-permute-start(bf16[48,3584]{1,0:T(8,128)(2,1)S(1)} %get-tuple-element.41), channel_id=1, source_target_pairs={{0,112},{1,15},{2,114},{3,5},{4,116},{5,3},{6,118},{7,9},{8,120},{... | collective-permute-start | bytes 1032200 | tf_op jit(solution)/shard_map/ppermute | solution.py:42
  151.7 7.6 %collective-permute-start.33 = (bf16[48,3584]{1,0:T(8,128)(2,1)S(1)}, bf16[48,3584]{1,0:T(8,128)(2,1)S(1)}, u32[]{:S(2)}, u32[]{:S(2)}) collective-permute-start(bf16[48,3584]{1,0:T(8,128)(2,1)S(1)} %get-tuple-element.38), channel_id=1, source_target_pairs={{0,112},{1,15},{2,114},{3,5},{4,116},{5,3},{6,118},{7,9},{8,120},{... | collective-permute-start | bytes 1032200 | tf_op jit(solution)/shard_map/ppermute | solution.py:42
  153.6 7.2 %collective-permute-start.29 = (bf16[48,3584]{1,0:T(8,128)(2,1)S(1)}, bf16[48,3584]{1,0:T(8,128)(2,1)S(1)}, u32[]{:S(2)}, u32[]{:S(2)}) collective-permute-start(bf16[48,3584]{1,0:T(8,128)(2,1)S(1)} %get-tuple-element.39), channel_id=1, source_target_pairs={{0,16},{1,3},{2,18},{3,1},{4,20},{5,7},{6,22},{7,5},{8,24},{9,11},... | collective-permute-start | bytes 1032200 | tf_op jit(solution)/shard_map/ppermute | solution.py:38
  154.0 11.1 %collective-permute-start.31 = (bf16[48,3584]{1,0:T(8,128)(2,1)S(1)}, bf16[48,3584]{1,0:T(8,128)(2,1)S(1)}, u32[]{:S(2)}, u32[]{:S(2)}) collective-permute-start(bf16[48,3584]{1,0:T(8,128)(2,1)S(1)} %get-tuple-element.31), channel_id=1, source_target_pairs={{0,112},{1,15},{2,114},{3,5},{4,116},{5,3},{6,118},{7,9},{8,120},{... | collective-permute-start | bytes 1032200 | tf_op jit(solution)/shard_map/ppermute | solution.py:42
  157.3 7.8 %collective-permute-start.32 = (bf16[48,3584]{1,0:T(8,128)(2,1)S(1)}, bf16[48,3584]{1,0:T(8,128)(2,1)S(1)}, u32[]{:S(2)}, u32[]{:S(2)}) collective-permute-start(bf16[48,3584]{1,0:T(8,128)(2,1)S(1)} %get-tuple-element.32), channel_id=1, source_target_pairs={{0,16},{1,3},{2,18},{3,1},{4,20},{5,7},{6,22},{7,5},{8,24},{9,11},... | collective-permute-start | bytes 1032200 | tf_op jit(solution)/shard_map/ppermute | solution.py:38
  161.2 7.4 %collective-permute-start.34 = (bf16[48,3584]{1,0:T(8,128)(2,1)S(1)}, bf16[48,3584]{1,0:T(8,128)(2,1)S(1)}, u32[]{:S(2)}, u32[]{:S(2)}) collective-permute-start(bf16[48,3584]{1,0:T(8,128)(2,1)S(1)} %get-tuple-element.34), channel_id=1, source_target_pairs={{0,16},{1,3},{2,18},{3,1},{4,20},{5,7},{6,22},{7,5},{8,24},{9,11},... | collective-permute-start | bytes 1032200 | tf_op jit(solution)/shard_map/ppermute | solution.py:38
  161.6 8.6 %collective-permute-start.30 = (bf16[48,3584]{1,0:T(8,128)(2,1)S(1)}, bf16[48,3584]{1,0:T(8,128)(2,1)S(1)}, u32[]{:S(2)}, u32[]{:S(2)}) collective-permute-start(bf16[48,3584]{1,0:T(8,128)(2,1)S(1)} %get-tuple-element.35), channel_id=1, source_target_pairs={{0,112},{1,15},{2,114},{3,5},{4,116},{5,3},{6,118},{7,9},{8,120},{... | collective-permute-start | bytes 1032200 | tf_op jit(solution)/shard_map/ppermute | solution.py:42
  171.1 17.8 %copy-start.19 = (bf16[4,7168]{1,0:T(4,128)(2,1)S(1)}, bf16[4,7168]{1,0:T(4,128)(2,1)}, u32[]{:S(2)}) copy-start(bf16[4,7168]{1,0:T(4,128)(2,1)} %b_ref.1) | copy-start | bytes 172036
  171.1 17.8 %copy-start.20 = (bf16[2,7168]{1,0:T(2,128)(2,1)S(1)}, bf16[2,7168]{1,0:T(2,128)(2,1)}, u32[]{:S(2)}) copy-start(bf16[2,7168]{1,0:T(2,128)(2,1)} %a_ref.1) | copy-start | bytes 86020

commit v4 on v3

--- a/solution.py
+++ b/solution.py
@@ -97,12 +97,14 @@
         even, odd = (over_odd, over_even) if step == 0 else (over_even, over_odd)
         if k:
             short = add(side * k, head, short_head), add(-side * k, tail, short_tail)
-            long_head, long_tail, *short = lax.optimization_barrier((long_head, long_tail, *short))
-            short_head, short_tail = even(short[0]), odd(short[1])
+            long_head, long_tail, *_ = lax.optimization_barrier((long_head, long_tail, *short))
+            short_head = even(short[0])
+            short_tail = odd(short[1])
         side = 1 if step == 1 else -1
         even, odd = (over_even, over_odd) if step == 1 else (over_odd, over_even)
-        long_head = even(add(side * (k + 1), head, long_head))
-        long_tail = odd(add(-side * (k + 1), tail, long_tail))
+        long = add(side * (k + 1), head, long_head), add(-side * (k + 1), tail, long_tail)
+        long_head = even(long[0])
+        long_tail = odd(long[1])
     return (long_head, short_tail), (short_head, long_tail)
 
 
@@ -421,10 +423,14 @@
     block = pack(exchange(ready), a_rows, b_tokens.shape[0], width)
     cut = width // 2
     slots = gather_ring(block, cut)
-    swapped = {
-        k: tuple(swap_cores(p) for p in s) if isinstance(s, tuple) else swap_cores(s)
-        for k, s in slots.items()
-    }
+    swapped = {}
+    for k, piece in slots.items():
+        if isinstance(piece, tuple):
+            low = swap_cores(piece[0])
+            high = swap_cores(piece[1])
+            swapped[k] = (low, high)
+        else:
+            swapped[k] = swap_cores(piece)
     expert = lax.axis_index(EXP) // group_size
     lanes = jnp.arange(full - width)
     pick = ((lanes % EXPERTS == expert) & (lanes < 3 * EXPERTS)).astype(jnp.float32)[None, :]

time: 192 us -> 188 us (0.979)
  waiting for transfers between devices: 46.8 us -> 42.4 us
    ppermute x11, waiting for transfers between devices: 17.1 us -> 14.1 us  [over_even(): return lax.ppermute(array, EXP, pairs_along(2, even_partner))]
  transfers between devices with their start and end apart: 35 -> 35, of which waited for: 17 -> 16; matrix products, arithmetic and copies ran while one was open for 1% -> 1% of each run, Pallas kernels for 14% -> 14%
where the time goes in v4:
time: 188 us; the launch traced here: 187 us
  starting transfers between devices  52.3 us (28%)
  blocking collectives  46.5 us (25%)
  waiting for transfers between devices  42.4 us (23%)
  Pallas kernels  30.3 us (16%)
  local copies, waits for them, and re-layouts  12.6 us (7%)
    all_to_all x2, blocking collectives, exchange(): lax.all_to_all(blocks, EXP, split_axis=0, concat_axis=0, tiled=True, axis...  46.5 us
    ppermute x11, starting transfers between devices, over_odd(): return lax.ppermute(array, EXP, pairs_along(2, odd_partner))  37.6 us
    ppermute x11, waiting for transfers between devices, over_odd(): return lax.ppermute(array, EXP, pairs_along(2, odd_partner))  28 us
    pallas_call x4, Pallas kernels, layers(): pl.pallas_call(body, in_specs=[hbm_spec] * n_blocks + [vmem_spec] * 7, ou...  25.9 us
    ppermute x11, waiting for transfers between devices, over_even(): return lax.ppermute(array, EXP, pairs_along(2, even_partner))  14.1 us
    unnamed x42, local copies, waits for them, and re-layouts  11.5 us
    ppermute x11, starting transfers between devices, over_even(): return lax.ppermute(array, EXP, pairs_along(2, even_partner))  11.2 us
  transfers between devices with their start and end apart: 35, of which 16 were waited for; matrix products, arithmetic and copies ran while one was open for 1% of the time, Pallas kernels for 14%

profile of v4, /device:TPU:516, one launch (start us, length us, event | category | flops | bytes accessed | tf_op | source)
XLA Modules:
  0.0 186.9 jit_solution(10747298575952027191)
XLA Ops:
  0.6 2.1 %prepare.1 = bf16[8,352,128]{2,1,0:T(8,128)(2,1)} custom-call(bf16[2,7168]{1,0:T(2,128)(2,1)} %a_ref.1, f32[1,7168]{1,0:T(1,128)} %bitcast.32, bf16[4,7168]{1,0:T(4,128)(2,1)} %b_ref.1, f32[1,7168]{1,0:T(1,128)} %bitcast.33, s32[4,8]{1,0:T(4,128)} %refs_4_.1, f32[4,8]{1,0:T(4,128)} %refs_5_.1), custom_call_target="tpu_custom_call" | custom-call | tf_op jit(solution)/shard_map/prepare/pallas_call | solution.py:274
  2.8 28.7 %all_to_all.10.near_ref = bf16[8,352,128]{2,1,0:T(8,128)(2,1)S(1)} all-to-all(bf16[8,352,128]{2,1,0:T(8,128)(2,1)} %prepare.1), channel_id=1, replica_groups={{0,2,4,6,8,10,12,14},{16,18,20,22,24,26,28,30},{32,34,36,38,40,42,44,46..., dimensions={0} | all-to-all | bytes 1441792 | tf_op jit(solution)/shard_map/all_to_all | solution.py:64
  31.5 0.5 pack.1.refs_0_
  32.0 0.5 collective-permute-start.1
  32.5 4.1 %collective-permute-start = (bf16[48,7296]{1,0:T(8,128)(2,1)S(1)}, bf16[48,7296]{1,0:T(8,128)(2,1)S(1)}, u32[]{:S(2)}, u32[]{:S(2)}) collective-permute-start(bf16[48,7296]{1,0:T(8,128)(2,1)S(1)} %pack.1.refs_0_), channel_id=1, source_target_pairs={{0,16},{1,3},{2,18},{3,1},{4,20},{5,7},{6,22},{7,5},{8,24},{9,11},... | collective-permute-start | bytes 2101256 | tf_op jit(solution)/shard_map/ppermute | solution.py:38
  36.6 6.6 %collective-permute-done.1.refs_2_ = bf16[48,7296]{1,0:T(8,128)(2,1)S(1)} collective-permute-done((bf16[48,7296]{1,0:T(8,128)(2,1)S(1)}, bf16[48,7296]{1,0:T(8,128)(2,1)S(1)}, u32[]{:S(2)}, u32[]{:S(2)}) %collective-permute-start.1) | collective-permute-done | bytes 700448 | tf_op jit(solution)/shard_map/ppermute | solution.py:42
  43.2 2.8 %collective-permute-start.6 = (bf16[48,7296]{1,0:T(8,128)(2,1)S(1)}, bf16[48,7296]{1,0:T(8,128)(2,1)S(1)}, u32[]{:S(2)}, u32[]{:S(2)}) collective-permute-start(bf16[48,7296]{1,0:T(8,128)(2,1)S(1)} %collective-permute-done.1.refs_2_), channel_id=1, source_target_pairs={{0,16},{1,3},{2,18},{3,1},{4,20},{5,7},{6,22},{7,5},{8,24},{9,11},... | collective-permute-start | bytes 2101256 | tf_op jit(solution)/shard_map/ppermute | solution.py:38
  46.0 9.0 %collective-permute-start.7 = (bf16[48,7296]{1,0:T(8,128)(2,1)S(1)}, bf16[48,7296]{1,0:T(8,128)(2,1)S(1)}, u32[]{:S(2)}, u32[]{:S(2)}) collective-permute-start(bf16[48,7296]{1,0:T(8,128)(2,1)S(1)} %collective-permute-done.refs_1_), channel_id=1, source_target_pairs={{0,112},{1,15},{2,114},{3,5},{4,116},{5,3},{6,118},{7,9},{8,120},{... | collective-permute-start | bytes 2101256 | tf_op jit(solution)/shard_map/ppermute | solution.py:42
  55.1 9.0 %collective-permute-start.12 = (bf16[48,7296]{1,0:T(8,128)(2,1)S(1)}, bf16[48,7296]{1,0:T(8,128)(2,1)}, u32[]{:S(2)}, u32[]{:S(2)}) collective-permute-start(bf16[48,7296]{1,0:T(8,128)(2,1)S(1)} %collective-permute-done.6.refs_0_), channel_id=1, source_target_pairs={{0,112},{1,15},{2,114},{3,5},{4,116},{5,3},{6,118},{7,9},{8,120},{... | collective-permute-start | bytes 2101256 | tf_op jit(solution)/shard_map/ppermute | solution.py:42
  64.1 9.1 %collective-permute-done.12.refs_1_ = bf16[48,7296]{1,0:T(8,128)(2,1)} collective-permute-done((bf16[48,7296]{1,0:T(8,128)(2,1)S(1)}, bf16[48,7296]{1,0:T(8,128)(2,1)}, u32[]{:S(2)}, u32[]{:S(2)}) %collective-permute-start.12) | collective-permute-done | bytes 700448 | tf_op jit(solution)/shard_map/ppermute | solution.py:42
  73.2 1.9 %collective-permute-done.11.refs_0_ = bf16[48,7296]{1,0:T(8,128)(2,1)S(1)} collective-permute-done((bf16[48,7296]{1,0:T(8,128)(2,1)S(1)}, bf16[48,7296]{1,0:T(8,128)(2,1)S(1)}, u32[]{:S(2)}, u32[]{:S(2)}) %collective-permute-start.11) | collective-permute-done | bytes 700448 | tf_op jit(solution)/shard_map/ppermute | solution.py:38
  75.2 0.6 collective-permute-start.2
  75.8 1.6 copy-done.1
  77.4 1.6 copy-done.3
  79.0 1.5 copy-done.5
  80.5 1.5 copy-done.7
  82.0 1.5 copy-done.9
  83.5 1.1 copy-done.16
  84.8 0.3 collective-permute-start.3
  85.1 0.4 copy-done.2
  85.5 0.6 copy-done.4
  86.1 0.5 copy-done.6
  86.6 0.5 copy-done.8
  87.2 0.5 copy-done.10
  87.7 6.3 %shard_map.133 = (bf16[96,7168]{1,0:T(8,128)(2,1)S(1)}, bf16[96,7168]{1,0:T(8,128)(2,1)S(1)}) custom-call(bf16[48,7296]{1,0:T(8,128)(2,1)S(1)} %collective-permute-done.11.refs_0_, bf16[48,7296]{1,0:T(8,128)(2,1)} %collective-permute-done.12.refs_1_, bf16[48,7296]{1,0:T(8,128)(2,1)} %collective-permute-done.13.refs_2_, ...), custom_call_target="tpu_custom_call" | custom-call | flops 1101004800 | bytes 17203200 | tf_op jit(solution)/shard_map/pallas_call | solution.py:207
  94.2 0.5 collective-permute-start.8
  94.9 2.1 %collective-permute-start.17 = (bf16[48,3712]{1,0:T(8,128)(2,1)S(1)}, bf16[48,3712]{1,0:T(8,128)(2,1)S(1)}, u32[]{:S(2)}, u32[]{:S(2)}) collective-permute-start(bf16[48,3712]{1,0:T(8,128)(2,1)S(1)} %slice.169), channel_id=1, source_target_pairs={{0,112},{1,15},{2,114},{3,5},{4,116},{5,3},{6,118},{7,9},{8,120},{... | collective-permute-start | bytes 1069064 | tf_op jit(solution)/shard_map/ppermute | solution.py:42
  97.0 1.0 slice.168
  98.2 4.2 %collective-permute-done.17.refs_1_ = bf16[48,3712]{1,0:T(8,128)(2,1)S(1)} collective-permute-done((bf16[48,3712]{1,0:T(8,128)(2,1)S(1)}, bf16[48,3712]{1,0:T(8,128)(2,1)S(1)}, u32[]{:S(2)}, u32[]{:S(2)}) %collective-permute-start.17) | collective-permute-done | bytes 356384 | tf_op jit(solution)/shard_map/ppermute | solution.py:42
  102.4 0.4 collective-permute-start.19
  102.8 2.6 %collective-permute-done.16.refs_0_ = bf16[48,3584]{1,0:T(8,128)(2,1)S(1)} collective-permute-done((bf16[48,3584]{1,0:T(8,128)(2,1)S(1)}, bf16[48,3584]{1,0:T(8,128)(2,1)S(1)}, u32[]{:S(2)}, u32[]{:S(2)}) %collective-permute-start.16) | collective-permute-done | bytes 344096 | tf_op jit(solution)/shard_map/ppermute | solution.py:38
  105.4 8.1 %shard_map.131 = (bf16[144,7168]{1,0:T(8,128)(2,1)S(1)}, bf16[144,7168]{1,0:T(8,128)(2,1)S(1)}) custom-call(bf16[48,7296]{1,0:T(8,128)(2,1)S(1)} %pack.1.refs_0_, bf16[48,7296]{1,0:T(8,128)(2,1)S(1)} %copy-done.18, bf16[48,7296]{1,0:T(8,128)(2,1)S(1)} %copy-done.16, bf16[48,7296]{1,0:T(8,128)(2,1)S(1)} %collective-permute-done.2.refs_3_, ...), custom_call_target="tpu_custom_call" | custom-call | flops 1651507200 | bytes 19955712 | tf_op jit(solution)/shard_map/pallas_call | solution.py:207
  113.6 0.6 collective-permute-start.5
  114.2 6.5 %shard_map.132 = (bf16[96,7168]{1,0:T(8,128)(2,1)S(1)}, bf16[96,7168]{1,0:T(8,128)(2,1)S(1)}) custom-call(bf16[48,7296]{1,0:T(8,128)(2,1)S(1)} %copy-done.12, bf16[48,7296]{1,0:T(8,128)(2,1)S(1)} %copy-done.14, bf16[48,7296]{1,0:T(8,128)(2,1)S(1)} %collective-permute-done.8.refs_2_, bf16[48,7296]{1,0:T(8,128)(2,1)S(1)} %collective-permute-done.9.refs_3_, ...), custom_call_target="tpu_custom_call" | custom-call | flops 1101004800 | bytes 17203200 | tf_op jit(solution)/shard_map/pallas_call | solution.py:207
  120.9 4.9 %shard_map.134 = (bf16[48,7168]{1,0:T(8,128)(2,1)S(1)}, bf16[48,7168]{1,0:T(8,128)(2,1)S(1)}) custom-call(bf16[48,3584]{1,0:T(8,128)(2,1)S(1)} %collective-permute-done.16.refs_0_, bf16[48,3712]{1,0:T(8,128)(2,1)S(1)} %collective-permute-done.17.refs_1_, bf16[48,3584]{1,0:T(8,128)(2,1)S(1)} %collective-permute-done.18.refs_2_, ...), custom_call_target="tpu_custom_call" | custom-call | flops 550502400 | bytes 14450688 | tf_op jit(solution)/shard_map/pallas_call | solution.py:207
  125.8 0.6 collective-permute-start.20
  126.5 1.4 collective-permute-start.24
  127.9 0.2 collective-permute-done.20
  128.3 3.6 %collective-permute-start.22 = (bf16[48,3584]{1,0:T(8,128)(2,1)S(1)}, bf16[48,3584]{1,0:T(8,128)(2,1)S(1)}, u32[]{:S(2)}, u32[]{:S(2)}) collective-permute-start(bf16[48,3584]{1,0:T(8,128)(2,1)S(1)} %get-tuple-element.38), channel_id=1, source_target_pairs={{0,112},{1,15},{2,114},{3,5},{4,116},{5,3},{6,118},{7,9},{8,120},{... | collective-permute-start | bytes 1032200 | tf_op jit(solution)/shard_map/ppermute | solution.py:42
  131.9 2.0 %collective-permute-done.24 = bf16[48,3584]{1,0:T(8,128)(2,1)S(1)} collective-permute-done((bf16[48,3584]{1,0:T(8,128)(2,1)S(1)}, bf16[48,3584]{1,0:T(8,128)(2,1)S(1)}, u32[]{:S(2)}, u32[]{:S(2)}) %collective-permute-start.24) | collective-permute-done | bytes 344096 | tf_op jit(solution)/shard_map/ppermute | solution.py:42
  133.9 1.2 collective-permute-done.23
  135.1 0.3 add_convert_fusion.8
  135.6 3.6 %collective-permute-start.27 = (bf16[48,3584]{1,0:T(8,128)(2,1)S(1)}, bf16[48,3584]{1,0:T(8,128)(2,1)S(1)}, u32[]{:S(2)}, u32[]{:S(2)}) collective-permute-start(bf16[48,3584]{1,0:T(8,128)(2,1)S(1)} %get-tuple-element.35), channel_id=1, source_target_pairs={{0,112},{1,15},{2,114},{3,5},{4,116},{5,3},{6,118},{7,9},{8,120},{... | collective-permute-start | bytes 1032200 | tf_op jit(solution)/shard_map/ppermute | solution.py:42
  139.3 0.3 add_convert_fusion.6
  139.7 3.2 %collective-permute-start.25 = (bf16[48,3584]{1,0:T(8,128)(2,1)S(1)}, bf16[48,3584]{1,0:T(8,128)(2,1)S(1)}, u32[]{:S(2)}, u32[]{:S(2)}) collective-permute-start(bf16[48,3584]{1,0:T(8,128)(2,1)S(1)} %get-tuple-element.33), channel_id=1, source_target_pairs={{0,112},{1,15},{2,114},{3,5},{4,116},{5,3},{6,118},{7,9},{8,120},{... | collective-permute-start | bytes 1032200 | tf_op jit(solution)/shard_map/ppermute | solution.py:42
  142.9 1.6 collective-permute-done.27
  144.5 0.3 add_convert_fusion.4
  144.8 2.1 %collective-permute-done.26 = bf16[48,3584]{1,0:T(8,128)(2,1)S(1)} collective-permute-done((bf16[48,3584]{1,0:T(8,128)(2,1)S(1)}, bf16[48,3584]{1,0:T(8,128)(2,1)S(1)}, u32[]{:S(2)}, u32[]{:S(2)}) %collective-permute-start.26) | collective-permute-done | bytes 344096 | tf_op jit(solution)/shard_map/ppermute | solution.py:38
  146.9 1.3 collective-permute-done.25
  148.2 0.3 add_convert_fusion.1
  148.5 2.4 %collective-permute-start.33 = (bf16[48,3584]{1,0:T(8,128)(2,1)S(1)}, bf16[48,3584]{1,0:T(8,128)(2,1)S(1)}, u32[]{:S(2)}, u32[]{:S(2)}) collective-permute-start(bf16[48,3584]{1,0:T(8,128)(2,1)S(1)} %get-tuple-element.30), channel_id=1, source_target_pairs={{0,112},{1,15},{2,114},{3,5},{4,116},{5,3},{6,118},{7,9},{8,120},{... | collective-permute-start | bytes 1032200 | tf_op jit(solution)/shard_map/ppermute | solution.py:42
  150.9 1.5 collective-permute-start.29
  152.4 1.4 collective-permute-start.31
  153.8 0.7 collective-permute-start.32
  154.5 1.6 collective-permute-done.33
  156.1 2.0 %collective-permute-done.29 = bf16[48,3584]{1,0:T(8,128)(2,1)S(1)} collective-permute-done((bf16[48,3584]{1,0:T(8,128)(2,1)S(1)}, bf16[48,3584]{1,0:T(8,128)(2,1)S(1)}, u32[]{:S(2)}, u32[]{:S(2)}) %collective-permute-start.29) | collective-permute-done | bytes 344096 | tf_op jit(solution)/shard_map/ppermute | solution.py:38
  158.1 0.3 add_convert_fusion
  158.4 1.7 collective-permute-start.34
  160.1 1.4 collective-permute-start.30
  161.8 4.0 %collective-permute-done.34.refs_5_ = bf16[48,3584]{1,0:T(8,128)(2,1)S(1)} collective-permute-done((bf16[48,3584]{1,0:T(8,128)(2,1)S(1)}, bf16[48,3584]{1,0:T(8,128)(2,1)S(1)}, u32[]{:S(2)}, u32[]{:S(2)}) %collective-permute-start.34) | collective-permute-done | bytes 344096 | tf_op jit(solution)/shard_map/ppermute | solution.py:38
  165.8 1.5 collective-permute-done.30.refs_2_
  167.3 0.9 unpack.1
  168.3 17.8 %all_to_all.11.piece_ref = bf16[8,336,128]{2,1,0:T(8,128)(2,1)S(1)} all-to-all(bf16[8,336,128]{2,1,0:T(8,128)(2,1)S(1)} %unpack.1), channel_id=1, replica_groups={{0,2,4,6,8,10,12,14},{16,18,20,22,24,26,28,30},{32,34,36,38,40,42,44,46..., dimensions={0} | all-to-all | bytes 1376256 | tf_op jit(solution)/shard_map/all_to_all | solution.py:64
  186.1 0.9 finish.1
  (71 shorter events, 2.0 us)
Async XLA Ops:
  2.8 73.0 %copy-start = (bf16[7168,144]{0,1:T(8,128)(2,1)S(1)}, bf16[7168,144]{0,1:T(8,128)(2,1)}, u32[]{:S(2)}) copy-start(bf16[7168,144]{0,1:T(8,128)(2,1)} %param.14) | copy-start | bytes 6193156
  32.0 11.2 %collective-permute-start.1 = (bf16[48,7296]{1,0:T(8,128)(2,1)S(1)}, bf16[48,7296]{1,0:T(8,128)(2,1)S(1)}, u32[]{:S(2)}, u32[]{:S(2)}) collective-permute-start(bf16[48,7296]{1,0:T(8,128)(2,1)S(1)} %pack.1.refs_0_), channel_id=1, source_target_pairs={{0,112},{1,15},{2,114},{3,5},{4,116},{5,3},{6,118},{7,9},{8,120},{... | collective-permute-start | bytes 2101256 | tf_op jit(solution)/shard_map/ppermute | solution.py:42
  32.5 13.5 %collective-permute-start = (bf16[48,7296]{1,0:T(8,128)(2,1)S(1)}, bf16[48,7296]{1,0:T(8,128)(2,1)S(1)}, u32[]{:S(2)}, u32[]{:S(2)}) collective-permute-start(bf16[48,7296]{1,0:T(8,128)(2,1)S(1)} %pack.1.refs_0_), channel_id=1, source_target_pairs={{0,16},{1,3},{2,18},{3,1},{4,20},{5,7},{6,22},{7,5},{8,24},{9,11},... | collective-permute-start | bytes 2101256 | tf_op jit(solution)/shard_map/ppermute | solution.py:38
  43.2 32.0 %copy-start.15 = (bf16[48,7296]{1,0:T(8,128)(2,1)}, bf16[48,7296]{1,0:T(8,128)(2,1)S(1)}, u32[]{:S(2)}) copy-start(bf16[48,7296]{1,0:T(8,128)(2,1)S(1)} %collective-permute-done.1.refs_2_) | copy-start | bytes 2101252
  43.2 11.9 %collective-permute-start.6 = (bf16[48,7296]{1,0:T(8,128)(2,1)S(1)}, bf16[48,7296]{1,0:T(8,128)(2,1)S(1)}, u32[]{:S(2)}, u32[]{:S(2)}) collective-permute-start(bf16[48,7296]{1,0:T(8,128)(2,1)S(1)} %collective-permute-done.1.refs_2_), channel_id=1, source_target_pairs={{0,16},{1,3},{2,18},{3,1},{4,20},{5,7},{6,22},{7,5},{8,24},{9,11},... | collective-permute-start | bytes 2101256 | tf_op jit(solution)/shard_map/ppermute | solution.py:38
  46.0 29.1 %copy-start.17 = (bf16[48,7296]{1,0:T(8,128)(2,1)}, bf16[48,7296]{1,0:T(8,128)(2,1)S(1)}, u32[]{:S(2)}) copy-start(bf16[48,7296]{1,0:T(8,128)(2,1)S(1)} %collective-permute-done.refs_1_) | copy-start | bytes 2101252
  46.0 18.1 %collective-permute-start.7 = (bf16[48,7296]{1,0:T(8,128)(2,1)S(1)}, bf16[48,7296]{1,0:T(8,128)(2,1)S(1)}, u32[]{:S(2)}, u32[]{:S(2)}) collective-permute-start(bf16[48,7296]{1,0:T(8,128)(2,1)S(1)} %collective-permute-done.refs_1_), channel_id=1, source_target_pairs={{0,112},{1,15},{2,114},{3,5},{4,116},{5,3},{6,118},{7,9},{8,120},{... | collective-permute-start | bytes 2101256 | tf_op jit(solution)/shard_map/ppermute | solution.py:42
  55.1 20.1 %copy-start.11 = (bf16[48,7296]{1,0:T(8,128)(2,1)}, bf16[48,7296]{1,0:T(8,128)(2,1)S(1)}, u32[]{:S(2)}) copy-start(bf16[48,7296]{1,0:T(8,128)(2,1)S(1)} %collective-permute-done.6.refs_0_) | copy-start | bytes 2101252
  55.1 18.2 %collective-permute-start.12 = (bf16[48,7296]{1,0:T(8,128)(2,1)S(1)}, bf16[48,7296]{1,0:T(8,128)(2,1)}, u32[]{:S(2)}, u32[]{:S(2)}) collective-permute-start(bf16[48,7296]{1,0:T(8,128)(2,1)S(1)} %collective-permute-done.6.refs_0_), channel_id=1, source_target_pairs={{0,112},{1,15},{2,114},{3,5},{4,116},{5,3},{6,118},{7,9},{8,120},{... | collective-permute-start | bytes 2101256 | tf_op jit(solution)/shard_map/ppermute | solution.py:42
  64.1 11.1 %copy-start.13 = (bf16[48,7296]{1,0:T(8,128)(2,1)}, bf16[48,7296]{1,0:T(8,128)(2,1)S(1)}, u32[]{:S(2)}) copy-start(bf16[48,7296]{1,0:T(8,128)(2,1)S(1)} %collective-permute-done.7.refs_1_) | copy-start | bytes 2101252
  64.1 11.1 %collective-permute-start.11 = (bf16[48,7296]{1,0:T(8,128)(2,1)S(1)}, bf16[48,7296]{1,0:T(8,128)(2,1)S(1)}, u32[]{:S(2)}, u32[]{:S(2)}) collective-permute-start(bf16[48,7296]{1,0:T(8,128)(2,1)S(1)} %collective-permute-done.7.refs_1_), channel_id=1, source_target_pairs={{0,16},{1,3},{2,18},{3,1},{4,20},{5,7},{6,22},{7,5},{8,24},{9,11},... | collective-permute-start | bytes 2101256 | tf_op jit(solution)/shard_map/ppermute | solution.py:38
  73.2 11.9 %collective-permute-start.14 = (bf16[48,7296]{1,0:T(8,128)(2,1)}, bf16[48,7296]{1,0:T(8,128)(2,1)}, u32[]{:S(2)}, u32[]{:S(2)}) collective-permute-start(bf16[48,7296]{1,0:T(8,128)(2,1)} %collective-permute-done.12.refs_1_), channel_id=1, source_target_pairs={{0,1},{1,0},{2,3},{3,2},{4,5},{5,4},{6,7},{7,6},{8,9},{9,8},{10,11... | collective-permute-start | bytes 2101256 | tf_op jit(solution)/shard_map/ppermute | solution.py:47
  75.2 9.9 %collective-permute-start.13 = (bf16[48,7296]{1,0:T(8,128)(2,1)S(1)}, bf16[48,7296]{1,0:T(8,128)(2,1)}, u32[]{:S(2)}, u32[]{:S(2)}) collective-permute-start(bf16[48,7296]{1,0:T(8,128)(2,1)S(1)} %collective-permute-done.11.refs_0_), channel_id=1, source_target_pairs={{0,1},{1,0},{2,3},{3,2},{4,5},{5,4},{6,7},{7,6},{8,9},{9,8},{10,11... | collective-permute-start | bytes 2101256 | tf_op jit(solution)/shard_map/ppermute | solution.py:47
  75.2 19.5 %collective-permute-start.2 = (bf16[48,7296]{1,0:T(8,128)(2,1)S(1)}, bf16[48,7296]{1,0:T(8,128)(2,1)S(1)}, u32[]{:S(2)}, u32[]{:S(2)}) collective-permute-start(bf16[48,7296]{1,0:T(8,128)(2,1)S(1)} %pack.1.refs_0_), channel_id=1, source_target_pairs={{0,1},{1,0},{2,3},{3,2},{4,5},{5,4},{6,7},{7,6},{8,9},{9,8},{10,11... | collective-permute-start | bytes 2101256 | tf_op jit(solution)/shard_map/ppermute | solution.py:47
  75.8 1.6 copy-start.1
  77.4 1.6 copy-start.3
  79.0 1.5 copy-start.5
  80.5 1.5 copy-start.7
  82.0 1.5 copy-start.9
  83.5 1.1 copy-start.16
  83.5 1.3 copy-start.18
  83.5 2.0 %copy-start.2 = (bf16[7168,144]{0,1:T(8,128)(2,1)S(1)}, bf16[7168,144]{0,1:T(8,128)(2,1)}, u32[]{:S(2)}) copy-start(bf16[7168,144]{0,1:T(8,128)(2,1)} %param.15) | copy-start | bytes 6193156
  83.5 2.6 %copy-start.4 = (bf16[144,7168]{1,0:T(8,128)(2,1)S(1)}, bf16[144,7168]{1,0:T(8,128)(2,1)}, u32[]{:S(2)}) copy-start(bf16[144,7168]{1,0:T(8,128)(2,1)} %refs_6_.5) | copy-start | bytes 6193156
  83.5 3.2 %copy-start.6 = (bf16[1,7168,128]{2,1,0:T(8,128)(2,1)S(1)}, bf16[1,7168,128]{2,1,0:T(8,128)(2,1)}, u32[]{:S(2)}) copy-start(bf16[1,7168,128]{2,1,0:T(8,128)(2,1)} %param.21) | copy-start | bytes 5505028
  83.5 3.7 %copy-start.8 = (bf16[1,7168,128]{2,1,0:T(8,128)(2,1)S(1)}, bf16[1,7168,128]{2,1,0:T(8,128)(2,1)}, u32[]{:S(2)}) copy-start(bf16[1,7168,128]{2,1,0:T(8,128)(2,1)} %param.22) | copy-start | bytes 5505028
  83.5 4.2 %copy-start.10 = (bf16[1,128,7168]{2,1,0:T(8,128)(2,1)S(1)}, bf16[1,128,7168]{2,1,0:T(8,128)(2,1)}, u32[]{:S(2)}) copy-start(bf16[1,128,7168]{2,1,0:T(8,128)(2,1)} %param.23) | copy-start | bytes 5505028
  84.6 9.6 %copy-start.12 = (bf16[48,7296]{1,0:T(8,128)(2,1)S(1)}, bf16[48,7296]{1,0:T(8,128)(2,1)}, u32[]{:S(2)}) copy-start(bf16[48,7296]{1,0:T(8,128)(2,1)} %copy-done.11) | copy-start | bytes 2101252
  84.6 10.1 %copy-start.14 = (bf16[48,7296]{1,0:T(8,128)(2,1)S(1)}, bf16[48,7296]{1,0:T(8,128)(2,1)}, u32[]{:S(2)}) copy-start(bf16[48,7296]{1,0:T(8,128)(2,1)} %copy-done.13) | copy-start | bytes 2101252
  84.6 10.3 %collective-permute-start.4 = (bf16[48,7296]{1,0:T(8,128)(2,1)S(1)}, bf16[48,7296]{1,0:T(8,128)(2,1)S(1)}, u32[]{:S(2)}, u32[]{:S(2)}) collective-permute-start(bf16[48,7296]{1,0:T(8,128)(2,1)S(1)} %copy-done.16), channel_id=1, source_target_pairs={{0,1},{1,0},{2,3},{3,2},{4,5},{5,4},{6,7},{7,6},{8,9},{9,8},{10,11... | collective-permute-start | bytes 2101256 | tf_op jit(solution)/shard_map/ppermute | solution.py:47
  84.8 13.2 %collective-permute-start.3 = (bf16[48,7296]{1,0:T(8,128)(2,1)S(1)}, bf16[48,7296]{1,0:T(8,128)(2,1)S(1)}, u32[]{:S(2)}, u32[]{:S(2)}) collective-permute-start(bf16[48,7296]{1,0:T(8,128)(2,1)S(1)} %copy-done.18), channel_id=1, source_target_pairs={{0,1},{1,0},{2,3},{3,2},{4,5},{5,4},{6,7},{7,6},{8,9},{9,8},{10,11... | collective-permute-start | bytes 2101256 | tf_op jit(solution)/shard_map/ppermute | solution.py:47
  94.0 32.3 %collective-permute-start.15 = (bf16[96,7168]{1,0:T(8,128)(2,1)S(1)}, bf16[96,7168]{1,0:T(8,128)(2,1)S(1)}, u32[]{:S(2)}, u32[]{:S(2)}) collective-permute-start(bf16[96,7168]{1,0:T(8,128)(2,1)S(1)} %get-tuple-element.19), channel_id=1, source_target_pairs={{0,1},{1,0},{2,3},{3,2},{4,5},{5,4},{6,7},{7,6},{8,9},{9,8},{10,11... | collective-permute-start | bytes 4128776 | tf_op jit(solution)/shard_map/ppermute | solution.py:47
  94.2 19.3 %collective-permute-start.8 = (bf16[48,7296]{1,0:T(8,128)(2,1)S(1)}, bf16[48,7296]{1,0:T(8,128)(2,1)S(1)}, u32[]{:S(2)}, u32[]{:S(2)}) collective-permute-start(bf16[48,7296]{1,0:T(8,128)(2,1)S(1)} %copy-done.12), channel_id=1, source_target_pairs={{0,1},{1,0},{2,3},{3,2},{4,5},{5,4},{6,7},{7,6},{8,9},{9,8},{10,11... | collective-permute-start | bytes 2101256 | tf_op jit(solution)/shard_map/ppermute | solution.py:47
  94.7 19.5 %collective-permute-start.9 = (bf16[48,7296]{1,0:T(8,128)(2,1)S(1)}, bf16[48,7296]{1,0:T(8,128)(2,1)S(1)}, u32[]{:S(2)}, u32[]{:S(2)}) collective-permute-start(bf16[48,7296]{1,0:T(8,128)(2,1)S(1)} %copy-done.14), channel_id=1, source_target_pairs={{0,1},{1,0},{2,3},{3,2},{4,5},{5,4},{6,7},{7,6},{8,9},{9,8},{10,11... | collective-permute-start | bytes 2101256 | tf_op jit(solution)/shard_map/ppermute | solution.py:47
  94.9 7.5 %collective-permute-start.17 = (bf16[48,3712]{1,0:T(8,128)(2,1)S(1)}, bf16[48,3712]{1,0:T(8,128)(2,1)S(1)}, u32[]{:S(2)}, u32[]{:S(2)}) collective-permute-start(bf16[48,3712]{1,0:T(8,128)(2,1)S(1)} %slice.169), channel_id=1, source_target_pairs={{0,112},{1,15},{2,114},{3,5},{4,116},{5,3},{6,118},{7,9},{8,120},{... | collective-permute-start | bytes 1069064 | tf_op jit(solution)/shard_map/ppermute | solution.py:42
  98.0 7.4 %collective-permute-start.16 = (bf16[48,3584]{1,0:T(8,128)(2,1)S(1)}, bf16[48,3584]{1,0:T(8,128)(2,1)S(1)}, u32[]{:S(2)}, u32[]{:S(2)}) collective-permute-start(bf16[48,3584]{1,0:T(8,128)(2,1)S(1)} %slice.168), channel_id=1, source_target_pairs={{0,16},{1,3},{2,18},{3,1},{4,20},{5,7},{6,22},{7,5},{8,24},{9,11},... | collective-permute-start | bytes 1032200 | tf_op jit(solution)/shard_map/ppermute | solution.py:38
  102.4 18.5 %collective-permute-start.19 = (bf16[48,3712]{1,0:T(8,128)(2,1)S(1)}, bf16[48,3712]{1,0:T(8,128)(2,1)S(1)}, u32[]{:S(2)}, u32[]{:S(2)}) collective-permute-start(bf16[48,3712]{1,0:T(8,128)(2,1)S(1)} %collective-permute-done.17.refs_1_), channel_id=1, source_target_pairs={{0,1},{1,0},{2,3},{3,2},{4,5},{5,4},{6,7},{7,6},{8,9},{9,8},{10,11... | collective-permute-start | bytes 1069064 | tf_op jit(solution)/shard_map/ppermute | solution.py:47
  105.4 15.5 %collective-permute-start.18 = (bf16[48,3584]{1,0:T(8,128)(2,1)S(1)}, bf16[48,3584]{1,0:T(8,128)(2,1)S(1)}, u32[]{:S(2)}, u32[]{:S(2)}) collective-permute-start(bf16[48,3584]{1,0:T(8,128)(2,1)S(1)} %collective-permute-done.16.refs_0_), channel_id=1, source_target_pairs={{0,1},{1,0},{2,3},{3,2},{4,5},{5,4},{6,7},{7,6},{8,9},{9,8},{10,11... | collective-permute-start | bytes 1032200 | tf_op jit(solution)/shard_map/ppermute | solution.py:47
  113.6 29.3 %collective-permute-start.5 = (bf16[144,7168]{1,0:T(8,128)(2,1)S(1)}, bf16[144,7168]{1,0:T(8,128)(2,1)S(1)}, u32[]{:S(2)}, u32[]{:S(2)}) collective-permute-start(bf16[144,7168]{1,0:T(8,128)(2,1)S(1)} %get-tuple-element.15), channel_id=1, source_target_pairs={{0,1},{1,0},{2,3},{3,2},{4,5},{5,4},{6,7},{7,6},{8,9},{9,8},{10,11... | collective-permute-start | bytes 6193160 | tf_op jit(solution)/shard_map/ppermute | solution.py:47
  120.7 11.2 %collective-permute-start.10 = (bf16[96,7168]{1,0:T(8,128)(2,1)S(1)}, bf16[96,7168]{1,0:T(8,128)(2,1)S(1)}, u32[]{:S(2)}, u32[]{:S(2)}) collective-permute-start(bf16[96,7168]{1,0:T(8,128)(2,1)S(1)} %get-tuple-element.17), channel_id=1, source_target_pairs={{0,1},{1,0},{2,3},{3,2},{4,5},{5,4},{6,7},{7,6},{8,9},{9,8},{10,11... | collective-permute-start | bytes 4128776 | tf_op jit(solution)/shard_map/ppermute | solution.py:47
  125.8 2.4 %collective-permute-start.20 = (bf16[48,7168]{1,0:T(8,128)(2,1)S(1)}, bf16[48,7168]{1,0:T(8,128)(2,1)S(1)}, u32[]{:S(2)}, u32[]{:S(2)}) collective-permute-start(bf16[48,7168]{1,0:T(8,128)(2,1)S(1)} %get-tuple-element.21), channel_id=1, source_target_pairs={{0,1},{1,0},{2,3},{3,2},{4,5},{5,4},{6,7},{7,6},{8,9},{9,8},{10,11... | collective-permute-start | bytes 2064392 | tf_op jit(solution)/shard_map/ppermute | solution.py:47
  126.5 7.4 %collective-permute-start.24 = (bf16[48,3584]{1,0:T(8,128)(2,1)S(1)}, bf16[48,3584]{1,0:T(8,128)(2,1)S(1)}, u32[]{:S(2)}, u32[]{:S(2)}) collective-permute-start(bf16[48,3584]{1,0:T(8,128)(2,1)S(1)} %get-tuple-element.36), channel_id=1, source_target_pairs={{0,112},{1,15},{2,114},{3,5},{4,116},{5,3},{6,118},{7,9},{8,120},{... | collective-permute-start | bytes 1032200 | tf_op jit(solution)/shard_map/ppermute | solution.py:42
  127.9 7.2 %collective-permute-start.23 = (bf16[48,3584]{1,0:T(8,128)(2,1)S(1)}, bf16[48,3584]{1,0:T(8,128)(2,1)S(1)}, u32[]{:S(2)}, u32[]{:S(2)}) collective-permute-start(bf16[48,3584]{1,0:T(8,128)(2,1)S(1)} %get-tuple-element.37), channel_id=1, source_target_pairs={{0,16},{1,3},{2,18},{3,1},{4,20},{5,7},{6,22},{7,5},{8,24},{9,11},... | collective-permute-start | bytes 1032200 | tf_op jit(solution)/shard_map/ppermute | solution.py:38
  128.3 11.0 %collective-permute-start.22 = (bf16[48,3584]{1,0:T(8,128)(2,1)S(1)}, bf16[48,3584]{1,0:T(8,128)(2,1)S(1)}, u32[]{:S(2)}, u32[]{:S(2)}) collective-permute-start(bf16[48,3584]{1,0:T(8,128)(2,1)S(1)} %get-tuple-element.38), channel_id=1, source_target_pairs={{0,112},{1,15},{2,114},{3,5},{4,116},{5,3},{6,118},{7,9},{8,120},{... | collective-permute-start | bytes 1032200 | tf_op jit(solution)/shard_map/ppermute | solution.py:42
  131.9 7.4 %collective-permute-start.21 = (bf16[48,3584]{1,0:T(8,128)(2,1)S(1)}, bf16[48,3584]{1,0:T(8,128)(2,1)S(1)}, u32[]{:S(2)}, u32[]{:S(2)}) collective-permute-start(bf16[48,3584]{1,0:T(8,128)(2,1)S(1)} %get-tuple-element.39), channel_id=1, source_target_pairs={{0,16},{1,3},{2,18},{3,1},{4,20},{5,7},{6,22},{7,5},{8,24},{9,11},... | collective-permute-start | bytes 1032200 | tf_op jit(solution)/shard_map/ppermute | solution.py:38
  135.5 7.4 %collective-permute-start.28 = (bf16[48,3584]{1,0:T(8,128)(2,1)S(1)}, bf16[48,3584]{1,0:T(8,128)(2,1)S(1)}, u32[]{:S(2)}, u32[]{:S(2)}) collective-permute-start(bf16[48,3584]{1,0:T(8,128)(2,1)S(1)} %get-tuple-element.34), channel_id=1, source_target_pairs={{0,16},{1,3},{2,18},{3,1},{4,20},{5,7},{6,22},{7,5},{8,24},{9,11},... | collective-permute-start | bytes 1032200 | tf_op jit(solution)/shard_map/ppermute | solution.py:38
  135.6 8.9 %collective-permute-start.27 = (bf16[48,3584]{1,0:T(8,128)(2,1)S(1)}, bf16[48,3584]{1,0:T(8,128)(2,1)S(1)}, u32[]{:S(2)}, u32[]{:S(2)}) collective-permute-start(bf16[48,3584]{1,0:T(8,128)(2,1)S(1)} %get-tuple-element.35), channel_id=1, source_target_pairs={{0,112},{1,15},{2,114},{3,5},{4,116},{5,3},{6,118},{7,9},{8,120},{... | collective-permute-start | bytes 1032200 | tf_op jit(solution)/shard_map/ppermute | solution.py:42
  139.6 7.4 %collective-permute-start.26 = (bf16[48,3584]{1,0:T(8,128)(2,1)S(1)}, bf16[48,3584]{1,0:T(8,128)(2,1)S(1)}, u32[]{:S(2)}, u32[]{:S(2)}) collective-permute-start(bf16[48,3584]{1,0:T(8,128)(2,1)S(1)} %get-tuple-element.32), channel_id=1, source_target_pairs={{0,16},{1,3},{2,18},{3,1},{4,20},{5,7},{6,22},{7,5},{8,24},{9,11},... | collective-permute-start | bytes 1032200 | tf_op jit(solution)/shard_map/ppermute | solution.py:38
  139.7 8.5 %collective-permute-start.25 = (bf16[48,3584]{1,0:T(8,128)(2,1)S(1)}, bf16[48,3584]{1,0:T(8,128)(2,1)S(1)}, u32[]{:S(2)}, u32[]{:S(2)}) collective-permute-start(bf16[48,3584]{1,0:T(8,128)(2,1)S(1)} %get-tuple-element.33), channel_id=1, source_target_pairs={{0,112},{1,15},{2,114},{3,5},{4,116},{5,3},{6,118},{7,9},{8,120},{... | collective-permute-start | bytes 1032200 | tf_op jit(solution)/shard_map/ppermute | solution.py:42
  148.5 7.6 %collective-permute-start.33 = (bf16[48,3584]{1,0:T(8,128)(2,1)S(1)}, bf16[48,3584]{1,0:T(8,128)(2,1)S(1)}, u32[]{:S(2)}, u32[]{:S(2)}) collective-permute-start(bf16[48,3584]{1,0:T(8,128)(2,1)S(1)} %get-tuple-element.30), channel_id=1, source_target_pairs={{0,112},{1,15},{2,114},{3,5},{4,116},{5,3},{6,118},{7,9},{8,120},{... | collective-permute-start | bytes 1032200 | tf_op jit(solution)/shard_map/ppermute | solution.py:42
  150.9 7.2 %collective-permute-start.29 = (bf16[48,3584]{1,0:T(8,128)(2,1)S(1)}, bf16[48,3584]{1,0:T(8,128)(2,1)S(1)}, u32[]{:S(2)}, u32[]{:S(2)}) collective-permute-start(bf16[48,3584]{1,0:T(8,128)(2,1)S(1)} %get-tuple-element.31), channel_id=1, source_target_pairs={{0,16},{1,3},{2,18},{3,1},{4,20},{5,7},{6,22},{7,5},{8,24},{9,11},... | collective-permute-start | bytes 1032200 | tf_op jit(solution)/shard_map/ppermute | solution.py:38
  152.4 9.2 %collective-permute-start.31 = (bf16[48,3584]{1,0:T(8,128)(2,1)S(1)}, bf16[48,3584]{1,0:T(8,128)(2,1)S(1)}, u32[]{:S(2)}, u32[]{:S(2)}) collective-permute-start(bf16[48,3584]{1,0:T(8,128)(2,1)S(1)} %get-tuple-element.28), channel_id=1, source_target_pairs={{0,112},{1,15},{2,114},{3,5},{4,116},{5,3},{6,118},{7,9},{8,120},{... | collective-permute-start | bytes 1032200 | tf_op jit(solution)/shard_map/ppermute | solution.py:42
  153.8 8.0 %collective-permute-start.32 = (bf16[48,3584]{1,0:T(8,128)(2,1)S(1)}, bf16[48,3584]{1,0:T(8,128)(2,1)S(1)}, u32[]{:S(2)}, u32[]{:S(2)}) collective-permute-start(bf16[48,3584]{1,0:T(8,128)(2,1)S(1)} %get-tuple-element.29), channel_id=1, source_target_pairs={{0,16},{1,3},{2,18},{3,1},{4,20},{5,7},{6,22},{7,5},{8,24},{9,11},... | collective-permute-start | bytes 1032200 | tf_op jit(solution)/shard_map/ppermute | solution.py:38
  158.4 7.4 %collective-permute-start.34 = (bf16[48,3584]{1,0:T(8,128)(2,1)S(1)}, bf16[48,3584]{1,0:T(8,128)(2,1)S(1)}, u32[]{:S(2)}, u32[]{:S(2)}) collective-permute-start(bf16[48,3584]{1,0:T(8,128)(2,1)S(1)} %get-tuple-element.26), channel_id=1, source_target_pairs={{0,16},{1,3},{2,18},{3,1},{4,20},{5,7},{6,22},{7,5},{8,24},{9,11},... | collective-permute-start | bytes 1032200 | tf_op jit(solution)/shard_map/ppermute | solution.py:38
  160.1 7.2 %collective-permute-start.30 = (bf16[48,3584]{1,0:T(8,128)(2,1)S(1)}, bf16[48,3584]{1,0:T(8,128)(2,1)S(1)}, u32[]{:S(2)}, u32[]{:S(2)}) collective-permute-start(bf16[48,3584]{1,0:T(8,128)(2,1)S(1)} %get-tuple-element.27), channel_id=1, source_target_pairs={{0,112},{1,15},{2,114},{3,5},{4,116},{5,3},{6,118},{7,9},{8,120},{... | collective-permute-start | bytes 1032200 | tf_op jit(solution)/shard_map/ppermute | solution.py:42
  168.2 17.8 %copy-start.19 = (bf16[4,7168]{1,0:T(4,128)(2,1)S(1)}, bf16[4,7168]{1,0:T(4,128)(2,1)}, u32[]{:S(2)}) copy-start(bf16[4,7168]{1,0:T(4,128)(2,1)} %b_ref.1) | copy-start | bytes 172036
  168.2 17.8 %copy-start.20 = (bf16[2,7168]{1,0:T(2,128)(2,1)S(1)}, bf16[2,7168]{1,0:T(2,128)(2,1)}, u32[]{:S(2)}) copy-start(bf16[2,7168]{1,0:T(2,128)(2,1)} %a_ref.1) | copy-start | bytes 86020

commit v5 on v4

--- a/solution.py
+++ b/solution.py
@@ -51,7 +51,7 @@
     return values * lax.rsqrt(jnp.mean(values * values, axis=-1, keepdims=True) + 1e-06) * gain_vec
 
 
-GROUPS = ((0, 1, -1), (2, -2), (3, -3), (4,))
+GROUPS = ((0, 1, -1), (2, -2, 3, -3), (4,))
 
 
 def stage_1_groups():
@@ -68,11 +68,16 @@
 
 def gather_ring(block, cut):
     slots = {0: block}
-    for k in (1, 2, 3):
+    for k in (1, 2):
         slots[k] = over_even(slots[1 - k])
         slots[-k] = over_odd(slots[k - 1])
-    low = over_even(slots[-3][:, :cut])
-    high = over_odd(slots[3][:, cut:])
+    even_high = over_even(slots[-2][:, cut:])
+    odd_low = over_odd(slots[2][:, :cut])
+    even_low = over_even(slots[-2][:, :cut])
+    odd_high = over_odd(slots[2][:, cut:])
+    slots[3], slots[-3] = (even_low, even_high), (odd_low, odd_high)
+    low = over_even(odd_low)
+    high = over_odd(even_high)
     slots[4] = (low, high)
     return slots
 

time: 188 us -> 184 us (0.979)
  Pallas kernels: 30.3 us -> 26.2 us
  waiting for transfers between devices: 42.4 us -> 38.8 us
  starting transfers between devices: 52.3 us -> 54.4 us
    ppermute x11 -> x12, waiting for transfers between devices: 28 us -> 13.4 us  [over_odd(): return lax.ppermute(array, EXP, pairs_along(2, odd_partner))]
    ppermute x11 -> x12, waiting for transfers between devices: 14.1 us -> 23.9 us  [over_even(): return lax.ppermute(array, EXP, pairs_along(2, even_partner))]
    pallas_call x4 -> x3, Pallas kernels: 25.9 us -> 21.8 us  [layers(): pl.pallas_call(body, in_specs=[hbm_spec] * n_blocks + [vmem_spec] * 7, ou...]
    ppermute x11 -> x12, starting transfers between devices: 11.2 us -> 13.4 us  [over_even(): return lax.ppermute(array, EXP, pairs_along(2, even_partner))]
    unnamed x42 -> x46, local copies, waits for them, and re-layouts: 11.5 us -> 13.1 us
    ppermute x11 -> x12, starting transfers between devices: 37.6 us -> 38.3 us  [over_odd(): return lax.ppermute(array, EXP, pairs_along(2, odd_partner))]
  transfers between devices with their start and end apart: 35 -> 38, of which waited for: 16 -> 16; matrix products, arithmetic and copies ran while one was open for 1% -> 1% of each run, Pallas kernels for 14% -> 7%
where the time goes in v5:
time: 184 us; the launch traced here: 182 us
  starting transfers between devices  54.4 us (30%)
  blocking collectives  46.4 us (25%)
  waiting for transfers between devices  38.8 us (21%)
  Pallas kernels  26.2 us (14%)
  local copies, waits for them, and re-layouts  13.3 us (7%)
  other arithmetic  1.9 us (1%)
    all_to_all x2, blocking collectives, exchange(): lax.all_to_all(blocks, EXP, split_axis=0, concat_axis=0, tiled=True, axis...  46.4 us
    ppermute x12, starting transfers between devices, over_odd(): return lax.ppermute(array, EXP, pairs_along(2, odd_partner))  38.3 us
    ppermute x12, waiting for transfers between devices, over_even(): return lax.ppermute(array, EXP, pairs_along(2, even_partner))  23.9 us
    pallas_call x3, Pallas kernels, layers(): pl.pallas_call(body, in_specs=[hbm_spec] * n_blocks + [vmem_spec] * 7, ou...  21.8 us
    ppermute x12, starting transfers between devices, over_even(): return lax.ppermute(array, EXP, pairs_along(2, even_partner))  13.4 us
    ppermute x12, waiting for transfers between devices, over_odd(): return lax.ppermute(array, EXP, pairs_along(2, odd_partner))  13.4 us
    unnamed x46, local copies, waits for them, and re-layouts  13.1 us
  transfers between devices with their start and end apart: 38, of which 16 were waited for; matrix products, arithmetic and copies ran while one was open for 1% of the time, Pallas kernels for 7%

profile of v5, /device:TPU:516, one launch (start us, length us, event | category | flops | bytes accessed | tf_op | source)
XLA Modules:
  0.0 181.9 jit_solution(8740245393401062888)
XLA Ops:
  0.6 2.1 %prepare.1 = bf16[8,352,128]{2,1,0:T(8,128)(2,1)} custom-call(bf16[2,7168]{1,0:T(2,128)(2,1)} %a_ref.1, f32[1,7168]{1,0:T(1,128)} %bitcast.27, bf16[4,7168]{1,0:T(4,128)(2,1)} %b_ref.1, f32[1,7168]{1,0:T(1,128)} %bitcast.28, s32[4,8]{1,0:T(4,128)} %refs_4_.1, f32[4,8]{1,0:T(4,128)} %refs_5_.1), custom_call_target="tpu_custom_call" | custom-call | tf_op jit(solution)/shard_map/prepare/pallas_call | solution.py:279
  2.8 28.7 %all_to_all.10.near_ref = bf16[8,352,128]{2,1,0:T(8,128)(2,1)S(1)} all-to-all(bf16[8,352,128]{2,1,0:T(8,128)(2,1)} %prepare.1), channel_id=1, replica_groups={{0,2,4,6,8,10,12,14},{16,18,20,22,24,26,28,30},{32,34,36,38,40,42,44,46..., dimensions={0} | all-to-all | bytes 1441792 | tf_op jit(solution)/shard_map/all_to_all | solution.py:64
  31.5 0.5 pack.1.refs_0_
  32.0 0.5 collective-permute-start.1
  32.5 4.1 %collective-permute-start = (bf16[48,7296]{1,0:T(8,128)(2,1)S(1)}, bf16[48,7296]{1,0:T(8,128)(2,1)S(1)}, u32[]{:S(2)}, u32[]{:S(2)}) collective-permute-start(bf16[48,7296]{1,0:T(8,128)(2,1)S(1)} %pack.1.refs_0_), channel_id=1, source_target_pairs={{0,16},{1,3},{2,18},{3,1},{4,20},{5,7},{6,22},{7,5},{8,24},{9,11},... | collective-permute-start | bytes 2101256 | tf_op jit(solution)/shard_map/ppermute | solution.py:38
  36.6 6.6 %collective-permute-done.1.refs_2_ = bf16[48,7296]{1,0:T(8,128)(2,1)S(1)} collective-permute-done((bf16[48,7296]{1,0:T(8,128)(2,1)S(1)}, bf16[48,7296]{1,0:T(8,128)(2,1)S(1)}, u32[]{:S(2)}, u32[]{:S(2)}) %collective-permute-start.1) | collective-permute-done | bytes 700448 | tf_op jit(solution)/shard_map/ppermute | solution.py:42
  43.2 2.8 %collective-permute-start.6 = (bf16[48,7296]{1,0:T(8,128)(2,1)S(1)}, bf16[48,7296]{1,0:T(8,128)(2,1)S(1)}, u32[]{:S(2)}, u32[]{:S(2)}) collective-permute-start(bf16[48,7296]{1,0:T(8,128)(2,1)S(1)} %collective-permute-done.1.refs_2_), channel_id=1, source_target_pairs={{0,16},{1,3},{2,18},{3,1},{4,20},{5,7},{6,22},{7,5},{8,24},{9,11},... | collective-permute-start | bytes 2101256 | tf_op jit(solution)/shard_map/ppermute | solution.py:38
  46.0 9.1 %collective-permute-start.7 = (bf16[48,7296]{1,0:T(8,128)(2,1)S(1)}, bf16[48,7296]{1,0:T(8,128)(2,1)S(1)}, u32[]{:S(2)}, u32[]{:S(2)}) collective-permute-start(bf16[48,7296]{1,0:T(8,128)(2,1)S(1)} %collective-permute-done.refs_1_), channel_id=1, source_target_pairs={{0,112},{1,15},{2,114},{3,5},{4,116},{5,3},{6,118},{7,9},{8,120},{... | collective-permute-start | bytes 2101256 | tf_op jit(solution)/shard_map/ppermute | solution.py:42
  55.2 9.0 %collective-permute-start.10 = (bf16[48,3584]{1,0:T(8,128)(2,1)S(1)}, bf16[48,3584]{1,0:T(8,128)(2,1)S(1)}, u32[]{:S(2)}, u32[]{:S(2)}) collective-permute-start(bf16[48,3584]{1,0:T(8,128)(2,1)S(1)} %slice.176), channel_id=1, source_target_pairs={{0,112},{1,15},{2,114},{3,5},{4,116},{5,3},{6,118},{7,9},{8,120},{... | collective-permute-start | bytes 1032200 | tf_op jit(solution)/shard_map/ppermute | solution.py:42
  64.4 3.3 %collective-permute-start.11 = (bf16[48,3712]{1,0:T(8,128)(2,1)S(1)}, bf16[48,3712]{1,0:T(8,128)(2,1)}, u32[]{:S(2)}, u32[]{:S(2)}) collective-permute-start(bf16[48,3712]{1,0:T(8,128)(2,1)S(1)} %slice.177), channel_id=1, source_target_pairs={{0,112},{1,15},{2,114},{3,5},{4,116},{5,3},{6,118},{7,9},{8,120},{... | collective-permute-start | bytes 1069064 | tf_op jit(solution)/shard_map/ppermute | solution.py:42
  68.1 1.4 collective-permute-done.10.refs_4_
  69.4 2.3 %collective-permute-done.8.refs_2_ = bf16[48,3584]{1,0:T(8,128)(2,1)} collective-permute-done((bf16[48,3584]{1,0:T(8,128)(2,1)S(1)}, bf16[48,3584]{1,0:T(8,128)(2,1)}, u32[]{:S(2)}, u32[]{:S(2)}) %collective-permute-start.8) | collective-permute-done | bytes 344096 | tf_op jit(solution)/shard_map/ppermute | solution.py:38
  71.7 0.7 copy-done.17
  72.5 0.9 collective-permute-done.11.refs_5_
  73.4 2.2 %collective-permute-done.9.refs_3_ = bf16[48,3712]{1,0:T(8,128)(2,1)} collective-permute-done((bf16[48,3712]{1,0:T(8,128)(2,1)S(1)}, bf16[48,3712]{1,0:T(8,128)(2,1)}, u32[]{:S(2)}, u32[]{:S(2)}) %collective-permute-start.9) | collective-permute-done | bytes 356384 | tf_op jit(solution)/shard_map/ppermute | solution.py:38
  75.5 0.7 copy-done.19
  76.3 0.5 collective-permute-start.14
  76.8 1.6 copy-done.1
  78.4 1.6 copy-done.3
  80.0 1.5 copy-done.5
  81.5 1.5 copy-done.7
  83.0 1.5 copy-done.9
  84.6 1.4 copy-done.2
  86.0 0.6 copy-done.4
  86.7 0.5 copy-done.6
  87.2 0.5 copy-done.8
  87.7 0.5 copy-done.10
  88.5 8.8 %shard_map.132 = (bf16[192,7168]{1,0:T(8,128)(2,1)S(1)}, bf16[192,7168]{1,0:T(8,128)(2,1)S(1)}) custom-call(bf16[48,7296]{1,0:T(8,128)(2,1)S(1)} %collective-permute-done.6.refs_0_, bf16[48,7296]{1,0:T(8,128)(2,1)S(1)} %collective-permute-done.7.refs_1_, bf16[48,3584]{1,0:T(8,128)(2,1)} %collective-permute-done.8.refs_2_, ...), custom_call_target="tpu_custom_call" | custom-call | flops 2202009600 | bytes 22708224 | tf_op jit(solution)/shard_map/pallas_call | solution.py:212
  97.4 2.3 %collective-permute-start.20 = (bf16[48,3712]{1,0:T(8,128)(2,1)}, bf16[48,3712]{1,0:T(8,128)(2,1)S(1)}, u32[]{:S(2)}, u32[]{:S(2)}) collective-permute-start(bf16[48,3712]{1,0:T(8,128)(2,1)} %collective-permute-done.9.refs_3_), channel_id=1, source_target_pairs={{0,112},{1,15},{2,114},{3,5},{4,116},{5,3},{6,118},{7,9},{8,120},{... | collective-permute-start | bytes 1069064 | tf_op jit(solution)/shard_map/ppermute | solution.py:42
  99.7 0.5 collective-permute-start.4
  100.2 6.7 %collective-permute-done.19.refs_0_ = bf16[48,3584]{1,0:T(8,128)(2,1)S(1)} collective-permute-done((bf16[48,3584]{1,0:T(8,128)(2,1)S(1)}, bf16[48,3584]{1,0:T(8,128)(2,1)S(1)}, u32[]{:S(2)}, u32[]{:S(2)}) %collective-permute-start.19) | collective-permute-done | bytes 344096 | tf_op jit(solution)/shard_map/ppermute | solution.py:38
  107.0 0.5 collective-permute-start.21
  107.7 1.4 collective-permute-start.27
  109.1 8.1 %shard_map.131 = (bf16[144,7168]{1,0:T(8,128)(2,1)S(1)}, bf16[144,7168]{1,0:T(8,128)(2,1)S(1)}) custom-call(bf16[48,7296]{1,0:T(8,128)(2,1)S(1)} %copy-done.12, bf16[48,7296]{1,0:T(8,128)(2,1)S(1)} %copy-done.16, bf16[48,7296]{1,0:T(8,128)(2,1)S(1)} %copy-done.14, bf16[48,7296]{1,0:T(8,128)(2,1)S(1)} %collective-permute-done.2.refs_3_, ...), custom_call_target="tpu_custom_call" | custom-call | flops 1651507200 | bytes 19955712 | tf_op jit(solution)/shard_map/pallas_call | solution.py:212
  117.3 0.3 collective-permute-start.5
  117.6 4.9 %shard_map.133 = (bf16[48,7168]{1,0:T(8,128)(2,1)S(1)}, bf16[48,7168]{1,0:T(8,128)(2,1)S(1)}) custom-call(bf16[48,3584]{1,0:T(8,128)(2,1)S(1)} %collective-permute-done.19.refs_0_, bf16[48,3712]{1,0:T(8,128)(2,1)S(1)} %collective-permute-done.20.refs_1_, bf16[48,3584]{1,0:T(8,128)(2,1)S(1)} %collective-permute-done.21.refs_2_, ...), custom_call_target="tpu_custom_call" | custom-call | flops 550502400 | bytes 14450688 | tf_op jit(solution)/shard_map/pallas_call | solution.py:212
  122.5 0.5 collective-permute-start.23
  123.0 0.2 add_convert_fusion.8
  123.4 1.4 collective-permute-done.23
  124.9 2.1 %collective-permute-start.25 = (bf16[48,3584]{1,0:T(8,128)(2,1)S(1)}, bf16[48,3584]{1,0:T(8,128)(2,1)S(1)}, u32[]{:S(2)}, u32[]{:S(2)}) collective-permute-start(bf16[48,3584]{1,0:T(8,128)(2,1)S(1)} %get-tuple-element.32), channel_id=1, source_target_pairs={{0,112},{1,15},{2,114},{3,5},{4,116},{5,3},{6,118},{7,9},{8,120},{... | collective-permute-start | bytes 1032200 | tf_op jit(solution)/shard_map/ppermute | solution.py:42
  127.0 2.0 %collective-permute-start.31 = (bf16[48,3584]{1,0:T(8,128)(2,1)S(1)}, bf16[48,3584]{1,0:T(8,128)(2,1)S(1)}, u32[]{:S(2)}, u32[]{:S(2)}) collective-permute-start(bf16[48,3584]{1,0:T(8,128)(2,1)S(1)} %get-tuple-element.26), channel_id=1, source_target_pairs={{0,16},{1,3},{2,18},{3,1},{4,20},{5,7},{6,22},{7,5},{8,24},{9,11},... | collective-permute-start | bytes 1032200 | tf_op jit(solution)/shard_map/ppermute | solution.py:38
  129.1 1.5 collective-permute-done.26
  130.7 1.5 collective-permute-start.30
  132.3 2.0 %collective-permute-done.24 = bf16[48,3584]{1,0:T(8,128)(2,1)S(1)} collective-permute-done((bf16[48,3584]{1,0:T(8,128)(2,1)S(1)}, bf16[48,3584]{1,0:T(8,128)(2,1)S(1)}, u32[]{:S(2)}, u32[]{:S(2)}) %collective-permute-start.24) | collective-permute-done | bytes 344096 | tf_op jit(solution)/shard_map/ppermute | solution.py:38
  134.3 0.3 add_convert_fusion.6
  134.8 3.4 %collective-permute-start.28 = (bf16[48,3584]{1,0:T(8,128)(2,1)S(1)}, bf16[48,3584]{1,0:T(8,128)(2,1)S(1)}, u32[]{:S(2)}, u32[]{:S(2)}) collective-permute-start(bf16[48,3584]{1,0:T(8,128)(2,1)S(1)} %get-tuple-element.25), channel_id=1, source_target_pairs={{0,112},{1,15},{2,114},{3,5},{4,116},{5,3},{6,118},{7,9},{8,120},{... | collective-permute-start | bytes 1032200 | tf_op jit(solution)/shard_map/ppermute | solution.py:42
  138.1 0.3 add_convert_fusion.4
  138.4 3.5 %collective-permute-done.29 = bf16[48,3584]{1,0:T(8,128)(2,1)S(1)} collective-permute-done((bf16[48,3584]{1,0:T(8,128)(2,1)S(1)}, bf16[48,3584]{1,0:T(8,128)(2,1)S(1)}, u32[]{:S(2)}, u32[]{:S(2)}) %collective-permute-start.29) | collective-permute-done | bytes 344096 | tf_op jit(solution)/shard_map/ppermute | solution.py:38
  142.0 1.4 collective-permute-done.28
  143.4 0.3 add_convert_fusion.1
  143.7 2.1 %collective-permute-start.36 = (bf16[48,3584]{1,0:T(8,128)(2,1)S(1)}, bf16[48,3584]{1,0:T(8,128)(2,1)S(1)}, u32[]{:S(2)}, u32[]{:S(2)}) collective-permute-start(bf16[48,3584]{1,0:T(8,128)(2,1)S(1)} %get-tuple-element.22), channel_id=1, source_target_pairs={{0,112},{1,15},{2,114},{3,5},{4,116},{5,3},{6,118},{7,9},{8,120},{... | collective-permute-start | bytes 1032200 | tf_op jit(solution)/shard_map/ppermute | solution.py:42
  145.8 1.7 collective-permute-start.32
  147.5 1.7 collective-permute-start.34
  149.2 0.4 collective-permute-start.35
  149.7 1.4 collective-permute-done.36
  151.1 2.0 %collective-permute-done.32 = bf16[48,3584]{1,0:T(8,128)(2,1)S(1)} collective-permute-done((bf16[48,3584]{1,0:T(8,128)(2,1)S(1)}, bf16[48,3584]{1,0:T(8,128)(2,1)S(1)}, u32[]{:S(2)}, u32[]{:S(2)}) %collective-permute-start.32) | collective-permute-done | bytes 344096 | tf_op jit(solution)/shard_map/ppermute | solution.py:38
  153.1 0.3 add_convert_fusion
  153.4 1.8 collective-permute-start.37
  155.2 1.7 collective-permute-start.33
  157.1 3.7 %collective-permute-done.37.refs_5_ = bf16[48,3584]{1,0:T(8,128)(2,1)S(1)} collective-permute-done((bf16[48,3584]{1,0:T(8,128)(2,1)S(1)}, bf16[48,3584]{1,0:T(8,128)(2,1)S(1)}, u32[]{:S(2)}, u32[]{:S(2)}) %collective-permute-start.37) | collective-permute-done | bytes 344096 | tf_op jit(solution)/shard_map/ppermute | solution.py:38
  160.8 1.7 collective-permute-done.33.refs_2_
  162.4 0.9 unpack.1
  163.3 17.7 %all_to_all.11.piece_ref = bf16[8,336,128]{2,1,0:T(8,128)(2,1)S(1)} all-to-all(bf16[8,336,128]{2,1,0:T(8,128)(2,1)S(1)} %unpack.1), channel_id=1, replica_groups={{0,2,4,6,8,10,12,14},{16,18,20,22,24,26,28,30},{32,34,36,38,40,42,44,46..., dimensions={0} | all-to-all | bytes 1376256 | tf_op jit(solution)/shard_map/all_to_all | solution.py:64
  181.1 0.9 finish.1
  (83 shorter events, 2.0 us)
Async XLA Ops:
  2.8 74.0 %copy-start = (bf16[7168,144]{0,1:T(8,128)(2,1)S(1)}, bf16[7168,144]{0,1:T(8,128)(2,1)}, u32[]{:S(2)}) copy-start(bf16[7168,144]{0,1:T(8,128)(2,1)} %param.14) | copy-start | bytes 6193156
  32.0 14.0 %copy-start.11 = (bf16[48,7296]{1,0:T(8,128)(2,1)}, bf16[48,7296]{1,0:T(8,128)(2,1)S(1)}, u32[]{:S(2)}) copy-start(bf16[48,7296]{1,0:T(8,128)(2,1)S(1)} %pack.1.refs_0_) | copy-start | bytes 2101252
  32.0 11.2 %collective-permute-start.1 = (bf16[48,7296]{1,0:T(8,128)(2,1)S(1)}, bf16[48,7296]{1,0:T(8,128)(2,1)S(1)}, u32[]{:S(2)}, u32[]{:S(2)}) collective-permute-start(bf16[48,7296]{1,0:T(8,128)(2,1)S(1)} %pack.1.refs_0_), channel_id=1, source_target_pairs={{0,112},{1,15},{2,114},{3,5},{4,116},{5,3},{6,118},{7,9},{8,120},{... | collective-permute-start | bytes 2101256 | tf_op jit(solution)/shard_map/ppermute | solution.py:42
  32.5 13.5 %collective-permute-start = (bf16[48,7296]{1,0:T(8,128)(2,1)S(1)}, bf16[48,7296]{1,0:T(8,128)(2,1)S(1)}, u32[]{:S(2)}, u32[]{:S(2)}) collective-permute-start(bf16[48,7296]{1,0:T(8,128)(2,1)S(1)} %pack.1.refs_0_), channel_id=1, source_target_pairs={{0,16},{1,3},{2,18},{3,1},{4,20},{5,7},{6,22},{7,5},{8,24},{9,11},... | collective-permute-start | bytes 2101256 | tf_op jit(solution)/shard_map/ppermute | solution.py:38
  43.2 11.9 %copy-start.13 = (bf16[48,7296]{1,0:T(8,128)(2,1)}, bf16[48,7296]{1,0:T(8,128)(2,1)S(1)}, u32[]{:S(2)}) copy-start(bf16[48,7296]{1,0:T(8,128)(2,1)S(1)} %collective-permute-done.1.refs_2_) | copy-start | bytes 2101252
  43.2 11.9 %collective-permute-start.6 = (bf16[48,7296]{1,0:T(8,128)(2,1)S(1)}, bf16[48,7296]{1,0:T(8,128)(2,1)S(1)}, u32[]{:S(2)}, u32[]{:S(2)}) collective-permute-start(bf16[48,7296]{1,0:T(8,128)(2,1)S(1)} %collective-permute-done.1.refs_2_), channel_id=1, source_target_pairs={{0,16},{1,3},{2,18},{3,1},{4,20},{5,7},{6,22},{7,5},{8,24},{9,11},... | collective-permute-start | bytes 2101256 | tf_op jit(solution)/shard_map/ppermute | solution.py:38
  46.0 22.0 %copy-start.15 = (bf16[48,7296]{1,0:T(8,128)(2,1)}, bf16[48,7296]{1,0:T(8,128)(2,1)S(1)}, u32[]{:S(2)}) copy-start(bf16[48,7296]{1,0:T(8,128)(2,1)S(1)} %collective-permute-done.refs_1_) | copy-start | bytes 2101252
  46.0 18.2 %collective-permute-start.7 = (bf16[48,7296]{1,0:T(8,128)(2,1)S(1)}, bf16[48,7296]{1,0:T(8,128)(2,1)S(1)}, u32[]{:S(2)}, u32[]{:S(2)}) collective-permute-start(bf16[48,7296]{1,0:T(8,128)(2,1)S(1)} %collective-permute-done.refs_1_), channel_id=1, source_target_pairs={{0,112},{1,15},{2,114},{3,5},{4,116},{5,3},{6,118},{7,9},{8,120},{... | collective-permute-start | bytes 2101256 | tf_op jit(solution)/shard_map/ppermute | solution.py:42
  55.2 14.3 %collective-permute-start.10 = (bf16[48,3584]{1,0:T(8,128)(2,1)S(1)}, bf16[48,3584]{1,0:T(8,128)(2,1)S(1)}, u32[]{:S(2)}, u32[]{:S(2)}) collective-permute-start(bf16[48,3584]{1,0:T(8,128)(2,1)S(1)} %slice.176), channel_id=1, source_target_pairs={{0,112},{1,15},{2,114},{3,5},{4,116},{5,3},{6,118},{7,9},{8,120},{... | collective-permute-start | bytes 1032200 | tf_op jit(solution)/shard_map/ppermute | solution.py:42
  64.2 7.5 %collective-permute-start.8 = (bf16[48,3584]{1,0:T(8,128)(2,1)S(1)}, bf16[48,3584]{1,0:T(8,128)(2,1)}, u32[]{:S(2)}, u32[]{:S(2)}) collective-permute-start(bf16[48,3584]{1,0:T(8,128)(2,1)S(1)} %slice.174), channel_id=1, source_target_pairs={{0,16},{1,3},{2,18},{3,1},{4,20},{5,7},{6,22},{7,5},{8,24},{9,11},... | collective-permute-start | bytes 1032200 | tf_op jit(solution)/shard_map/ppermute | solution.py:38
  64.4 9.0 %collective-permute-start.11 = (bf16[48,3712]{1,0:T(8,128)(2,1)S(1)}, bf16[48,3712]{1,0:T(8,128)(2,1)}, u32[]{:S(2)}, u32[]{:S(2)}) collective-permute-start(bf16[48,3712]{1,0:T(8,128)(2,1)S(1)} %slice.177), channel_id=1, source_target_pairs={{0,112},{1,15},{2,114},{3,5},{4,116},{5,3},{6,118},{7,9},{8,120},{... | collective-permute-start | bytes 1069064 | tf_op jit(solution)/shard_map/ppermute | solution.py:42
  67.8 7.8 %collective-permute-start.9 = (bf16[48,3712]{1,0:T(8,128)(2,1)S(1)}, bf16[48,3712]{1,0:T(8,128)(2,1)}, u32[]{:S(2)}, u32[]{:S(2)}) collective-permute-start(bf16[48,3712]{1,0:T(8,128)(2,1)S(1)} %slice.175), channel_id=1, source_target_pairs={{0,16},{1,3},{2,18},{3,1},{4,20},{5,7},{6,22},{7,5},{8,24},{9,11},... | collective-permute-start | bytes 1069064 | tf_op jit(solution)/shard_map/ppermute | solution.py:38
  67.9 16.6 %collective-permute-start.12 = (bf16[48,7296]{1,0:T(8,128)(2,1)S(1)}, bf16[48,7296]{1,0:T(8,128)(2,1)}, u32[]{:S(2)}, u32[]{:S(2)}) collective-permute-start(bf16[48,7296]{1,0:T(8,128)(2,1)S(1)} %collective-permute-done.6.refs_0_), channel_id=1, source_target_pairs={{0,1},{1,0},{2,3},{3,2},{4,5},{5,4},{6,7},{7,6},{8,9},{9,8},{10,11... | collective-permute-start | bytes 2101256 | tf_op jit(solution)/shard_map/ppermute | solution.py:47
  69.4 15.1 %collective-permute-start.13 = (bf16[48,7296]{1,0:T(8,128)(2,1)S(1)}, bf16[48,7296]{1,0:T(8,128)(2,1)}, u32[]{:S(2)}, u32[]{:S(2)}) collective-permute-start(bf16[48,7296]{1,0:T(8,128)(2,1)S(1)} %collective-permute-done.7.refs_1_), channel_id=1, source_target_pairs={{0,1},{1,0},{2,3},{3,2},{4,5},{5,4},{6,7},{7,6},{8,9},{9,8},{10,11... | collective-permute-start | bytes 2101256 | tf_op jit(solution)/shard_map/ppermute | solution.py:47
  71.7 3.8 %collective-permute-start.16 = (bf16[48,3584]{1,0:T(8,128)(2,1)S(1)}, bf16[48,3584]{1,0:T(8,128)(2,1)S(1)}, u32[]{:S(2)}, u32[]{:S(2)}) collective-permute-start(bf16[48,3584]{1,0:T(8,128)(2,1)S(1)} %collective-permute-done.10.refs_4_), channel_id=1, source_target_pairs={{0,1},{1,0},{2,3},{3,2},{4,5},{5,4},{6,7},{7,6},{8,9},{9,8},{10,11... | collective-permute-start | bytes 1032200 | tf_op jit(solution)/shard_map/ppermute | solution.py:47
  71.7 0.7 copy-start.17
  73.4 11.2 %collective-permute-start.17 = (bf16[48,3712]{1,0:T(8,128)(2,1)}, bf16[48,3712]{1,0:T(8,128)(2,1)}, u32[]{:S(2)}, u32[]{:S(2)}) collective-permute-start(bf16[48,3712]{1,0:T(8,128)(2,1)} %collective-permute-done.11.refs_5_), channel_id=1, source_target_pairs={{0,1},{1,0},{2,3},{3,2},{4,5},{5,4},{6,7},{7,6},{8,9},{9,8},{10,11... | collective-permute-start | bytes 1069064 | tf_op jit(solution)/shard_map/ppermute | solution.py:47
  75.5 9.1 %collective-permute-start.15 = (bf16[48,3712]{1,0:T(8,128)(2,1)}, bf16[48,3712]{1,0:T(8,128)(2,1)}, u32[]{:S(2)}, u32[]{:S(2)}) collective-permute-start(bf16[48,3712]{1,0:T(8,128)(2,1)} %collective-permute-done.9.refs_3_), channel_id=1, source_target_pairs={{0,1},{1,0},{2,3},{3,2},{4,5},{5,4},{6,7},{7,6},{8,9},{9,8},{10,11... | collective-permute-start | bytes 1069064 | tf_op jit(solution)/shard_map/ppermute | solution.py:47
  75.5 0.8 copy-start.19
  76.3 8.3 %collective-permute-start.14 = (bf16[48,3584]{1,0:T(8,128)(2,1)}, bf16[48,3584]{1,0:T(8,128)(2,1)}, u32[]{:S(2)}, u32[]{:S(2)}) collective-permute-start(bf16[48,3584]{1,0:T(8,128)(2,1)} %collective-permute-done.8.refs_2_), channel_id=1, source_target_pairs={{0,1},{1,0},{2,3},{3,2},{4,5},{5,4},{6,7},{7,6},{8,9},{9,8},{10,11... | collective-permute-start | bytes 1032200 | tf_op jit(solution)/shard_map/ppermute | solution.py:47
  76.8 1.6 copy-start.1
  78.4 1.6 copy-start.3
  80.0 1.5 copy-start.5
  81.5 1.5 copy-start.7
  83.0 1.5 copy-start.9
  84.5 1.6 copy-start.2
  84.5 2.2 %copy-start.4 = (bf16[144,7168]{1,0:T(8,128)(2,1)S(1)}, bf16[144,7168]{1,0:T(8,128)(2,1)}, u32[]{:S(2)}) copy-start(bf16[144,7168]{1,0:T(8,128)(2,1)} %refs_6_.1) | copy-start | bytes 6193156
  84.5 2.7 %copy-start.6 = (bf16[1,7168,128]{2,1,0:T(8,128)(2,1)S(1)}, bf16[1,7168,128]{2,1,0:T(8,128)(2,1)}, u32[]{:S(2)}) copy-start(bf16[1,7168,128]{2,1,0:T(8,128)(2,1)} %param.21) | copy-start | bytes 5505028
  84.5 3.3 %copy-start.8 = (bf16[1,7168,128]{2,1,0:T(8,128)(2,1)S(1)}, bf16[1,7168,128]{2,1,0:T(8,128)(2,1)}, u32[]{:S(2)}) copy-start(bf16[1,7168,128]{2,1,0:T(8,128)(2,1)} %param.22) | copy-start | bytes 5505028
  84.5 3.8 %copy-start.10 = (bf16[1,128,7168]{2,1,0:T(8,128)(2,1)S(1)}, bf16[1,128,7168]{2,1,0:T(8,128)(2,1)}, u32[]{:S(2)}) copy-start(bf16[1,128,7168]{2,1,0:T(8,128)(2,1)} %param.23) | copy-start | bytes 5505028
  84.5 3.9 %copy-start.18 = (bf16[48,3584]{1,0:T(8,128)(2,1)S(1)}, bf16[48,3584]{1,0:T(8,128)(2,1)}, u32[]{:S(2)}) copy-start(bf16[48,3584]{1,0:T(8,128)(2,1)} %copy-done.17) | copy-start | bytes 1032196
  84.5 4.0 %copy-start.20 = (bf16[48,3584]{1,0:T(8,128)(2,1)S(1)}, bf16[48,3584]{1,0:T(8,128)(2,1)}, u32[]{:S(2)}) copy-start(bf16[48,3584]{1,0:T(8,128)(2,1)} %copy-done.19) | copy-start | bytes 1032196
  84.5 15.2 %copy-start.12 = (bf16[48,7296]{1,0:T(8,128)(2,1)S(1)}, bf16[48,7296]{1,0:T(8,128)(2,1)}, u32[]{:S(2)}) copy-start(bf16[48,7296]{1,0:T(8,128)(2,1)} %copy-done.11) | copy-start | bytes 2101252
  84.5 15.2 %copy-start.14 = (bf16[48,7296]{1,0:T(8,128)(2,1)S(1)}, bf16[48,7296]{1,0:T(8,128)(2,1)}, u32[]{:S(2)}) copy-start(bf16[48,7296]{1,0:T(8,128)(2,1)} %copy-done.13) | copy-start | bytes 2101252
  84.5 22.4 %copy-start.16 = (bf16[48,7296]{1,0:T(8,128)(2,1)S(1)}, bf16[48,7296]{1,0:T(8,128)(2,1)}, u32[]{:S(2)}) copy-start(bf16[48,7296]{1,0:T(8,128)(2,1)} %copy-done.15) | copy-start | bytes 2101252
  97.3 10.2 %collective-permute-start.18 = (bf16[192,7168]{1,0:T(8,128)(2,1)S(1)}, bf16[192,7168]{1,0:T(8,128)(2,1)S(1)}, u32[]{:S(2)}, u32[]{:S(2)}) collective-permute-start(bf16[192,7168]{1,0:T(8,128)(2,1)S(1)} %get-tuple-element.15), channel_id=1, source_target_pairs={{0,1},{1,0},{2,3},{3,2},{4,5},{5,4},{6,7},{7,6},{8,9},{9,8},{10,11... | collective-permute-start | bytes 8257544 | tf_op jit(solution)/shard_map/ppermute | solution.py:47
  97.4 9.6 %collective-permute-start.20 = (bf16[48,3712]{1,0:T(8,128)(2,1)}, bf16[48,3712]{1,0:T(8,128)(2,1)S(1)}, u32[]{:S(2)}, u32[]{:S(2)}) collective-permute-start(bf16[48,3712]{1,0:T(8,128)(2,1)} %collective-permute-done.9.refs_3_), channel_id=1, source_target_pairs={{0,112},{1,15},{2,114},{3,5},{4,116},{5,3},{6,118},{7,9},{8,120},{... | collective-permute-start | bytes 1069064 | tf_op jit(solution)/shard_map/ppermute | solution.py:42
  99.7 7.2 %collective-permute-start.19 = (bf16[48,3584]{1,0:T(8,128)(2,1)S(1)}, bf16[48,3584]{1,0:T(8,128)(2,1)S(1)}, u32[]{:S(2)}, u32[]{:S(2)}) collective-permute-start(bf16[48,3584]{1,0:T(8,128)(2,1)S(1)} %copy-done.18), channel_id=1, source_target_pairs={{0,16},{1,3},{2,18},{3,1},{4,20},{5,7},{6,22},{7,5},{8,24},{9,11},... | collective-permute-start | bytes 1032200 | tf_op jit(solution)/shard_map/ppermute | solution.py:38
  99.7 8.0 %collective-permute-start.2 = (bf16[48,7296]{1,0:T(8,128)(2,1)S(1)}, bf16[48,7296]{1,0:T(8,128)(2,1)S(1)}, u32[]{:S(2)}, u32[]{:S(2)}) collective-permute-start(bf16[48,7296]{1,0:T(8,128)(2,1)S(1)} %copy-done.12), channel_id=1, source_target_pairs={{0,1},{1,0},{2,3},{3,2},{4,5},{5,4},{6,7},{7,6},{8,9},{9,8},{10,11... | collective-permute-start | bytes 2101256 | tf_op jit(solution)/shard_map/ppermute | solution.py:47
  99.7 9.3 %collective-permute-start.4 = (bf16[48,7296]{1,0:T(8,128)(2,1)S(1)}, bf16[48,7296]{1,0:T(8,128)(2,1)S(1)}, u32[]{:S(2)}, u32[]{:S(2)}) collective-permute-start(bf16[48,7296]{1,0:T(8,128)(2,1)S(1)} %copy-done.14), channel_id=1, source_target_pairs={{0,1},{1,0},{2,3},{3,2},{4,5},{5,4},{6,7},{7,6},{8,9},{9,8},{10,11... | collective-permute-start | bytes 2101256 | tf_op jit(solution)/shard_map/ppermute | solution.py:47
  107.0 2.2 %collective-permute-start.3 = (bf16[48,7296]{1,0:T(8,128)(2,1)S(1)}, bf16[48,7296]{1,0:T(8,128)(2,1)S(1)}, u32[]{:S(2)}, u32[]{:S(2)}) collective-permute-start(bf16[48,7296]{1,0:T(8,128)(2,1)S(1)} %copy-done.16), channel_id=1, source_target_pairs={{0,1},{1,0},{2,3},{3,2},{4,5},{5,4},{6,7},{7,6},{8,9},{9,8},{10,11... | collective-permute-start | bytes 2101256 | tf_op jit(solution)/shard_map/ppermute | solution.py:47
  107.0 10.6 %collective-permute-start.21 = (bf16[48,3584]{1,0:T(8,128)(2,1)S(1)}, bf16[48,3584]{1,0:T(8,128)(2,1)S(1)}, u32[]{:S(2)}, u32[]{:S(2)}) collective-permute-start(bf16[48,3584]{1,0:T(8,128)(2,1)S(1)} %collective-permute-done.19.refs_0_), channel_id=1, source_target_pairs={{0,1},{1,0},{2,3},{3,2},{4,5},{5,4},{6,7},{7,6},{8,9},{9,8},{10,11... | collective-permute-start | bytes 1032200 | tf_op jit(solution)/shard_map/ppermute | solution.py:47
  107.5 10.1 %collective-permute-start.22 = (bf16[48,3712]{1,0:T(8,128)(2,1)S(1)}, bf16[48,3712]{1,0:T(8,128)(2,1)S(1)}, u32[]{:S(2)}, u32[]{:S(2)}) collective-permute-start(bf16[48,3712]{1,0:T(8,128)(2,1)S(1)} %collective-permute-done.20.refs_1_), channel_id=1, source_target_pairs={{0,1},{1,0},{2,3},{3,2},{4,5},{5,4},{6,7},{7,6},{8,9},{9,8},{10,11... | collective-permute-start | bytes 1069064 | tf_op jit(solution)/shard_map/ppermute | solution.py:47
  107.7 15.2 %collective-permute-start.27 = (bf16[48,3584]{1,0:T(8,128)(2,1)S(1)}, bf16[48,3584]{1,0:T(8,128)(2,1)S(1)}, u32[]{:S(2)}, u32[]{:S(2)}) collective-permute-start(bf16[48,3584]{1,0:T(8,128)(2,1)S(1)} %add_convert_fusion.9), channel_id=1, source_target_pairs={{0,112},{1,15},{2,114},{3,5},{4,116},{5,3},{6,118},{7,9},{8,120},{... | collective-permute-start | bytes 1032200 | tf_op jit(solution)/shard_map/ppermute | solution.py:42
  117.3 20.8 %collective-permute-start.5 = (bf16[144,7168]{1,0:T(8,128)(2,1)S(1)}, bf16[144,7168]{1,0:T(8,128)(2,1)S(1)}, u32[]{:S(2)}, u32[]{:S(2)}) collective-permute-start(bf16[144,7168]{1,0:T(8,128)(2,1)S(1)} %get-tuple-element.13), channel_id=1, source_target_pairs={{0,1},{1,0},{2,3},{3,2},{4,5},{5,4},{6,7},{7,6},{8,9},{9,8},{10,11... | collective-permute-start | bytes 6193160 | tf_op jit(solution)/shard_map/ppermute | solution.py:47
  122.5 2.3 %collective-permute-start.23 = (bf16[48,7168]{1,0:T(8,128)(2,1)S(1)}, bf16[48,7168]{1,0:T(8,128)(2,1)S(1)}, u32[]{:S(2)}, u32[]{:S(2)}) collective-permute-start(bf16[48,7168]{1,0:T(8,128)(2,1)S(1)} %get-tuple-element.17), channel_id=1, source_target_pairs={{0,1},{1,0},{2,3},{3,2},{4,5},{5,4},{6,7},{7,6},{8,9},{9,8},{10,11... | collective-permute-start | bytes 2064392 | tf_op jit(solution)/shard_map/ppermute | solution.py:47
  123.2 7.4 %collective-permute-start.26 = (bf16[48,3584]{1,0:T(8,128)(2,1)S(1)}, bf16[48,3584]{1,0:T(8,128)(2,1)S(1)}, u32[]{:S(2)}, u32[]{:S(2)}) collective-permute-start(bf16[48,3584]{1,0:T(8,128)(2,1)S(1)} %get-tuple-element.27), channel_id=1, source_target_pairs={{0,16},{1,3},{2,18},{3,1},{4,20},{5,7},{6,22},{7,5},{8,24},{9,11},... | collective-permute-start | bytes 1032200 | tf_op jit(solution)/shard_map/ppermute | solution.py:38
  124.9 7.4 %collective-permute-start.25 = (bf16[48,3584]{1,0:T(8,128)(2,1)S(1)}, bf16[48,3584]{1,0:T(8,128)(2,1)S(1)}, u32[]{:S(2)}, u32[]{:S(2)}) collective-permute-start(bf16[48,3584]{1,0:T(8,128)(2,1)S(1)} %get-tuple-element.32), channel_id=1, source_target_pairs={{0,112},{1,15},{2,114},{3,5},{4,116},{5,3},{6,118},{7,9},{8,120},{... | collective-permute-start | bytes 1032200 | tf_op jit(solution)/shard_map/ppermute | solution.py:42
  127.0 7.2 %collective-permute-start.24 = (bf16[48,3584]{1,0:T(8,128)(2,1)S(1)}, bf16[48,3584]{1,0:T(8,128)(2,1)S(1)}, u32[]{:S(2)}, u32[]{:S(2)}) collective-permute-start(bf16[48,3584]{1,0:T(8,128)(2,1)S(1)} %get-tuple-element.33), channel_id=1, source_target_pairs={{0,16},{1,3},{2,18},{3,1},{4,20},{5,7},{6,22},{7,5},{8,24},{9,11},... | collective-permute-start | bytes 1032200 | tf_op jit(solution)/shard_map/ppermute | solution.py:38
  127.0 11.1 %collective-permute-start.31 = (bf16[48,3584]{1,0:T(8,128)(2,1)S(1)}, bf16[48,3584]{1,0:T(8,128)(2,1)S(1)}, u32[]{:S(2)}, u32[]{:S(2)}) collective-permute-start(bf16[48,3584]{1,0:T(8,128)(2,1)S(1)} %get-tuple-element.26), channel_id=1, source_target_pairs={{0,16},{1,3},{2,18},{3,1},{4,20},{5,7},{6,22},{7,5},{8,24},{9,11},... | collective-permute-start | bytes 1032200 | tf_op jit(solution)/shard_map/ppermute | solution.py:38
  130.7 7.4 %collective-permute-start.30 = (bf16[48,3584]{1,0:T(8,128)(2,1)S(1)}, bf16[48,3584]{1,0:T(8,128)(2,1)S(1)}, u32[]{:S(2)}, u32[]{:S(2)}) collective-permute-start(bf16[48,3584]{1,0:T(8,128)(2,1)S(1)} %add_convert_fusion.10), channel_id=1, source_target_pairs={{0,112},{1,15},{2,114},{3,5},{4,116},{5,3},{6,118},{7,9},{8,120},{... | collective-permute-start | bytes 1032200 | tf_op jit(solution)/shard_map/ppermute | solution.py:42
  134.6 7.4 %collective-permute-start.29 = (bf16[48,3584]{1,0:T(8,128)(2,1)S(1)}, bf16[48,3584]{1,0:T(8,128)(2,1)S(1)}, u32[]{:S(2)}, u32[]{:S(2)}) collective-permute-start(bf16[48,3584]{1,0:T(8,128)(2,1)S(1)} %get-tuple-element.24), channel_id=1, source_target_pairs={{0,16},{1,3},{2,18},{3,1},{4,20},{5,7},{6,22},{7,5},{8,24},{9,11},... | collective-permute-start | bytes 1032200 | tf_op jit(solution)/shard_map/ppermute | solution.py:38
  134.8 8.6 %collective-permute-start.28 = (bf16[48,3584]{1,0:T(8,128)(2,1)S(1)}, bf16[48,3584]{1,0:T(8,128)(2,1)S(1)}, u32[]{:S(2)}, u32[]{:S(2)}) collective-permute-start(bf16[48,3584]{1,0:T(8,128)(2,1)S(1)} %get-tuple-element.25), channel_id=1, source_target_pairs={{0,112},{1,15},{2,114},{3,5},{4,116},{5,3},{6,118},{7,9},{8,120},{... | collective-permute-start | bytes 1032200 | tf_op jit(solution)/shard_map/ppermute | solution.py:42
  143.7 7.4 %collective-permute-start.36 = (bf16[48,3584]{1,0:T(8,128)(2,1)S(1)}, bf16[48,3584]{1,0:T(8,128)(2,1)S(1)}, u32[]{:S(2)}, u32[]{:S(2)}) collective-permute-start(bf16[48,3584]{1,0:T(8,128)(2,1)S(1)} %get-tuple-element.22), channel_id=1, source_target_pairs={{0,112},{1,15},{2,114},{3,5},{4,116},{5,3},{6,118},{7,9},{8,120},{... | collective-permute-start | bytes 1032200 | tf_op jit(solution)/shard_map/ppermute | solution.py:42
  145.8 7.2 %collective-permute-start.32 = (bf16[48,3584]{1,0:T(8,128)(2,1)S(1)}, bf16[48,3584]{1,0:T(8,128)(2,1)S(1)}, u32[]{:S(2)}, u32[]{:S(2)}) collective-permute-start(bf16[48,3584]{1,0:T(8,128)(2,1)S(1)} %get-tuple-element.23), channel_id=1, source_target_pairs={{0,16},{1,3},{2,18},{3,1},{4,20},{5,7},{6,22},{7,5},{8,24},{9,11},... | collective-permute-start | bytes 1032200 | tf_op jit(solution)/shard_map/ppermute | solution.py:38
  147.5 9.6 %collective-permute-start.34 = (bf16[48,3584]{1,0:T(8,128)(2,1)S(1)}, bf16[48,3584]{1,0:T(8,128)(2,1)S(1)}, u32[]{:S(2)}, u32[]{:S(2)}) collective-permute-start(bf16[48,3584]{1,0:T(8,128)(2,1)S(1)} %get-tuple-element.30), channel_id=1, source_target_pairs={{0,112},{1,15},{2,114},{3,5},{4,116},{5,3},{6,118},{7,9},{8,120},{... | collective-permute-start | bytes 1032200 | tf_op jit(solution)/shard_map/ppermute | solution.py:42
  149.2 7.8 %collective-permute-start.35 = (bf16[48,3584]{1,0:T(8,128)(2,1)S(1)}, bf16[48,3584]{1,0:T(8,128)(2,1)S(1)}, u32[]{:S(2)}, u32[]{:S(2)}) collective-permute-start(bf16[48,3584]{1,0:T(8,128)(2,1)S(1)} %get-tuple-element.31), channel_id=1, source_target_pairs={{0,16},{1,3},{2,18},{3,1},{4,20},{5,7},{6,22},{7,5},{8,24},{9,11},... | collective-permute-start | bytes 1032200 | tf_op jit(solution)/shard_map/ppermute | solution.py:38
  153.4 7.4 %collective-permute-start.37 = (bf16[48,3584]{1,0:T(8,128)(2,1)S(1)}, bf16[48,3584]{1,0:T(8,128)(2,1)S(1)}, u32[]{:S(2)}, u32[]{:S(2)}) collective-permute-start(bf16[48,3584]{1,0:T(8,128)(2,1)S(1)} %get-tuple-element.28), channel_id=1, source_target_pairs={{0,16},{1,3},{2,18},{3,1},{4,20},{5,7},{6,22},{7,5},{8,24},{9,11},... | collective-permute-start | bytes 1032200 | tf_op jit(solution)/shard_map/ppermute | solution.py:38
  155.2 7.2 %collective-permute-start.33 = (bf16[48,3584]{1,0:T(8,128)(2,1)S(1)}, bf16[48,3584]{1,0:T(8,128)(2,1)S(1)}, u32[]{:S(2)}, u32[]{:S(2)}) collective-permute-start(bf16[48,3584]{1,0:T(8,128)(2,1)S(1)} %get-tuple-element.29), channel_id=1, source_target_pairs={{0,112},{1,15},{2,114},{3,5},{4,116},{5,3},{6,118},{7,9},{8,120},{... | collective-permute-start | bytes 1032200 | tf_op jit(solution)/shard_map/ppermute | solution.py:42
  157.0 24.1 %copy-start.21 = (bf16[4,7168]{1,0:T(4,128)(2,1)S(1)}, bf16[4,7168]{1,0:T(4,128)(2,1)}, u32[]{:S(2)}) copy-start(bf16[4,7168]{1,0:T(4,128)(2,1)} %b_ref.1) | copy-start | bytes 172036
  157.0 24.1 %copy-start.22 = (bf16[2,7168]{1,0:T(2,128)(2,1)S(1)}, bf16[2,7168]{1,0:T(2,128)(2,1)}, u32[]{:S(2)}) copy-start(bf16[2,7168]{1,0:T(2,128)(2,1)} %a_ref.1) | copy-start | bytes 86020
